TPU v7x, 512 devices: a whole 4x8x8 slice. The times are simulated.
512 devices in a mesh: heads: 16 (over y, core), batch: 32 (over z, x).
Axes of the slice: x: 4, y: 8, z: 8, core: 2. Of those that a mesh axis runs over, the one named last changes fastest.
Arguments:
- queries: bfloat16 [256, 4096], P('batch', 'heads'), may hold values from -6 to 6
- keys_new: bfloat16 [256, 4096], P('batch', 'heads'), may hold values from -6 to 6
- values_new: bfloat16 [256, 4096], P('batch', 'heads'), may hold values from -6 to 6
- out_gate: bfloat16 [256, 4096], P('batch', 'heads'), may hold values from -6 to 6
- decay_logit: float32 [256, 32], P('batch', 'heads'), may hold values from -6 to 6
- beta_logit: float32 [256, 32], P('batch', 'heads'), may hold values from -6 to 6
- decay_rate: float32 [32], P('heads'), may hold values from 0.05 to 2
- state: float32 [256, 32, 128, 128], P('batch', 'heads'), may hold values from -0.6 to 0.6
- norm_gain: float32 [128], replicated, may hold values from 0.1 to 1.9
- out_proj: bfloat16 [4096, 4096], P('heads'), may hold values from -0.09375 to 0.09375
- residual: bfloat16 [256, 4096], P('batch'), may hold values from -40 to 40, as said below
- final_gain: float32 [4096], replicated, may hold values from 0.1 to 1.9
- value_weight: float32 [4096], replicated, may hold values from -0.09375 to 0.09375
- lm_head: bfloat16 [4096, 65536], P(None, ('heads', 'batch')), may hold values from -15 to 15
- sampled: int32 [256], replicated, may hold values from 0 to 65535
Outputs:
- logprob: float32 [256], P('batch')
- value: float32 [256], P('batch')
Inputs may be any that keep to these rules, and one draw needn't show every extreme that they name: The residual stream's entries have scales that differ by row and by column (up to tenfold each), so neither rows nor columns share one magnitude.
All inputs are finite; a program needn't handle non-finite values.
Results may differ from a plain program's by a relative error of at most 0.0013.
Values may be sent and summed in bfloat16 or wider, within the bound.
No kernel may reach another device: no remote copies, remote signals or barrier semaphores. Data moves between devices by JAX's collectives and lax.ppermute only.
A program may use at most 64 MiB of HBM per device.

v0:
```python
import jax
import jax.numpy as jnp
from jax import lax
from jax.sharding import Mesh
from jax.sharding import PartitionSpec as P

HEADS = ("heads_0", "heads_1")
BATCH = ("batch_0", "batch_1")
HEADS_BATCH = ("heads_0", "heads_1", "batch_0", "batch_1")


epsilon = 1e-06


def cut_along(array, dim, size):
    before, after = (array.shape[:dim], array.shape[dim + 1 :])
    return jnp.moveaxis(array.reshape(*before, size, -1, *after), dim, 0)


def sum_at_owner(array, axis, dim):
    parts = cut_along(array, dim, lax.axis_size(axis))
    arrived = lax.all_to_all(parts, axis, split_axis=0, concat_axis=0, tiled=True)
    return arrived.sum(axis=0)


def copy_for_each(array, axis):
    size = lax.axis_size(axis)
    return lax.all_to_all(
        jnp.broadcast_to(array[None], (size, *array.shape)), axis, 0, 0, tiled=True
    )


def over_copies(array, axis):
    return copy_for_each(array, axis).sum(axis=0)


def together(arrays, axis):
    ends = [0]
    for a in arrays:
        ends.append(ends[-1] + a.size)
    subtotal = over_copies(jnp.concatenate([a.ravel() for a in arrays]), axis)
    return tuple((subtotal[b:e].reshape(a.shape) for a, b, e in zip(arrays, ends, ends[1:])))


def laid_out(parts, dim):
    parts = jnp.moveaxis(parts, 0, dim)
    shape = parts.shape
    return parts.reshape(*shape[:dim], shape[dim] * shape[dim + 1], *shape[dim + 2 :])


def collect(array, axis, dim):
    return laid_out(copy_for_each(array, axis), dim)


def gathered_once(array, axis):
    leaves = jax.tree.leaves(array)
    order = sorted(range(len(leaves)), key=lambda k: -leaves[k].size)
    width = (1, *leaves[order[0]].shape)[-1]
    lines = [
        jnp.pad(leaves[k].reshape(-1), (0, -leaves[k].size % width)).reshape(-1, width)
        for k in order
    ]
    both, at, found = (lax.all_gather(jnp.concatenate(lines), axis), 0, {})
    for k, line in zip(order, lines):
        share = both[:, at : at + len(line)].reshape(len(both), -1)
        found[k] = share[:, : leaves[k].size].reshape(-1, *leaves[k].shape)
        at += len(line)
    numbers = iter(range(len(leaves)))
    return jax.tree.map(lambda _: found[next(numbers)], array)


def combined_by_axis(array, axes, combine):
    for axis in axes:
        pieces = gathered_once(array, axis)
        array = jax.tree.map(lambda part: part[0], pieces)
        for k in range(1, lax.axis_size(axis)):
            array = combine(array, jax.tree.map(lambda part: part[k], pieces))
    return array


def head_outputs(
    queries, keys_new, values_new, out_gate, decay_logit, beta_logit, decay_rate, state, norm_gain
):
    rows_here, heads_here = decay_logit.shape
    query_f = queries.astype(jnp.float32).reshape(rows_here, heads_here, -1)
    key_f = keys_new.astype(jnp.float32).reshape(rows_here, heads_here, -1)
    value_f = values_new.astype(jnp.float32).reshape(rows_here, heads_here, -1)
    gate_f = out_gate.astype(jnp.float32).reshape(rows_here, heads_here, -1)
    key_size = query_f.shape[2]
    query_n = query_f / jnp.sqrt(jnp.sum(query_f * query_f, axis=2, keepdims=True) + epsilon)
    query_n = query_n * key_size ** (-0.5)
    key_n = key_f / jnp.sqrt(jnp.sum(key_f * key_f, axis=2, keepdims=True) + epsilon)
    decay = jnp.exp(-decay_rate[None, :] * jax.nn.softplus(decay_logit))
    strength = jax.nn.sigmoid(beta_logit)
    state_query = jnp.einsum("bhk,bhkv->bhv", query_n, state, precision=lax.Precision.HIGHEST)
    state_key = jnp.einsum("bhk,bhkv->bhv", key_n, state, precision=lax.Precision.HIGHEST)
    intersection = jnp.sum(query_n * key_n, axis=2, keepdims=True)
    written = value_f - decay[..., None] * state_key
    output = decay[..., None] * state_query + strength[..., None] * intersection * written
    normed = output / jnp.sqrt(jnp.mean(output * output, axis=2, keepdims=True) + epsilon)
    result = normed * norm_gain * jax.nn.silu(gate_f)
    return result.reshape(rows_here, -1).astype(jnp.bfloat16)


def merge_stats(earlier, later):
    top = jnp.maximum(earlier[0], later[0])
    total = earlier[1] * jnp.exp(earlier[0] - top) + later[1] * jnp.exp(later[0] - top)
    return (top, total, earlier[2] + later[2])


def per_device(
    queries,
    keys_new,
    values_new,
    out_gate,
    decay_logit,
    beta_logit,
    decay_rate,
    state,
    norm_gain,
    out_proj,
    residual,
    final_gain,
    value_weight,
    lm_head,
    sampled,
):
    headout = head_outputs(
        queries,
        keys_new,
        values_new,
        out_gate,
        decay_logit,
        beta_logit,
        decay_rate,
        state,
        norm_gain,
    )
    partial_out = jnp.dot(headout, out_proj, preferred_element_type=jnp.float32)
    rows_own = residual.shape[0]
    width_all = residual.shape[1]
    attn = sum_at_owner(partial_out, HEADS, 1)
    width_own = attn.shape[1]
    col_first = lax.axis_index(HEADS) * width_own
    resid_cols = lax.dynamic_slice_in_dim(residual, col_first, width_own, 1).astype(jnp.float32)
    gain_cols = lax.dynamic_slice_in_dim(final_gain, col_first, width_own, 0)
    weight_cols = lax.dynamic_slice_in_dim(value_weight, col_first, width_own, 0)
    hsum = resid_cols + attn
    squares, value_part = together(
        (jnp.sum(hsum * hsum, axis=1), jnp.sum(hsum * gain_cols * weight_cols, axis=1)), HEADS
    )
    rstd = 1.0 / jnp.sqrt(squares / width_all + epsilon)
    value = rstd * value_part
    normed = (hsum * rstd[:, None] * gain_cols).astype(jnp.bfloat16)
    all_rows = collect(normed, BATCH, 0)
    logits = jnp.dot(collect(all_rows, HEADS, 1), lm_head, preferred_element_type=jnp.float32)
    vocab_own = lm_head.shape[1]
    vocab_first = lax.axis_index(HEADS_BATCH) * vocab_own
    local_ids = sampled - vocab_first
    columns = lax.broadcasted_iota(jnp.int32, logits.shape, 1)
    chosen = jnp.sum(jnp.where(columns == local_ids[:, None], logits, 0.0), axis=1)
    local_top = jnp.max(logits, axis=1)
    local_total = jnp.sum(jnp.exp(logits - local_top[:, None]), axis=1)
    top, total, chosen_all = combined_by_axis(
        (local_top, local_total, chosen), HEADS_BATCH, merge_stats
    )
    every_logprob = chosen_all - (top + jnp.log(total))
    logprob = lax.dynamic_slice_in_dim(every_logprob, lax.axis_index(BATCH) * rows_own, rows_own, 0)
    return (logprob, value)


def solution(mesh):
    torus = Mesh(mesh.devices.reshape(8, 2, 8, 4), ("heads_0", "heads_1", "batch_0", "batch_1"))
    return jax.shard_map(
        per_device,
        mesh=torus,
        in_specs=(
            P(BATCH, HEADS),
            P(BATCH, HEADS),
            P(BATCH, HEADS),
            P(BATCH, HEADS),
            P(BATCH, HEADS),
            P(BATCH, HEADS),
            P(HEADS),
            P(BATCH, HEADS, None, None),
            P(),
            P(HEADS, None),
            P(BATCH, None),
            P(),
            P(),
            P(None, HEADS_BATCH),
            P(),
        ),
        out_specs=(P(BATCH), P(BATCH)),
        check_vma=False,
    )
```

profile of v0, /device:TPU:24, one launch (start us, length us, event | category | flops | bytes accessed | tf_op | source)
XLA Modules:
  0.0 184.1 jit_solution(13667553858254470906)
XLA Ops:
  0.6 0.0 copy-start
  0.6 0.0 copy-start.4
  0.7 0.0 copy-start.3
  0.7 0.0 copy-start.1
  0.7 0.7 neg.15
  1.4 0.8 fusion
  2.2 0.8 fusion.2
  3.0 0.9 fusion.15
  3.8 2.2 %fusion.11 = f32[8,2,1,128]{3,2,1,0:T(1,128)S(1)} fusion(f32[8,2,128,128]{3,2,1,0:T(8,128)} %param.22, f32[8,2,128,1]{2,0,1,3:T(8,128)S(1)} %get-tuple-element.21), kind=kOutput, calls=%fused_computation.24 | convolution fusion | flops 3145728 | bytes 1064960 | tf_op jit(solution)/shard_map/bhk,bhkv->bhv/dot_general | solution.py:95
  6.0 2.2 %fusion.9 = f32[8,2,1,128]{3,2,1,0:T(1,128)S(1)} fusion(f32[8,2,128,128]{3,2,1,0:T(8,128)} %param.22, f32[8,2,128,1]{2,0,1,3:T(8,128)S(1)} %get-tuple-element.23), kind=kOutput, calls=%fused_computation.22 | convolution fusion | flops 3145728 | bytes 1064960 | tf_op jit(solution)/shard_map/bhk,bhkv->bhv/dot_general | solution.py:96
  8.2 0.0 copy-done.4
  8.2 0.1 fusion.22
  8.3 0.0 copy-done.3
  8.3 0.0 copy-done.1
  8.3 0.2 multiply_reduce_fusion.2
  8.5 0.0 copy-start.2
  8.5 0.0 copy-start.6
  8.5 3.3 %copy.33 = bf16[4096,256]{1,0:T(8,128)(2,1)S(1)} copy(bf16[4096,256]{0,1:T(8,128)(2,1)} %bitcast.430) | data formatting | bytes 4194304 | tf_op jit(solution)/shard_map/dot_general | solution.py:139
  11.8 0.0 copy-done.2
  11.8 0.0 copy-done.6
  11.8 1.3 convolution_bitcast_fusion
  13.1 8.9 %all-to-all-start = ((f32[16,8,256]{2,1,0:T(8,128)}), f32[16,8,256]{2,1,0:T(8,128)S(1)}, u32[]{:S(2)}, u32[]{:S(2)}) async-start(f32[16,8,256]{2,1,0:T(8,128)} %convolution_bitcast_fusion), calls=%async_computation | async-start | bytes 262144 | tf_op jit(solution)/shard_map/all_to_all | solution.py:22
  22.0 0.8 dynamic_slice.13
  22.8 0.8 dynamic_slice.14
  23.5 4.8 %all-to-all-done = f32[16,8,256]{2,1,0:T(8,128)S(1)} async-done(((f32[16,8,256]{2,1,0:T(8,128)}), f32[16,8,256]{2,1,0:T(8,128)S(1)}, u32[]{:S(2)}, u32[]{:S(2)}) %all-to-all-start) | async-done | bytes 131104 | tf_op jit(solution)/shard_map/all_to_all | solution.py:22
  28.3 0.8 multiply_reduce_fusion.1
  29.2 0.1 pad_maximum_fusion
  29.3 9.8 %all_to_all.21 = f32[16,1,16]{2,1,0:T(1,128)S(1)} all-to-all(f32[16,1,16]{2,1,0:T(1,128)S(1)} %broadcast_in_dim.11), channel_id=1, replica_groups=mesh['heads_0'=8,'heads_1'=2,'batch_0'=8,'batch_1'=4] {'heads_0','heads_1'}, dimensions={0} | all-to-all | bytes 2048 | tf_op jit(solution)/shard_map/all_to_all | solution.py:28
  39.0 0.6 slice_multiply_fusion
  39.6 0.8 multiply_convert_fusion
  40.4 21.8 %all_to_all.22 = bf16[32,8,256]{2,1,0:T(8,128)(2,1)S(1)} all-to-all(bf16[32,8,256]{2,1,0:T(8,128)(2,1)S(1)} %broadcast_in_dim.12), channel_id=1, replica_groups=mesh['heads_0'=8,'heads_1'=2,'batch_0'=8,'batch_1'=4] {'batch_0','batch_1'}, dimensions={0} | all-to-all | bytes 262144 | tf_op jit(solution)/shard_map/all_to_all | solution.py:28
  62.2 0.1 copy.28
  62.3 1.6 broadcast_in_dim.14
  63.9 0.0 copy-start.5
  63.9 6.9 %all-to-all-start.3 = ((bf16[16,256,256]{1,2,0:T(8,128)(2,1)}), bf16[16,256,256]{1,2,0:T(8,128)(2,1)S(1)}, u32[]{:S(2)}, u32[]{:S(2)}) async-start(bf16[16,256,256]{1,2,0:T(8,128)(2,1)} %broadcast_in_dim.14), calls=%async_computation.3 | async-start | bytes 4194304 | tf_op jit(solution)/shard_map/all_to_all | solution.py:28
  70.8 0.0 copy-done.5
  70.8 48.7 %all-to-all-done.3 = bf16[16,256,256]{1,2,0:T(8,128)(2,1)S(1)} async-done(((bf16[16,256,256]{1,2,0:T(8,128)(2,1)}), bf16[16,256,256]{1,2,0:T(8,128)(2,1)S(1)}, u32[]{:S(2)}, u32[]{:S(2)}) %all-to-all-start.3) | async-done | bytes 2097184 | tf_op jit(solution)/shard_map/all_to_all | solution.py:28
  119.5 0.0 copy-done
  119.5 0.6 fusion.98
  120.1 0.1 exponential_reduce_fusion
  120.1 24.7 %all-gather.4 = f32[8,3,256]{2,1,0:T(4,128)S(1)} all-gather(f32[1,3,256]{2,1,0:T(4,128)S(1)} %maximum_bitcast_fusion), channel_id=2, replica_groups=mesh['heads_0'=8,'heads_1'=2,'batch_0'=8,'batch_1'=4] {'heads_0'}, dimensions={0}, use_global_device_ids=true | all-gather | bytes 27648 | tf_op jit(solution)/shard_map/all_gather | solution.py:63
  144.9 1.8 all-gather.5
  146.7 24.7 %all-gather.6 = f32[8,3,256]{2,1,0:T(4,128)S(1)} all-gather(f32[1,3,256]{2,1,0:T(4,128)S(1)} %maximum_bitcast_fusion.2), channel_id=4, replica_groups=mesh['heads_0'=8,'heads_1'=2,'batch_0'=8,'batch_1'=4] {'batch_0'}, dimensions={0}, use_global_device_ids=true | all-gather | bytes 27648 | tf_op jit(solution)/shard_map/all_gather | solution.py:63
  171.5 12.0 %all-gather.7 = f32[4,3,256]{2,1,0:T(4,128)S(1)} all-gather(f32[1,3,256]{2,1,0:T(4,128)S(1)} %maximum_bitcast_fusion.3), channel_id=5, replica_groups=mesh['heads_0'=8,'heads_1'=2,'batch_0'=8,'batch_1'=4] {'batch_1'}, dimensions={0}, use_global_device_ids=true | all-gather | bytes 15360 | tf_op jit(solution)/shard_map/all_gather | solution.py:63
  183.5 0.6 dynamic_slice.15
  (20 shorter events, 0.3 us)
Async XLA Ops:
  0.6 118.9 %copy-start = (bf16[4096,128]{1,0:T(8,128)(2,1)S(1)}, bf16[4096,128]{1,0:T(8,128)(2,1)}, u32[]{:S(2)}) copy-start(bf16[4096,128]{1,0:T(8,128)(2,1)} %param.28) | copy-start | bytes 3145732
  0.6 7.6 %copy-start.4 = (f32[8,2]{0,1:T(2,128)S(1)}, f32[8,2]{0,1:T(2,128)}, u32[]{:S(2)}) copy-start(f32[8,2]{0,1:T(2,128)} %param.19) | copy-start | bytes 196
  0.7 7.6 %copy-start.3 = (f32[8,2]{0,1:T(2,128)S(1)}, f32[8,2]{0,1:T(2,128)}, u32[]{:S(2)}) copy-start(f32[8,2]{0,1:T(2,128)} %param.20) | copy-start | bytes 196
  0.7 7.6 %copy-start.1 = (bf16[8,256]{1,0:T(8,128)(2,1)S(1)}, bf16[8,256]{1,0:T(8,128)(2,1)}, u32[]{:S(2)}) copy-start(bf16[8,256]{1,0:T(8,128)(2,1)} %param.17) | copy-start | bytes 12292
  8.5 3.3 %copy-start.2 = (bf16[8,256]{1,0:T(8,128)(2,1)S(1)}, bf16[8,256]{1,0:T(8,128)(2,1)}, u32[]{:S(2)}) copy-start(bf16[8,256]{1,0:T(8,128)(2,1)} %param.18) | copy-start | bytes 12292
  8.5 3.3 %copy-start.6 = (f32[128]{0:T(128)S(1)}, f32[128]{0:T(128)}, u32[]{:S(2)}) copy-start(f32[128]{0:T(128)} %param.23) | copy-start | bytes 1540
  13.1 15.2 %all-to-all-start = ((f32[16,8,256]{2,1,0:T(8,128)}), f32[16,8,256]{2,1,0:T(8,128)S(1)}, u32[]{:S(2)}, u32[]{:S(2)}) async-start(f32[16,8,256]{2,1,0:T(8,128)} %convolution_bitcast_fusion), calls=%async_computation | async-start | bytes 262144 | tf_op jit(solution)/shard_map/all_to_all | solution.py:22
  63.9 6.9 %copy-start.5 = (s32[256]{0:T(256)S(1)}, s32[256]{0:T(256)}, u32[]{:S(2)}) copy-start(s32[256]{0:T(256)} %param.29) | copy-start | bytes 3076
  63.9 55.6 %all-to-all-start.3 = ((bf16[16,256,256]{1,2,0:T(8,128)(2,1)}), bf16[16,256,256]{1,2,0:T(8,128)(2,1)S(1)}, u32[]{:S(2)}, u32[]{:S(2)}) async-start(bf16[16,256,256]{1,2,0:T(8,128)(2,1)} %broadcast_in_dim.14), calls=%async_computation.3 | async-start | bytes 4194304 | tf_op jit(solution)/shard_map/all_to_all | solution.py:28
where the time goes:
time: 185 us; the launch traced here: 184 us
  blocking collectives  94.8 us (51%)
  waiting for transfers between devices  53.4 us (29%)
  starting transfers between devices  15.8 us (9%)
  local copies, waits for them, and re-layouts  7.1 us (4%)
  matrix products  6.24 us (3%)
  other arithmetic  5.97 us (3%)
    all_gather x4, blocking collectives, gathered_once(): both, at, found = (lax.all_gather(jnp.concatenate(lines), axis), 0, {})  63.2 us
    all_to_all x1, waiting for transfers between devices, copy_for_each(): lax.all_to_all(jnp.broadcast_to(array[None], (size, *array.shape)), axis,...  48.7 us
    all_to_all x2, blocking collectives, copy_for_each(): lax.all_to_all(jnp.broadcast_to(array[None], (size, *array.shape)), axis,...  31.6 us
    all_to_all x1, starting transfers between devices, sum_at_owner(): lax.all_to_all(parts, axis, split_axis=0, concat_axis=0, tiled=True)  8.9 us
    all_to_all x1, starting transfers between devices, copy_for_each(): lax.all_to_all(jnp.broadcast_to(array[None], (size, *array.shape)), axis,...  6.9 us
    all_to_all x1, waiting for transfers between devices, sum_at_owner(): lax.all_to_all(parts, axis, split_axis=0, concat_axis=0, tiled=True)  4.76 us
  transfers between devices with their start and end apart: 2, of which 2 were waited for; matrix products, arithmetic and copies ran while one was open for 1% of the time, Pallas kernels for 0%

commit v1 on v0

v1 whole, which is shorter than its diff:
```python
import jax
import jax.numpy as jnp
from jax import lax
from jax.sharding import Mesh
from jax.sharding import PartitionSpec as P

HEADS = ("heads_0", "heads_1")
BATCH = ("batch_0", "batch_1")
HEADS_BATCH = ("heads_0", "heads_1", "batch_0", "batch_1")


epsilon = 1e-06


def exchange(parts, axis):
    return lax.all_to_all(parts, axis, split_axis=0, concat_axis=0, tiled=True)


def copy_for_each(array, axis):
    size = lax.axis_size(axis)
    return exchange(jnp.broadcast_to(array[None], (size, *array.shape)), axis)


def head_outputs(
    queries, keys_new, values_new, out_gate, decay_logit, beta_logit, decay_rate, state, norm_gain
):
    rows_here, heads_here = decay_logit.shape
    query_f = queries.astype(jnp.float32).reshape(rows_here, heads_here, -1)
    key_f = keys_new.astype(jnp.float32).reshape(rows_here, heads_here, -1)
    value_f = values_new.astype(jnp.float32).reshape(rows_here, heads_here, -1)
    gate_f = out_gate.astype(jnp.float32).reshape(rows_here, heads_here, -1)
    key_size = query_f.shape[2]
    query_n = query_f / jnp.sqrt(jnp.sum(query_f * query_f, axis=2, keepdims=True) + epsilon)
    query_n = query_n * key_size ** (-0.5)
    key_n = key_f / jnp.sqrt(jnp.sum(key_f * key_f, axis=2, keepdims=True) + epsilon)
    decay = jnp.exp(-decay_rate[None, :] * jax.nn.softplus(decay_logit))
    strength = jax.nn.sigmoid(beta_logit)
    state_query = jnp.einsum("bhk,bhkv->bhv", query_n, state, precision=lax.Precision.HIGHEST)
    state_key = jnp.einsum("bhk,bhkv->bhv", key_n, state, precision=lax.Precision.HIGHEST)
    intersection = jnp.sum(query_n * key_n, axis=2, keepdims=True)
    written = value_f - decay[..., None] * state_key
    output = decay[..., None] * state_query + strength[..., None] * intersection * written
    normed = output / jnp.sqrt(jnp.mean(output * output, axis=2, keepdims=True) + epsilon)
    result = normed * norm_gain * jax.nn.silu(gate_f)
    return result.reshape(rows_here, -1).astype(jnp.bfloat16)


def merged(top, total, chosen, axis):
    highest = jnp.max(top, axis=axis, keepdims=True)
    scaled = jnp.sum(total * jnp.exp(top - highest), axis=axis)
    return jnp.squeeze(highest, axis), scaled, jnp.sum(chosen, axis=axis)


def per_device(
    queries,
    keys_new,
    values_new,
    out_gate,
    decay_logit,
    beta_logit,
    decay_rate,
    state,
    norm_gain,
    out_proj,
    residual,
    final_gain,
    value_weight,
    lm_head,
    sampled,
):
    chips, cores = lax.axis_size("heads_0"), lax.axis_size("heads_1")
    groups = lax.axis_size(BATCH)
    chip, core = lax.axis_index("heads_0"), lax.axis_index("heads_1")
    rows_own, width = residual.shape
    rows_core = rows_own // cores
    copies = chips // rows_core
    lanes = 128
    lines = width // lanes
    half = width // copies

    other_head = lax.ppermute(lm_head, "heads_1", [(0, 1), (1, 0)])

    headout = head_outputs(
        queries,
        keys_new,
        values_new,
        out_gate,
        decay_logit,
        beta_logit,
        decay_rate,
        state,
        norm_gain,
    )
    for_owner = headout.reshape(cores, rows_core, 1, -1)
    for_owner = jnp.broadcast_to(for_owner, (cores, rows_core, copies, headout.shape[1]))
    for_owner = for_owner.transpose(1, 2, 0, 3).reshape(chips * cores, -1)
    partial_out = jnp.dot(for_owner, out_proj, preferred_element_type=jnp.float32)
    arrived = exchange(partial_out.reshape(chips * cores, lines, lanes), HEADS)
    row = rows_core * core + chip // copies
    own = lax.dynamic_slice_in_dim(residual, row, 1, 0).astype(jnp.float32).reshape(lines, lanes)
    gain = final_gain.reshape(lines, lanes)
    weight = value_weight.reshape(lines, lanes)
    hsum = own + arrived.sum(axis=0)
    rstd = 1.0 / jnp.sqrt(jnp.sum(hsum * hsum) / width + epsilon)
    value = rstd * jnp.sum(hsum * gain * weight)
    normed = (hsum * rstd * gain).astype(jnp.bfloat16)
    piece = lax.dynamic_slice_in_dim(normed, (chip % copies) * (lines // copies), lines // copies, 0)
    all_groups = copy_for_each(piece, BATCH).reshape(groups, half)
    all_rows = copy_for_each(all_groups, "heads_0").reshape(rows_core, copies, groups, half)

    heads_both = (lm_head, other_head)
    vocab_own = lm_head.shape[1]
    flat = lax.axis_index(HEADS_BATCH)
    firsts = (flat * vocab_own, (flat + (1 - 2 * core) * groups) * vocab_own)
    ids = lax.dynamic_index_in_dim(
        sampled.reshape(groups, cores, rows_core).transpose(1, 2, 0), core, 0, keepdims=False
    ).reshape(-1)
    operand = all_rows.transpose(0, 2, 1, 3).reshape(rows_core * groups, width)
    found = []
    for matrix, first in zip(heads_both, firsts):
        logits = jnp.dot(operand, matrix, preferred_element_type=jnp.float32)
        columns = lax.broadcasted_iota(jnp.int32, logits.shape, 1) + first
        found.append(
            (
                logits,
                jnp.max(logits, axis=1),
                jnp.sum(jnp.where(columns == ids[:, None], logits, 0.0), axis=1),
            )
        )
    top = jnp.maximum(found[0][1], found[1][1])
    total = sum(jnp.sum(jnp.exp(f[0] - top[:, None]), axis=1) for f in found)
    chosen = found[0][2] + found[1][2]
    stats = jnp.stack([top, total, chosen]).reshape(3, rows_core, groups).transpose(2, 0, 1)
    stats = exchange(stats.reshape(groups, 1, 3 * rows_core), BATCH).reshape(groups, 3, rows_core)
    stats = merged(stats[:, 0], stats[:, 1], stats[:, 2], 0)
    packed = jnp.concatenate([*stats, value[None]])
    packed = copy_for_each(packed[None], HEADS).reshape(chips, cores, -1)
    found = packed[..., : 3 * rows_core].reshape(chips, cores, 3, rows_core)
    top, total, chosen = merged(found[:, :, 0], found[:, :, 1], found[:, :, 2], 0)
    logprob = (chosen - (top + jnp.log(total))).reshape(-1)
    values = packed[::copies, :, 3 * rows_core].T.reshape(-1)
    return (logprob, values)


def solution(mesh):
    torus = Mesh(mesh.devices.reshape(8, 2, 8, 4), ("heads_0", "heads_1", "batch_0", "batch_1"))
    return jax.shard_map(
        per_device,
        mesh=torus,
        in_specs=(
            P(BATCH, HEADS),
            P(BATCH, HEADS),
            P(BATCH, HEADS),
            P(BATCH, HEADS),
            P(BATCH, HEADS),
            P(BATCH, HEADS),
            P(HEADS),
            P(BATCH, HEADS, None, None),
            P(),
            P(HEADS, None),
            P(BATCH, None),
            P(),
            P(),
            P(None, HEADS_BATCH),
            P(),
        ),
        out_specs=(P(BATCH), P(BATCH)),
        check_vma=False,
    )
```

time: 185 us -> 121 us (0.65)
  the two profiles are of different devices: /device:TPU:24 before, /device:TPU:1 now
where the time goes in v1:
time: 121 us; the launch traced here: 120 us
  waiting for transfers between devices  44.4 us (37%)
  blocking collectives  31.9 us (26%)
  starting transfers between devices  21 us (17%)
  local copies, waits for them, and re-layouts  9.88 us (8%)
  other arithmetic  5.8 us (5%)
  matrix products  4.94 us (4%)
  between operations  2.29 us (2%)
    all_to_all x3, waiting for transfers between devices, exchange(): return lax.all_to_all(parts, axis, split_axis=0, concat_axis=0, tiled=True)  44.4 us
    all_to_all x2, blocking collectives, exchange(): return lax.all_to_all(parts, axis, split_axis=0, concat_axis=0, tiled=True)  31.9 us
    all_to_all x3, starting transfers between devices, exchange(): return lax.all_to_all(parts, axis, split_axis=0, concat_axis=0, tiled=True)  17.6 us
    dot_general x2, local copies, waits for them, and re-layouts, per_device(): jnp.dot(for_owner, out_proj, preferred_element_type=jnp.float32)  4.07 us
    ppermute x1, starting transfers between devices, per_device(): other_head = lax.ppermute(lm_head, 'heads_1', [(0, 1), (1, 0)])  3.47 us
  transfers between devices with their start and end apart: 4, of which 3 were waited for; matrix products, arithmetic and copies ran while one was open for 2% of the time, Pallas kernels for 0%

profile of v1, /device:TPU:1, one launch (start us, length us, event | category | flops | bytes accessed | tf_op | source)
XLA Modules:
  0.0 120.2 jit_solution(11104550815254061605)
XLA Ops:
  0.7 0.8 fusion.5
  1.6 0.8 fusion.3
  2.3 0.9 fusion.20
  3.2 1.0 fusion.14
  4.2 1.0 fusion.16
  5.3 0.2 multiply_reduce_fusion.1
  5.5 0.1 fusion.18
  5.6 3.3 %copy.109 = bf16[4096,256]{1,0:T(8,128)(2,1)S(1)} copy(bf16[4096,256]{0,1:T(8,128)(2,1)} %bitcast.116) | data formatting | bytes 4194304 | tf_op jit(solution)/shard_map/dot_general | solution.py:97
  8.9 0.6 fusion.32
  9.6 0.8 copy.93
  10.4 10.2 %all-to-all-start = ((f32[16,32,128]{2,1,0:T(8,128)}), f32[16,32,128]{2,1,0:T(8,128)S(1)}, u32[]{:S(2)}, u32[]{:S(2)}) async-start(f32[16,32,128]{2,1,0:T(8,128)} %copy.93), calls=%async_computation | async-start | bytes 524288 | tf_op jit(solution)/shard_map/all_to_all | solution.py:16
  20.6 11.7 %all-to-all-done = f32[16,32,128]{2,1,0:T(8,128)S(1)} async-done(((f32[16,32,128]{2,1,0:T(8,128)}), f32[16,32,128]{2,1,0:T(8,128)S(1)}, u32[]{:S(2)}, u32[]{:S(2)}) %all-to-all-start) | async-done | bytes 262176 | tf_op jit(solution)/shard_map/all_to_all | solution.py:16
  32.3 1.5 %multiply_reduce_fusion = (f32[]{:T(128)}, f32[1,4096]{1,0:T(1,128)S(1)}) fusion(f32[1,4096]{1,0:T(1,128)S(1)} %bitcast.119, bf16[8,4096]{1,0:T(8,128)(2,1)} %param.25, s32[]{:T(128)S(6)} %select_n.33), kind=kLoop, calls=%fused_computation.10 | loop fusion | flops 16383 | bytes 40968 | tf_op jit(solution)/shard_map/reduce_sum | solution.py:104
  34.5 20.9 %all_to_all.25 = bf16[32,16,128]{2,1,0:T(8,128)(2,1)S(1)} all-to-all(bf16[32,16,128]{2,1,0:T(8,128)(2,1)S(1)} %broadcast_in_dim.17), channel_id=1, replica_groups=mesh['heads_0'=8,'heads_1'=2,'batch_0'=8,'batch_1'=4] {'batch_0','batch_1'}, dimensions={0} | all-to-all | bytes 262144 | tf_op jit(solution)/shard_map/all_to_all | solution.py:16
  55.5 1.1 broadcast_in_dim.19
  56.6 3.6 %all-to-all-start.2 = ((bf16[8,32,2048]{2,1,0:T(8,128)(2,1)}), bf16[8,32,2048]{2,1,0:T(8,128)(2,1)S(1)}, u32[]{:S(2)}, u32[]{:S(2)}) async-start(bf16[8,32,2048]{2,1,0:T(8,128)(2,1)} %broadcast_in_dim.19), calls=%async_computation.2 | async-start | bytes 2097152 | tf_op jit(solution)/shard_map/all_to_all | solution.py:16
  60.2 3.5 %collective-permute-start = (bf16[4096,128]{1,0:T(8,128)(2,1)S(1)}, bf16[4096,128]{1,0:T(8,128)(2,1)}, u32[]{:S(2)}, u32[]{:S(2)}) collective-permute-start(bf16[4096,128]{1,0:T(8,128)(2,1)S(1)} %copy-done.1), channel_id=1, source_target_pairs={{0,32},{32,0},{1,33},{33,1},{2,34},{34,2},{3,35},{35,3},{4,36},{36... | collective-permute-start | bytes 3145736 | tf_op jit(solution)/shard_map/ppermute | solution.py:81
  63.7 0.1 reshape.201
  63.8 0.1 copy.95
  63.9 0.1 eq.18
  64.0 25.3 %all-to-all-done.2 = bf16[8,32,2048]{2,1,0:T(8,128)(2,1)S(1)} async-done(((bf16[8,32,2048]{2,1,0:T(8,128)(2,1)}), bf16[8,32,2048]{2,1,0:T(8,128)(2,1)S(1)}, u32[]{:S(2)}, u32[]{:S(2)}) %all-to-all-start.2) | async-done | bytes 1048608 | tf_op jit(solution)/shard_map/all_to_all | solution.py:16
  89.3 1.1 copy.94
  90.3 0.4 copy.112
  90.7 0.6 fusion.30
  91.3 1.8 %fusion.31 = (f32[128]{0:T(128)S(1)}, f32[128,128]{0,1:T(8,128)S(1)}) fusion(bf16[128,4096]{1,0:T(8,128)(2,1)S(1)} %bitcast.112, bf16[4096,128]{1,0:T(8,128)(2,1)} %collective-permute-done), kind=kOutput, calls=%fused_computation.71 | convolution fusion | flops 134233984 | bytes 2163200 | tf_op jit(solution)/shard_map/dot_general | solution.py:121
  93.1 0.1 max.24
  93.2 0.1 exponential_reduce_fusion.1
  93.3 0.1 add.153
  93.4 0.1 add.142
  93.5 0.7 copy.96
  94.2 3.9 %all-to-all-start.3 = ((f32[32,1,12]{2,1,0:T(1,128)}), f32[32,1,12]{2,1,0:T(1,128)S(1)}, u32[]{:S(2)}, u32[]{:S(2)}) async-start(f32[32,1,12]{2,1,0:T(1,128)} %copy.96), calls=%async_computation.3 | async-start | bytes 32768 | tf_op jit(solution)/shard_map/all_to_all | solution.py:16
  98.1 0.6 fusion.2
  99.3 7.3 %all-to-all-done.3 = f32[32,1,12]{2,1,0:T(1,128)S(1)} async-done(((f32[32,1,12]{2,1,0:T(1,128)}), f32[32,1,12]{2,1,0:T(1,128)S(1)}, u32[]{:S(2)}, u32[]{:S(2)}) %all-to-all-start.3) | async-done | bytes 1568 | tf_op jit(solution)/shard_map/all_to_all | solution.py:16
  106.7 0.1 copy.97
  106.8 0.2 slice_reduce_fusion.2
  106.9 0.2 fusion.25
  107.1 0.1 pad_maximum_fusion
  107.2 11.0 %all_to_all.26 = f32[16,1,13]{2,1,0:T(1,128)S(1)} all-to-all(f32[16,1,13]{2,1,0:T(1,128)S(1)} %broadcast_in_dim.23), channel_id=1, replica_groups=mesh['heads_0'=8,'heads_1'=2,'batch_0'=8,'batch_1'=4] {'heads_0','heads_1'}, dimensions={0} | all-to-all | bytes 1664 | tf_op jit(solution)/shard_map/all_to_all | solution.py:16
  118.2 0.1 slice.31
  118.3 0.1 copy.98
  118.4 0.1 fusion.29
  118.5 0.1 copy.101
  118.6 0.2 fusion.23
  118.7 0.1 copy.102
  118.8 0.1 copy.103
  118.9 0.6 sub.58
  119.5 0.1 copy.104
  119.6 0.6 reshape.207
  (47 shorter events, 0.4 us)
Async XLA Ops:
  0.6 2.6 %copy-start = (f32[8,2,128,128]{3,2,1,0:T(8,128)S(1)}, f32[8,2,128,128]{3,2,1,0:T(8,128)}, u32[]{:S(2)}) copy-start(f32[8,2,128,128]{3,2,1,0:T(8,128)} %param.22) | copy-start | bytes 3145732
  0.6 4.5 %copy-start.10 = (f32[2]{0:T(128)S(1)}, f32[2]{0:T(128)}, u32[]{:S(2)}) copy-start(f32[2]{0:T(128)} %param.21) | copy-start | bytes 28
  0.7 4.5 %copy-start.6 = (f32[8,2]{0,1:T(2,128)S(1)}, f32[8,2]{0,1:T(2,128)}, u32[]{:S(2)}) copy-start(f32[8,2]{0,1:T(2,128)} %param.20) | copy-start | bytes 196
  0.7 4.5 %copy-start.8 = (f32[8,2]{0,1:T(2,128)S(1)}, f32[8,2]{0,1:T(2,128)}, u32[]{:S(2)}) copy-start(f32[8,2]{0,1:T(2,128)} %param.19) | copy-start | bytes 196
  0.7 4.6 %copy-start.4 = (bf16[8,256]{1,0:T(8,128)(2,1)S(1)}, bf16[8,256]{1,0:T(8,128)(2,1)}, u32[]{:S(2)}) copy-start(bf16[8,256]{1,0:T(8,128)(2,1)} %param.17) | copy-start | bytes 12292
  0.7 4.8 %copy-start.5 = (bf16[8,256]{1,0:T(8,128)(2,1)S(1)}, bf16[8,256]{1,0:T(8,128)(2,1)}, u32[]{:S(2)}) copy-start(bf16[8,256]{1,0:T(8,128)(2,1)} %param.18) | copy-start | bytes 12292
  0.7 4.8 %copy-start.9 = (f32[128]{0:T(128)S(1)}, f32[128]{0:T(128)}, u32[]{:S(2)}) copy-start(f32[128]{0:T(128)} %param.23) | copy-start | bytes 1540
  8.9 25.6 %copy-start.2 = (f32[4096]{0:T(1024)S(1)}, f32[4096]{0:T(1024)}, u32[]{:S(2)}) copy-start(f32[4096]{0:T(1024)} %param.26) | copy-start | bytes 49156
  10.4 21.9 %all-to-all-start = ((f32[16,32,128]{2,1,0:T(8,128)}), f32[16,32,128]{2,1,0:T(8,128)S(1)}, u32[]{:S(2)}, u32[]{:S(2)}) async-start(f32[16,32,128]{2,1,0:T(8,128)} %copy.93), calls=%async_computation | async-start | bytes 524288 | tf_op jit(solution)/shard_map/all_to_all | solution.py:16
  20.5 39.6 %copy-start.1 = (bf16[4096,128]{1,0:T(8,128)(2,1)S(1)}, bf16[4096,128]{1,0:T(8,128)(2,1)}, u32[]{:S(2)}) copy-start(bf16[4096,128]{1,0:T(8,128)(2,1)} %param.28) | copy-start | bytes 3145732
  20.5 43.1 %copy-start.7 = (s32[256]{0:T(256)S(1)}, s32[256]{0:T(256)}, u32[]{:S(2)}) copy-start(s32[256]{0:T(256)} %param.29) | copy-start | bytes 3076
  56.6 32.7 %all-to-all-start.2 = ((bf16[8,32,2048]{2,1,0:T(8,128)(2,1)}), bf16[8,32,2048]{2,1,0:T(8,128)(2,1)S(1)}, u32[]{:S(2)}, u32[]{:S(2)}) async-start(bf16[8,32,2048]{2,1,0:T(8,128)(2,1)} %broadcast_in_dim.19), calls=%async_computation.2 | async-start | bytes 2097152 | tf_op jit(solution)/shard_map/all_to_all | solution.py:16
  60.2 31.1 %collective-permute-start = (bf16[4096,128]{1,0:T(8,128)(2,1)S(1)}, bf16[4096,128]{1,0:T(8,128)(2,1)}, u32[]{:S(2)}, u32[]{:S(2)}) collective-permute-start(bf16[4096,128]{1,0:T(8,128)(2,1)S(1)} %copy-done.1), channel_id=1, source_target_pairs={{0,32},{32,0},{1,33},{33,1},{2,34},{34,2},{3,35},{35,3},{4,36},{36... | collective-permute-start | bytes 3145736 | tf_op jit(solution)/shard_map/ppermute | solution.py:81
  90.7 7.3 %copy-start.3 = (f32[4096]{0:T(1024)S(1)}, f32[4096]{0:T(1024)}, u32[]{:S(2)}) copy-start(f32[4096]{0:T(1024)} %param.27) | copy-start | bytes 49156
  94.2 12.5 %all-to-all-start.3 = ((f32[32,1,12]{2,1,0:T(1,128)}), f32[32,1,12]{2,1,0:T(1,128)S(1)}, u32[]{:S(2)}, u32[]{:S(2)}) async-start(f32[32,1,12]{2,1,0:T(1,128)} %copy.96), calls=%async_computation.3 | async-start | bytes 32768 | tf_op jit(solution)/shard_map/all_to_all | solution.py:16

commit v2 on v1

--- a/solution.py
+++ b/solution.py
@@ -5,8 +5,10 @@
 from jax.sharding import PartitionSpec as P
 
 HEADS = ("heads_0", "heads_1")
-BATCH = ("batch_0", "batch_1")
-HEADS_BATCH = ("heads_0", "heads_1", "batch_0", "batch_1")
+BATCH = ("z_pair", "z_side", "x")
+GROUP = ("z_pair", "x")
+HEADS_BATCH = ("heads_0", "heads_1", "z_pair", "z_side", "x")
+SWAP = [(0, 1), (1, 0)]
 
 
 epsilon = 1e-06
@@ -69,8 +71,9 @@
     sampled,
 ):
     chips, cores = lax.axis_size("heads_0"), lax.axis_size("heads_1")
-    groups = lax.axis_size(BATCH)
+    groups = lax.axis_size(GROUP)
     chip, core = lax.axis_index("heads_0"), lax.axis_index("heads_1")
+    side = lax.axis_index("z_side")
     rows_own, width = residual.shape
     rows_core = rows_own // cores
     copies = chips // rows_core
@@ -78,7 +81,9 @@
     lines = width // lanes
     half = width // copies
 
-    other_head = lax.ppermute(lm_head, "heads_1", [(0, 1), (1, 0)])
+    z_head = lax.ppermute(lm_head, "z_side", SWAP)
+    core_head = lax.ppermute(lm_head, "heads_1", SWAP)
+    both_head = lax.ppermute(z_head, "heads_1", SWAP)
 
     headout = head_outputs(
         queries,
@@ -105,19 +110,22 @@
     value = rstd * jnp.sum(hsum * gain * weight)
     normed = (hsum * rstd * gain).astype(jnp.bfloat16)
     piece = lax.dynamic_slice_in_dim(normed, (chip % copies) * (lines // copies), lines // copies, 0)
-    all_groups = copy_for_each(piece, BATCH).reshape(groups, half)
+    all_groups = copy_for_each(piece, GROUP).reshape(groups, half)
     all_rows = copy_for_each(all_groups, "heads_0").reshape(rows_core, copies, groups, half)
 
-    heads_both = (lm_head, other_head)
     vocab_own = lm_head.shape[1]
     flat = lax.axis_index(HEADS_BATCH)
-    firsts = (flat * vocab_own, (flat + (1 - 2 * core) * groups) * vocab_own)
-    ids = lax.dynamic_index_in_dim(
-        sampled.reshape(groups, cores, rows_core).transpose(1, 2, 0), core, 0, keepdims=False
-    ).reshape(-1)
+    across = (1 - 2 * core) * lax.axis_size(BATCH)
+    along = (1 - 2 * side) * lax.axis_size("x")
+    matrices = (lm_head, core_head, z_head, both_head)
+    firsts = [(flat + shift) * vocab_own for shift in (0, across, along, across + along)]
+    ids = sampled.reshape(-1, lax.axis_size("z_side"), lax.axis_size("x"), cores, rows_core)
+    ids = lax.dynamic_index_in_dim(ids, side, 1, keepdims=False)
+    ids = lax.dynamic_index_in_dim(ids, core, 2, keepdims=False)
+    ids = ids.reshape(groups, rows_core).T.reshape(-1)
     operand = all_rows.transpose(0, 2, 1, 3).reshape(rows_core * groups, width)
     found = []
-    for matrix, first in zip(heads_both, firsts):
+    for matrix, first in zip(matrices, firsts):
         logits = jnp.dot(operand, matrix, preferred_element_type=jnp.float32)
         columns = lax.broadcasted_iota(jnp.int32, logits.shape, 1) + first
         found.append(
@@ -127,11 +135,11 @@
                 jnp.sum(jnp.where(columns == ids[:, None], logits, 0.0), axis=1),
             )
         )
-    top = jnp.maximum(found[0][1], found[1][1])
+    top = jnp.max(jnp.stack([f[1] for f in found]), axis=0)
     total = sum(jnp.sum(jnp.exp(f[0] - top[:, None]), axis=1) for f in found)
-    chosen = found[0][2] + found[1][2]
+    chosen = sum(f[2] for f in found)
     stats = jnp.stack([top, total, chosen]).reshape(3, rows_core, groups).transpose(2, 0, 1)
-    stats = exchange(stats.reshape(groups, 1, 3 * rows_core), BATCH).reshape(groups, 3, rows_core)
+    stats = exchange(stats.reshape(groups, 1, 3 * rows_core), GROUP).reshape(groups, 3, rows_core)
     stats = merged(stats[:, 0], stats[:, 1], stats[:, 2], 0)
     packed = jnp.concatenate([*stats, value[None]])
     packed = copy_for_each(packed[None], HEADS).reshape(chips, cores, -1)
@@ -143,7 +151,9 @@
 
 
 def solution(mesh):
-    torus = Mesh(mesh.devices.reshape(8, 2, 8, 4), ("heads_0", "heads_1", "batch_0", "batch_1"))
+    torus = Mesh(
+        mesh.devices.reshape(8, 2, 4, 2, 4), ("heads_0", "heads_1", "z_pair", "z_side", "x")
+    )
     return jax.shard_map(
         per_device,
         mesh=torus,

time: 121 us -> 118 us (0.975)
  waiting for transfers between devices: 44.4 us -> 26.9 us
  starting transfers between devices: 21 us -> 28.4 us
  blocking collectives: 31.9 us -> 36.6 us
  matrix products: 4.94 us -> 8.01 us
    all_to_all x3, waiting for transfers between devices: 44.4 us -> 26.9 us  [exchange(): return lax.all_to_all(parts, axis, split_axis=0, concat_axis=0, tiled=True)]
    all_to_all x2, blocking collectives: 31.9 us -> 36.6 us  [exchange(): return lax.all_to_all(parts, axis, split_axis=0, concat_axis=0, tiled=True)]
    ppermute x1 -> x3, starting transfers between devices: 3.47 us -> 7.98 us  [the longest x1 3.62 us: per_device(): core_head = lax.ppermute(lm_head, 'heads_1', SWAP)]
    dot_general x2 -> x4, matrix products: 2.34 us -> 5.41 us  [per_device(): logits = jnp.dot(operand, matrix, preferred_element_type=jnp.float32)]
    all_to_all x3, starting transfers between devices: 17.6 us -> 20.5 us  [exchange(): return lax.all_to_all(parts, axis, split_axis=0, concat_axis=0, tiled=True)]
  transfers between devices with their start and end apart: 4 -> 6, of which waited for: 3 -> 3; matrix products, arithmetic and copies ran while one was open for 2% -> 7% of each run, Pallas kernels for 0% -> 0%
where the time goes in v2:
time: 118 us; the launch traced here: 117 us
  blocking collectives  36.6 us (31%)
  starting transfers between devices  28.4 us (24%)
  waiting for transfers between devices  26.9 us (23%)
  local copies, waits for them, and re-layouts  8.86 us (8%)
  matrix products  8.01 us (7%)
  other arithmetic  5.98 us (5%)
  between operations  2.4 us (2%)
    all_to_all x2, blocking collectives, exchange(): return lax.all_to_all(parts, axis, split_axis=0, concat_axis=0, tiled=True)  36.6 us
    all_to_all x3, waiting for transfers between devices, exchange(): return lax.all_to_all(parts, axis, split_axis=0, concat_axis=0, tiled=True)  26.9 us
    all_to_all x3, starting transfers between devices, exchange(): return lax.all_to_all(parts, axis, split_axis=0, concat_axis=0, tiled=True)  20.5 us
    dot_general x4, matrix products, per_device(): logits = jnp.dot(operand, matrix, preferred_element_type=jnp.float32)  5.41 us
    dot_general x2, local copies, waits for them, and re-layouts, per_device(): jnp.dot(for_owner, out_proj, preferred_element_type=jnp.float32)  4.09 us
    ppermute x1, starting transfers between devices, per_device(): core_head = lax.ppermute(lm_head, 'heads_1', SWAP)  3.62 us
    ppermute x1, starting transfers between devices, per_device(): z_head = lax.ppermute(lm_head, 'z_side', SWAP)  2.44 us
  transfers between devices with their start and end apart: 6, of which 3 were waited for; matrix products, arithmetic and copies ran while one was open for 7% of the time, Pallas kernels for 0%

profile of v2, /device:TPU:1, one launch (start us, length us, event | category | flops | bytes accessed | tf_op | source)
XLA Modules:
  0.0 117.2 jit_solution(9769751632973606343)
XLA Ops:
  0.7 0.8 fusion.5
  1.6 0.8 fusion.3
  2.3 0.9 fusion.20
  3.2 1.0 fusion.14
  4.2 1.0 fusion.16
  5.3 0.2 multiply_reduce_fusion.1
  5.6 3.3 %copy.109 = bf16[4096,256]{1,0:T(8,128)(2,1)S(1)} copy(bf16[4096,256]{0,1:T(8,128)(2,1)} %bitcast.120) | data formatting | bytes 4194304 | tf_op jit(solution)/shard_map/dot_general | solution.py:102
  8.9 0.6 fusion.34
  9.6 0.8 copy.93
  10.4 10.2 %all-to-all-start = ((f32[16,32,128]{2,1,0:T(8,128)}), f32[16,32,128]{2,1,0:T(8,128)S(1)}, u32[]{:S(2)}, u32[]{:S(2)}) async-start(f32[16,32,128]{2,1,0:T(8,128)} %copy.93), calls=%async_computation | async-start | bytes 524288 | tf_op jit(solution)/shard_map/all_to_all | solution.py:18
  20.6 2.4 %collective-permute-start.1 = (bf16[4096,128]{1,0:T(8,128)(2,1)}, bf16[4096,128]{1,0:T(8,128)(2,1)}, u32[]{:S(2)}, u32[]{:S(2)}) collective-permute-start(bf16[4096,128]{1,0:T(8,128)(2,1)} %param.28), channel_id=1, source_target_pairs={{0,4},{4,0},{1,5},{5,1},{2,6},{6,2},{3,7},{7,3},{8,12},{12,8},{9,1... | collective-permute-start | bytes 3145736 | tf_op jit(solution)/shard_map/ppermute | solution.py:84
  23.0 9.3 %all-to-all-done = f32[16,32,128]{2,1,0:T(8,128)S(1)} async-done(((f32[16,32,128]{2,1,0:T(8,128)}), f32[16,32,128]{2,1,0:T(8,128)S(1)}, u32[]{:S(2)}, u32[]{:S(2)}) %all-to-all-start) | async-done | bytes 262176 | tf_op jit(solution)/shard_map/all_to_all | solution.py:18
  32.3 1.5 %multiply_reduce_fusion = (f32[]{:T(128)}, f32[1,4096]{1,0:T(1,128)S(1)}) fusion(f32[1,4096]{1,0:T(1,128)S(1)} %bitcast.125, bf16[8,4096]{1,0:T(8,128)(2,1)} %param.25, s32[]{:T(128)S(6)} %select_n.47), kind=kLoop, calls=%fused_computation.13 | loop fusion | flops 16383 | bytes 40968 | tf_op jit(solution)/shard_map/reduce_sum | solution.py:109
  34.6 23.2 %all_to_all.25 = bf16[16,16,128]{2,1,0:T(8,128)(2,1)S(1)} all-to-all(bf16[16,16,128]{2,1,0:T(8,128)(2,1)S(1)} %broadcast_in_dim.19), channel_id=1, replica_groups=mesh['heads_0'=8,'heads_1'=2,'z_pair'=4,'z_side'=2,'x'=4] {'z_pair','x'}, dimensions={0} | all-to-all | bytes 131072 | tf_op jit(solution)/shard_map/all_to_all | solution.py:18
  57.8 0.8 broadcast_in_dim.22
  58.7 6.3 %all-to-all-start.2 = ((bf16[8,16,2048]{2,1,0:T(8,128)(2,1)}), bf16[8,16,2048]{2,1,0:T(8,128)(2,1)S(1)}, u32[]{:S(2)}, u32[]{:S(2)}) async-start(bf16[8,16,2048]{2,1,0:T(8,128)(2,1)} %broadcast_in_dim.22), calls=%async_computation.2 | async-start | bytes 1048576 | tf_op jit(solution)/shard_map/all_to_all | solution.py:18
  65.0 3.6 %collective-permute-start = (bf16[4096,128]{1,0:T(8,128)(2,1)S(1)}, bf16[4096,128]{1,0:T(8,128)(2,1)}, u32[]{:S(2)}, u32[]{:S(2)}) collective-permute-start(bf16[4096,128]{1,0:T(8,128)(2,1)S(1)} %copy-done.1), channel_id=1, source_target_pairs={{0,32},{32,0},{1,33},{33,1},{2,34},{34,2},{3,35},{35,3},{4,36},{36... | collective-permute-start | bytes 3145736 | tf_op jit(solution)/shard_map/ppermute | solution.py:85
  68.6 0.1 reshape.288
  68.8 1.9 %collective-permute-start.2 = (bf16[4096,128]{1,0:T(8,128)(2,1)}, bf16[4096,128]{1,0:T(8,128)(2,1)}, u32[]{:S(2)}, u32[]{:S(2)}) collective-permute-start(bf16[4096,128]{1,0:T(8,128)(2,1)} %collective-permute-done.1), channel_id=1, source_target_pairs={{0,32},{32,0},{1,33},{33,1},{2,34},{34,2},{3,35},{35,3},{4,36},{36... | collective-permute-start | bytes 3145736 | tf_op jit(solution)/shard_map/ppermute | solution.py:86
  70.8 0.1 eq.14
  70.9 10.1 %all-to-all-done.2 = bf16[8,16,2048]{2,1,0:T(8,128)(2,1)S(1)} async-done(((bf16[8,16,2048]{2,1,0:T(8,128)(2,1)}), bf16[8,16,2048]{2,1,0:T(8,128)(2,1)S(1)}, u32[]{:S(2)}, u32[]{:S(2)}) %all-to-all-start.2) | async-done | bytes 524320 | tf_op jit(solution)/shard_map/all_to_all | solution.py:18
  81.0 0.5 copy.94
  81.5 0.2 copy.113
  81.7 0.4 fusion.32
  82.1 1.7 %fusion.31 = (f32[64]{0:T(128)S(1)}, f32[64,128]{1,0:T(8,128)S(1)}) fusion(bf16[64,4096]{1,0:T(8,128)(2,1)S(1)} %bitcast.116, bf16[4096,128]{1,0:T(8,128)(2,1)} %collective-permute-done.1), kind=kOutput, calls=%fused_computation.80 | convolution fusion | flops 67116992 | bytes 1605888 | tf_op jit(solution)/shard_map/dot_general | solution.py:129
  83.8 1.7 %fusion.33 = (f32[64]{0:T(128)S(1)}, f32[64,128]{1,0:T(8,128)S(1)}) fusion(bf16[64,4096]{1,0:T(8,128)(2,1)S(1)} %bitcast.117, bf16[4096,128]{1,0:T(8,128)(2,1)} %collective-permute-done), kind=kOutput, calls=%fused_computation.82 | convolution fusion | flops 67116992 | bytes 1605888 | tf_op jit(solution)/shard_map/dot_general | solution.py:129
  85.5 1.7 %fusion.30 = (f32[64]{0:T(128)S(1)}, f32[64,128]{1,0:T(8,128)S(1)}) fusion(bf16[64,4096]{1,0:T(8,128)(2,1)S(1)} %bitcast.118, bf16[4096,128]{1,0:T(8,128)(2,1)} %collective-permute-done.2), kind=kOutput, calls=%fused_computation.79 | convolution fusion | flops 67116992 | bytes 1605888 | tf_op jit(solution)/shard_map/dot_general | solution.py:129
  87.2 0.1 reduce_max.115
  87.3 0.3 exponential_reduce_fusion
  87.6 0.1 add.249
  87.7 0.1 add.227
  87.8 0.7 copy.96
  88.5 4.0 %all-to-all-start.3 = ((f32[16,1,12]{2,1,0:T(1,128)}), f32[16,1,12]{2,1,0:T(1,128)S(1)}, u32[]{:S(2)}, u32[]{:S(2)}) async-start(f32[16,1,12]{2,1,0:T(1,128)} %copy.96), calls=%async_computation.3 | async-start | bytes 16384 | tf_op jit(solution)/shard_map/all_to_all | solution.py:18
  92.4 0.6 fusion.2
  93.7 7.6 %all-to-all-done.3 = f32[16,1,12]{2,1,0:T(1,128)S(1)} async-done(((f32[16,1,12]{2,1,0:T(1,128)}), f32[16,1,12]{2,1,0:T(1,128)S(1)}, u32[]{:S(2)}, u32[]{:S(2)}) %all-to-all-start.3) | async-done | bytes 800 | tf_op jit(solution)/shard_map/all_to_all | solution.py:18
  101.3 0.1 copy.97
  101.4 0.1 slice_reduce_fusion.2
  101.5 0.2 fusion.25
  101.8 13.4 %all_to_all.26 = f32[16,1,13]{2,1,0:T(1,128)S(1)} all-to-all(f32[16,1,13]{2,1,0:T(1,128)S(1)} %broadcast_in_dim.25), channel_id=1, replica_groups=mesh['heads_0'=8,'heads_1'=2,'z_pair'=4,'z_side'=2,'x'=4] {'heads_0','he..., dimensions={0} | all-to-all | bytes 1664 | tf_op jit(solution)/shard_map/all_to_all | solution.py:18
  115.3 0.1 copy.98
  115.3 0.1 fusion.29
  115.4 0.1 copy.101
  115.5 0.2 fusion.23
  115.7 0.1 copy.102
  115.8 0.1 copy.103
  115.9 0.6 sub.76
  116.5 0.1 copy.104
  116.6 0.6 reshape.295
  (54 shorter events, 0.7 us)
Async XLA Ops:
  0.6 2.6 %copy-start = (f32[8,2,128,128]{3,2,1,0:T(8,128)S(1)}, f32[8,2,128,128]{3,2,1,0:T(8,128)}, u32[]{:S(2)}) copy-start(f32[8,2,128,128]{3,2,1,0:T(8,128)} %param.22) | copy-start | bytes 3145732
  0.6 4.5 %copy-start.10 = (f32[2]{0:T(128)S(1)}, f32[2]{0:T(128)}, u32[]{:S(2)}) copy-start(f32[2]{0:T(128)} %param.21) | copy-start | bytes 28
  0.7 4.5 %copy-start.6 = (f32[8,2]{0,1:T(2,128)S(1)}, f32[8,2]{0,1:T(2,128)}, u32[]{:S(2)}) copy-start(f32[8,2]{0,1:T(2,128)} %param.20) | copy-start | bytes 196
  0.7 4.5 %copy-start.8 = (f32[8,2]{0,1:T(2,128)S(1)}, f32[8,2]{0,1:T(2,128)}, u32[]{:S(2)}) copy-start(f32[8,2]{0,1:T(2,128)} %param.19) | copy-start | bytes 196
  0.7 4.6 %copy-start.4 = (bf16[8,256]{1,0:T(8,128)(2,1)S(1)}, bf16[8,256]{1,0:T(8,128)(2,1)}, u32[]{:S(2)}) copy-start(bf16[8,256]{1,0:T(8,128)(2,1)} %param.17) | copy-start | bytes 12292
  0.7 4.8 %copy-start.5 = (bf16[8,256]{1,0:T(8,128)(2,1)S(1)}, bf16[8,256]{1,0:T(8,128)(2,1)}, u32[]{:S(2)}) copy-start(bf16[8,256]{1,0:T(8,128)(2,1)} %param.18) | copy-start | bytes 12292
  0.7 4.8 %copy-start.9 = (f32[128]{0:T(128)S(1)}, f32[128]{0:T(128)}, u32[]{:S(2)}) copy-start(f32[128]{0:T(128)} %param.23) | copy-start | bytes 1540
  8.9 25.6 %copy-start.2 = (f32[4096]{0:T(1024)S(1)}, f32[4096]{0:T(1024)}, u32[]{:S(2)}) copy-start(f32[4096]{0:T(1024)} %param.26) | copy-start | bytes 49156
  9.6 55.4 %copy-start.1 = (bf16[4096,128]{1,0:T(8,128)(2,1)S(1)}, bf16[4096,128]{1,0:T(8,128)(2,1)}, u32[]{:S(2)}) copy-start(bf16[4096,128]{1,0:T(8,128)(2,1)} %param.28) | copy-start | bytes 3145732
  9.6 59.0 %copy-start.7 = (s32[256]{0:T(256)S(1)}, s32[256]{0:T(256)}, u32[]{:S(2)}) copy-start(s32[256]{0:T(256)} %param.29) | copy-start | bytes 3076
  10.4 21.9 %all-to-all-start = ((f32[16,32,128]{2,1,0:T(8,128)}), f32[16,32,128]{2,1,0:T(8,128)S(1)}, u32[]{:S(2)}, u32[]{:S(2)}) async-start(f32[16,32,128]{2,1,0:T(8,128)} %copy.93), calls=%async_computation | async-start | bytes 524288 | tf_op jit(solution)/shard_map/all_to_all | solution.py:18
  20.6 48.2 %collective-permute-start.1 = (bf16[4096,128]{1,0:T(8,128)(2,1)}, bf16[4096,128]{1,0:T(8,128)(2,1)}, u32[]{:S(2)}, u32[]{:S(2)}) collective-permute-start(bf16[4096,128]{1,0:T(8,128)(2,1)} %param.28), channel_id=1, source_target_pairs={{0,4},{4,0},{1,5},{5,1},{2,6},{6,2},{3,7},{7,3},{8,12},{12,8},{9,1... | collective-permute-start | bytes 3145736 | tf_op jit(solution)/shard_map/ppermute | solution.py:84
  58.7 22.3 %all-to-all-start.2 = ((bf16[8,16,2048]{2,1,0:T(8,128)(2,1)}), bf16[8,16,2048]{2,1,0:T(8,128)(2,1)S(1)}, u32[]{:S(2)}, u32[]{:S(2)}) async-start(bf16[8,16,2048]{2,1,0:T(8,128)(2,1)} %broadcast_in_dim.22), calls=%async_computation.2 | async-start | bytes 1048576 | tf_op jit(solution)/shard_map/all_to_all | solution.py:18
  65.0 18.8 %collective-permute-start = (bf16[4096,128]{1,0:T(8,128)(2,1)S(1)}, bf16[4096,128]{1,0:T(8,128)(2,1)}, u32[]{:S(2)}, u32[]{:S(2)}) collective-permute-start(bf16[4096,128]{1,0:T(8,128)(2,1)S(1)} %copy-done.1), channel_id=1, source_target_pairs={{0,32},{32,0},{1,33},{33,1},{2,34},{34,2},{3,35},{35,3},{4,36},{36... | collective-permute-start | bytes 3145736 | tf_op jit(solution)/shard_map/ppermute | solution.py:85
  68.8 16.7 %collective-permute-start.2 = (bf16[4096,128]{1,0:T(8,128)(2,1)}, bf16[4096,128]{1,0:T(8,128)(2,1)}, u32[]{:S(2)}, u32[]{:S(2)}) collective-permute-start(bf16[4096,128]{1,0:T(8,128)(2,1)} %collective-permute-done.1), channel_id=1, source_target_pairs={{0,32},{32,0},{1,33},{33,1},{2,34},{34,2},{3,35},{35,3},{4,36},{36... | collective-permute-start | bytes 3145736 | tf_op jit(solution)/shard_map/ppermute | solution.py:86
  83.8 8.6 %copy-start.3 = (f32[4096]{0:T(1024)S(1)}, f32[4096]{0:T(1024)}, u32[]{:S(2)}) copy-start(f32[4096]{0:T(1024)} %param.27) | copy-start | bytes 49156
  88.5 12.8 %all-to-all-start.3 = ((f32[16,1,12]{2,1,0:T(1,128)}), f32[16,1,12]{2,1,0:T(1,128)S(1)}, u32[]{:S(2)}, u32[]{:S(2)}) async-start(f32[16,1,12]{2,1,0:T(1,128)} %copy.96), calls=%async_computation.3 | async-start | bytes 16384 | tf_op jit(solution)/shard_map/all_to_all | solution.py:18

commit v3 on v2

v3 whole, which is shorter than its diff:
```python
import jax
import jax.numpy as jnp
from jax import lax
from jax.experimental import pallas as pl
from jax.experimental.pallas import tpu as pltpu
from jax.sharding import Mesh
from jax.sharding import PartitionSpec as P

HEADS = ("heads_0", "heads_1")
BATCH = ("z_pair", "z_side", "x")
GROUP = ("z_pair", "x")
HEADS_BATCH = ("heads_0", "heads_1", "z_pair", "z_side", "x")
SWAP = [(0, 1), (1, 0)]


epsilon = 1e-06


def exchange(parts, axis):
    return lax.all_to_all(parts, axis, split_axis=0, concat_axis=0, tiled=True)


def copy_for_each(array, axis):
    size = lax.axis_size(axis)
    return exchange(jnp.broadcast_to(array[None], (size, *array.shape)), axis)


def any_spec():
    return pl.BlockSpec(memory_space=pl.ANY)


def vmem_spec():
    return pl.BlockSpec(memory_space=pltpu.VMEM)


def smem_spec():
    return pl.BlockSpec(memory_space=pltpu.SMEM)


def as_column(line):
    size = line.shape[1]
    shape = (size, size)
    here = lax.broadcasted_iota(jnp.int32, shape, 0) == lax.broadcasted_iota(jnp.int32, shape, 1)
    return jnp.sum(jnp.where(here, jnp.broadcast_to(line, shape), 0.0), axis=1, keepdims=True)


def heads_kernel(
    first_ref,
    rate_ref,
    *refs,
):
    inputs, out_ref, local, sems = refs[:10], refs[10], refs[11:21], refs[21]
    q_ref, k_ref, v_ref, g_ref, dl_ref, bl_ref, gain_ref, res_ref, state_ref, proj_ref = local
    copies = [pltpu.make_async_copy(inputs[n], local[n], sems.at[n]) for n in range(8)]
    heads = state_ref.shape[1]
    for h in range(heads):
        copies.append(
            pltpu.make_async_copy(inputs[8].at[:, h], state_ref.at[:, h], sems.at[8 + h])
        )
    blocks = 4
    wide = proj_ref.shape[1] // blocks
    for n in range(blocks):
        part = pl.ds(n * wide, wide)
        copies.append(
            pltpu.make_async_copy(
                inputs[9].at[:, part], proj_ref.at[:, part], sems.at[8 + heads + n]
            )
        )
    for copy in copies:
        copy.start()
    for copy in copies[:8]:
        copy.wait()
    rows = q_ref.shape[0]
    size = state_ref.shape[2]
    gain = gain_ref[...]
    queries, keys = [], []
    for h in range(heads):
        lanes = slice(h * size, (h + 1) * size)
        query = q_ref[:, lanes].astype(jnp.float32)
        key = k_ref[:, lanes].astype(jnp.float32)
        query = query / jnp.sqrt(jnp.sum(query * query, axis=1, keepdims=True) + epsilon)
        queries.append(query * size ** (-0.5))
        keys.append(key / jnp.sqrt(jnp.sum(key * key, axis=1, keepdims=True) + epsilon))
    turned = jnp.concatenate(queries + keys, axis=0).T
    parts = []
    for h in range(heads):
        lanes = slice(h * size, (h + 1) * size)
        logit = dl_ref[h : h + 1, :]
        soft = jnp.maximum(logit, 0.0) + jnp.log1p(jnp.exp(-jnp.abs(logit)))
        decay = as_column(jnp.exp(-rate_ref[h] * soft))
        strength = as_column(1.0 / (1.0 + jnp.exp(-bl_ref[h : h + 1, :])))
        inter = jnp.sum(queries[h] * keys[h], axis=1, keepdims=True)
        value = v_ref[:, lanes].astype(jnp.float32)
        gate = g_ref[:, lanes].astype(jnp.float32)
        copies[8 + h].wait()
        by_query, by_key = [], []
        for b in range(rows):
            block = state_ref[b, h]
            at = h * rows + b
            by_query.append(jnp.sum(turned[:, at : at + 1] * block, axis=0, keepdims=True))
            at += heads * rows
            by_key.append(jnp.sum(turned[:, at : at + 1] * block, axis=0, keepdims=True))
        state_query = jnp.concatenate(by_query, axis=0)
        state_key = jnp.concatenate(by_key, axis=0)
        written = value - decay * state_key
        output = decay * state_query + strength * inter * written
        mean = jnp.mean(output * output, axis=1, keepdims=True)
        normed = output / jnp.sqrt(mean + epsilon)
        parts.append(normed * gain * (gate / (1.0 + jnp.exp(-gate))))
    headout = jnp.concatenate(parts, axis=1).astype(jnp.bfloat16)
    first = first_ref[0]
    lines = wide // 128
    cores, halves = 2, out_ref.shape[0] // rows
    for n in range(blocks):
        copies[8 + heads + n].wait()
        part = slice(n * wide, (n + 1) * wide)
        total = jnp.dot(headout, proj_ref[:, part], preferred_element_type=jnp.float32)
        total = total + res_ref[:, part].astype(jnp.float32) * first
        total = total.reshape(rows, lines, 128)
        for row in range(rows):
            for half in range(halves):
                core, r = row // (rows // cores), row % (rows // cores)
                place = (r * halves + half) * cores + core
                out_ref[place, n * lines : (n + 1) * lines, :] = total[row]


def head_partials(
    queries,
    keys_new,
    values_new,
    out_gate,
    decay_logit,
    beta_logit,
    decay_rate,
    state,
    norm_gain,
    out_proj,
    residual,
    first,
    places,
):
    arrays = (
        queries,
        keys_new,
        values_new,
        out_gate,
        decay_logit.T,
        beta_logit.T,
        norm_gain.reshape(1, -1),
        residual,
        state,
        out_proj,
    )
    width = out_proj.shape[1]
    return pl.pallas_call(
        heads_kernel,
        out_shape=jax.ShapeDtypeStruct((places, width // 128, 128), jnp.float32),
        in_specs=[smem_spec(), smem_spec()] + [any_spec() for _ in arrays],
        out_specs=vmem_spec(),
        scratch_shapes=[pltpu.VMEM(a.shape, a.dtype) for a in arrays]
        + [pltpu.SemaphoreType.DMA((8 + state.shape[1] + 4,))],
        cost_estimate=pl.CostEstimate(flops=40000000, bytes_accessed=3500000, transcendentals=0),
        name="heads",
    )(first, decay_rate, *arrays)


def norm_kernel(half_ref, arrived_ref, gain_ref, weight_ref, piece_ref, value_ref, scratch):
    width = gain_ref.size
    hsum = arrived_ref[0]
    for n in range(1, arrived_ref.shape[0]):
        hsum = hsum + arrived_ref[n]
    gain = gain_ref[...]
    squares = jnp.sum(hsum * hsum, axis=(0, 1), keepdims=True)
    terms = jnp.sum(hsum * gain * weight_ref[...], axis=(0, 1), keepdims=True)
    rstd = 1.0 / jnp.sqrt(squares / width + epsilon)
    scratch[...] = hsum * rstd * gain
    lines = piece_ref.shape[1]
    start = pl.multiple_of(half_ref[0] * lines, lines)
    piece = scratch[pl.ds(start, lines), :].astype(jnp.bfloat16)
    for n in range(piece_ref.shape[0]):
        piece_ref[n] = piece
    value_ref[...] = jnp.broadcast_to(rstd * terms, value_ref.shape)


def norm_pieces(arrived, gain, weight, half, copies, lines):
    return pl.pallas_call(
        norm_kernel,
        out_shape=(
            jax.ShapeDtypeStruct((copies, lines, 128), jnp.bfloat16),
            jax.ShapeDtypeStruct((1, 128), jnp.float32),
        ),
        in_specs=[smem_spec(), vmem_spec(), vmem_spec(), vmem_spec()],
        out_specs=(vmem_spec(), vmem_spec()),
        scratch_shapes=[pltpu.VMEM(gain.shape, jnp.float32)],
        cost_estimate=pl.CostEstimate(flops=4000000, bytes_accessed=400000, transcendentals=0),
        name="norm",
    )(half, arrived, gain, weight)


def logits_kernel(firsts_ref, rows_ref, ids_ref, *refs):
    count = 4
    matrices, out_ref, local, sems = refs[:count], refs[count], refs[count + 1], refs[count + 2]
    pieces, groups, deep = rows_ref.shape
    halves = local.shape[1] // deep
    copies = []
    for k in range(halves):
        part = pl.ds(k * deep, deep)
        for n in range(count):
            at = k * count + n
            copies.append(
                pltpu.make_async_copy(
                    matrices[n].at[part], local.at[n, part], sems.at[at]
                )
            )
    for copy in copies:
        copy.start()
    sums = [None] * count
    for k in range(halves):
        part = slice(k * deep, (k + 1) * deep)
        lhs = jnp.concatenate([rows_ref[p] for p in range(k, pieces, halves)], axis=0)
        for n in range(count):
            copies[k * count + n].wait()
            term = jnp.dot(lhs, local[n, part], preferred_element_type=jnp.float32)
            sums[n] = term if k == 0 else sums[n] + term
    top = sums[0]
    for n in range(1, count):
        top = jnp.maximum(top, sums[n])
    top = jnp.max(top, axis=1, keepdims=True)
    ids = ids_ref[...]
    total = jnp.zeros(sums[0].shape, jnp.float32)
    chosen = jnp.zeros(sums[0].shape, jnp.float32)
    for n in range(count):
        total = total + jnp.exp(sums[n] - top)
        columns = lax.broadcasted_iota(jnp.int32, sums[n].shape, 1) + firsts_ref[n]
        chosen = chosen + jnp.where(columns == ids, sums[n], 0.0)
    total = jnp.sum(total, axis=1, keepdims=True)
    chosen = jnp.sum(chosen, axis=1, keepdims=True)
    lane = lax.broadcasted_iota(jnp.int32, (groups, 128), 1)
    packed = jnp.zeros((groups, 128), jnp.float32)
    owned = pieces // halves
    for n, column in enumerate((top, total, chosen)):
        for r in range(owned):
            part = column[r * groups : (r + 1) * groups]
            packed = jnp.where(lane == n * owned + r, part, packed)
    for g in range(groups):
        out_ref[g] = packed[g : g + 1]


def logit_stats(all_rows, matrices, firsts, ids):
    groups = all_rows.shape[1]
    depth = matrices[0].shape[0]
    return pl.pallas_call(
        logits_kernel,
        out_shape=jax.ShapeDtypeStruct((groups, 1, 128), jnp.float32),
        in_specs=[smem_spec(), vmem_spec(), vmem_spec()] + [any_spec() for _ in matrices],
        out_specs=vmem_spec(),
        scratch_shapes=[
            pltpu.VMEM((len(matrices), depth, 128), jnp.bfloat16),
            pltpu.SemaphoreType.DMA((2 * len(matrices),)),
        ],
        cost_estimate=pl.CostEstimate(flops=270000000, bytes_accessed=4700000, transcendentals=0),
        name="logits",
    )(firsts, all_rows, ids, *matrices)


def merged(top, total, chosen, axis):
    highest = jnp.max(top, axis=axis, keepdims=True)
    scaled = jnp.sum(total * jnp.exp(top - highest), axis=axis)
    return jnp.squeeze(highest, axis), scaled, jnp.sum(chosen, axis=axis)


def per_device(
    queries,
    keys_new,
    values_new,
    out_gate,
    decay_logit,
    beta_logit,
    decay_rate,
    state,
    norm_gain,
    out_proj,
    residual,
    final_gain,
    value_weight,
    lm_head,
    sampled,
):
    chips, cores = lax.axis_size("heads_0"), lax.axis_size("heads_1")
    groups = lax.axis_size(GROUP)
    chip, core = lax.axis_index("heads_0"), lax.axis_index("heads_1")
    side = lax.axis_index("z_side")
    rows_own, width = residual.shape
    rows_core = rows_own // cores
    copies = chips // rows_core
    lanes = 128
    lines = width // lanes
    half = width // copies

    z_head = lax.ppermute(lm_head, "z_side", SWAP)
    core_head = lax.ppermute(lm_head, "heads_1", SWAP)
    both_head = lax.ppermute(z_head, "heads_1", SWAP)

    first = jnp.where((chip == 0) & (core == 0), 1.0, 0.0).reshape(1)
    partial_out = head_partials(
        queries,
        keys_new,
        values_new,
        out_gate,
        decay_logit,
        beta_logit,
        decay_rate,
        state,
        norm_gain,
        out_proj,
        residual,
        first,
        chips * cores,
    )
    arrived = exchange(partial_out, HEADS)
    gain = final_gain.reshape(lines, lanes)
    weight = value_weight.reshape(lines, lanes)
    half_here = (chip % copies).astype(jnp.int32).reshape(1)
    pieces, value = norm_pieces(arrived, gain, weight, half_here, groups, lines // copies)
    all_groups = exchange(pieces, GROUP).reshape(groups, half)
    all_rows = copy_for_each(all_groups, "heads_0")

    vocab_own = lm_head.shape[1]
    flat = lax.axis_index(HEADS_BATCH)
    across = (1 - 2 * core) * lax.axis_size(BATCH)
    along = (1 - 2 * side) * lax.axis_size("x")
    matrices = (lm_head, core_head, z_head, both_head)
    firsts = jnp.stack([flat, flat + across, flat + along, flat + across + along]) * vocab_own
    ids = sampled.reshape(-1, lax.axis_size("z_side"), lax.axis_size("x"), cores, rows_core)
    ids = lax.dynamic_index_in_dim(ids, side, 1, keepdims=False)
    ids = lax.dynamic_index_in_dim(ids, core, 2, keepdims=False)
    ids = ids.reshape(groups, rows_core).T.reshape(-1, 1)
    stats = logit_stats(all_rows, matrices, firsts.astype(jnp.int32), ids)
    stats = exchange(stats, GROUP)[:, 0, : 3 * rows_core].reshape(groups, 3, rows_core)
    stats = merged(stats[:, 0], stats[:, 1], stats[:, 2], 0)
    packed = jnp.concatenate([*stats, value[0, :1]])
    packed = copy_for_each(packed[None], HEADS).reshape(chips, cores, -1)
    found = packed[..., : 3 * rows_core].reshape(chips, cores, 3, rows_core)
    top, total, chosen = merged(found[:, :, 0], found[:, :, 1], found[:, :, 2], 0)
    logprob = (chosen - (top + jnp.log(total))).reshape(-1)
    values = packed[::copies, :, 3 * rows_core].T.reshape(-1)
    return (logprob, values)


def solution(mesh):
    torus = Mesh(
        mesh.devices.reshape(8, 2, 4, 2, 4), ("heads_0", "heads_1", "z_pair", "z_side", "x")
    )
    return jax.shard_map(
        per_device,
        mesh=torus,
        in_specs=(
            P(BATCH, HEADS),
            P(BATCH, HEADS),
            P(BATCH, HEADS),
            P(BATCH, HEADS),
            P(BATCH, HEADS),
            P(BATCH, HEADS),
            P(HEADS),
            P(BATCH, HEADS, None, None),
            P(),
            P(HEADS, None),
            P(BATCH, None),
            P(),
            P(),
            P(None, HEADS_BATCH),
            P(),
        ),
        out_specs=(P(BATCH), P(BATCH)),
        check_vma=False,
    )
```

time: 118 us -> 113 us (0.958)
  Pallas kernels: 0 us -> 11 us
  blocking collectives: 36.6 us -> 46.1 us
  matrix products: 8.01 us -> 0 us
  waiting for transfers between devices: 26.9 us -> 19 us
  other arithmetic: 5.98 us -> 1.31 us
  local copies, waits for them, and re-layouts: 8.86 us -> 5.13 us
  between operations: 2.4 us -> 0.79 us
    all_to_all x3 -> x2, waiting for transfers between devices: 26.9 us -> 14.5 us  [exchange(): return lax.all_to_all(parts, axis, split_axis=0, concat_axis=0, tiled=True)]
    pallas_call x0 -> x3, Pallas kernels: none -> 11 us  [the longest x1 4.77 us: logit_stats(): pl.pallas_call(logits_kernel, out_shape=jax.ShapeDtypeStruct((groups, 1,...]
    all_to_all x2 -> x3, blocking collectives: 36.6 us -> 46.1 us  [exchange(): return lax.all_to_all(parts, axis, split_axis=0, concat_axis=0, tiled=True)]
    dot_general x7 -> x0, matrix products: 8.01 us -> none  [the longest x4 5.41 us: per_device(): logits = jnp.dot(operand, matrix, preferred_element_type=jnp.float32)]
    all_to_all x3 -> x2, starting transfers between devices: 20.5 us -> 14.9 us  [exchange(): return lax.all_to_all(parts, axis, split_axis=0, concat_axis=0, tiled=True)]
    ppermute x1, starting transfers between devices: 1.92 us -> 7.06 us  [per_device(): both_head = lax.ppermute(z_head, 'heads_1', SWAP)]
    ppermute x1, waiting for transfers between devices: 0.01 us -> 4.55 us  [per_device(): z_head = lax.ppermute(lm_head, 'z_side', SWAP)]
    reduce_sum x7 -> x0, other arithmetic: 4.2 us -> none  [the longest x1 1.49 us: per_device(): rstd = 1.0 / jnp.sqrt(jnp.sum(hsum * hsum) / width + epsilon)]
  transfers between devices with their start and end apart: 6 -> 5, of which waited for: 3 -> 2; matrix products, arithmetic and copies ran while one was open for 7% -> 2% of each run, Pallas kernels for 0% -> 6%
where the time goes in v3:
time: 113 us; the launch traced here: 112 us
  blocking collectives  46.1 us (41%)
  starting transfers between devices  28.9 us (26%)
  waiting for transfers between devices  19 us (17%)
  Pallas kernels  11 us (10%)
  local copies, waits for them, and re-layouts  5.13 us (5%)
  other arithmetic  1.31 us (1%)
    all_to_all x3, blocking collectives, exchange(): return lax.all_to_all(parts, axis, split_axis=0, concat_axis=0, tiled=True)  46.1 us
    all_to_all x2, starting transfers between devices, exchange(): return lax.all_to_all(parts, axis, split_axis=0, concat_axis=0, tiled=True)  14.9 us
    all_to_all x2, waiting for transfers between devices, exchange(): return lax.all_to_all(parts, axis, split_axis=0, concat_axis=0, tiled=True)  14.5 us
    ppermute x1, starting transfers between devices, per_device(): both_head = lax.ppermute(z_head, 'heads_1', SWAP)  7.06 us
    ppermute x1, starting transfers between devices, per_device(): z_head = lax.ppermute(lm_head, 'z_side', SWAP)  4.95 us
    pallas_call x1, Pallas kernels, logit_stats(): pl.pallas_call(logits_kernel, out_shape=jax.ShapeDtypeStruct((groups, 1,...  4.77 us
    ppermute x1, waiting for transfers between devices, per_device(): z_head = lax.ppermute(lm_head, 'z_side', SWAP)  4.55 us
    pallas_call x1, Pallas kernels, head_partials(): pl.pallas_call(heads_kernel, out_shape=jax.ShapeDtypeStruct((places, widt...  4.45 us
  transfers between devices with their start and end apart: 5, of which 2 were waited for; matrix products, arithmetic and copies ran while one was open for 2% of the time, Pallas kernels for 6%

profile of v3, /device:TPU:1, one launch (start us, length us, event | category | flops | bytes accessed | tf_op | source)
XLA Modules:
  0.0 112.3 jit_solution(12388200007267327119)
XLA Ops:
  0.6 0.0 copy-start.1
  0.6 5.0 %collective-permute-start.1 = (bf16[4096,128]{1,0:T(8,128)(2,1)}, bf16[4096,128]{1,0:T(8,128)(2,1)S(1)}, u32[]{:S(2)}, u32[]{:S(2)}) collective-permute-start(bf16[4096,128]{1,0:T(8,128)(2,1)} %refs_0_.3), channel_id=1, source_target_pairs={{0,4},{4,0},{1,5},{5,1},{2,6},{6,2},{3,7},{7,3},{8,12},{12,8},{9,1... | collective-permute-start | bytes 3145736 | tf_op jit(solution)/shard_map/ppermute | solution.py:300
  5.6 4.5 %heads.1 = f32[16,32,128]{2,1,0:T(8,128)} custom-call(f32[1]{0:T(128)} %bitcast.5.first_ref, f32[2]{0:T(128)} %rate_ref.1, bf16[8,256]{1,0:T(8,128)(2,1)} %refs_0_.2, bf16[8,256]{1,0:T(8,128)(2,1)} %refs_1_.1, bf16[8,256]{1,0:T(8,128)(2,1)} %refs_2_.1, bf16[8,256]{1,0:T(8,128)(2,1)} %refs_3_.1, f32[2,8]{1,0:T(2,128)} %bitcast.60, f32[2,8]{1,0:T(2,128)} %bitcast.61, ...), custom_call_target="tpu_custom_call" | custom-call | flops 40000000 | bytes 3500000 | tf_op jit(solution)/shard_map/heads/pallas_call | solution.py:155
  10.1 0.0 copy-start.4
  10.1 8.1 %all-to-all-start = ((f32[16,32,128]{2,1,0:T(8,128)}), f32[16,32,128]{2,1,0:T(8,128)S(1)}, u32[]{:S(2)}, u32[]{:S(2)}) async-start(f32[16,32,128]{2,1,0:T(8,128)} %heads.1), calls=%async_computation | async-start | bytes 524288 | tf_op jit(solution)/shard_map/all_to_all | solution.py:20
  18.2 0.0 copy-done.1
  18.2 2.0 %collective-permute-start = (bf16[4096,128]{1,0:T(8,128)(2,1)S(1)}, bf16[4096,128]{1,0:T(8,128)(2,1)}, u32[]{:S(2)}, u32[]{:S(2)}) collective-permute-start(bf16[4096,128]{1,0:T(8,128)(2,1)S(1)} %copy-done.1), channel_id=1, source_target_pairs={{0,32},{32,0},{1,33},{33,1},{2,34},{34,2},{3,35},{35,3},{4,36},{36... | collective-permute-start | bytes 3145736 | tf_op jit(solution)/shard_map/ppermute | solution.py:301
  20.2 4.5 %collective-permute-done.1.refs_2_ = bf16[4096,128]{1,0:T(8,128)(2,1)S(1)} collective-permute-done((bf16[4096,128]{1,0:T(8,128)(2,1)}, bf16[4096,128]{1,0:T(8,128)(2,1)S(1)}, u32[]{:S(2)}, u32[]{:S(2)}) %collective-permute-start.1) | collective-permute-done | bytes 1048608 | tf_op jit(solution)/shard_map/ppermute | solution.py:300
  24.8 0.0 copy-start.2
  24.8 7.1 %collective-permute-start.2 = (bf16[4096,128]{1,0:T(8,128)(2,1)S(1)}, bf16[4096,128]{1,0:T(8,128)(2,1)}, u32[]{:S(2)}, u32[]{:S(2)}) collective-permute-start(bf16[4096,128]{1,0:T(8,128)(2,1)S(1)} %collective-permute-done.1.refs_2_), channel_id=1, source_target_pairs={{0,32},{32,0},{1,33},{33,1},{2,34},{34,2},{3,35},{35,3},{4,36},{36... | collective-permute-start | bytes 3145736 | tf_op jit(solution)/shard_map/ppermute | solution.py:302
  31.8 0.0 all-to-all-done.arrived_ref
  31.8 0.0 copy-start.3
  31.9 0.7 copy-done.3
  32.6 1.8 %norm.1 = (bf16[16,16,128]{2,1,0:T(8,128)(2,1)}, f32[1,128]{1,0:T(1,128)}) custom-call(s32[1]{0:T(128)} %bitcast.4.half_ref, f32[16,32,128]{2,1,0:T(8,128)} %copy-done.3, f32[32,128]{1,0:T(8,128)} %bitcast.57, f32[32,128]{1,0:T(8,128)} %bitcast.58), custom_call_target="tpu_custom_call" | custom-call | flops 4000000 | bytes 400000 | tf_op jit(solution)/shard_map/norm/pallas_call | solution.py:186
  34.3 20.9 %all_to_all.25 = bf16[16,16,128]{2,1,0:T(8,128)(2,1)S(1)} all-to-all(bf16[16,16,128]{2,1,0:T(8,128)(2,1)} %get-tuple-element.4), channel_id=1, replica_groups=mesh['heads_0'=8,'heads_1'=2,'z_pair'=4,'z_side'=2,'x'=4] {'z_pair','x'}, dimensions={0} | all-to-all | bytes 131072 | tf_op jit(solution)/shard_map/all_to_all | solution.py:20
  55.3 0.8 broadcast_in_dim.7
  56.1 6.8 %all-to-all-start.2 = ((bf16[8,16,2048]{2,1,0:T(8,128)(2,1)}), bf16[8,16,2048]{2,1,0:T(8,128)(2,1)S(1)}, u32[]{:S(2)}, u32[]{:S(2)}) async-start(bf16[8,16,2048]{2,1,0:T(8,128)(2,1)} %broadcast_in_dim.7), calls=%async_computation.2 | async-start | bytes 1048576 | tf_op jit(solution)/shard_map/all_to_all | solution.py:20
  62.9 0.0 copy-done.4
  62.9 0.1 reshape.58
  63.1 0.1 copy.54
  63.1 0.7 reshape.64.ids_ref
  63.8 0.6 add_multiply_fusion.firsts_ref
  64.4 0.0 copy-start.5
  64.4 0.0 collective-permute-done.refs_1_
  64.4 14.5 %all-to-all-done.2.rows_ref = bf16[8,16,2048]{2,1,0:T(8,128)(2,1)S(1)} async-done(((bf16[8,16,2048]{2,1,0:T(8,128)(2,1)}), bf16[8,16,2048]{2,1,0:T(8,128)(2,1)S(1)}, u32[]{:S(2)}, u32[]{:S(2)}) %all-to-all-start.2) | async-done | bytes 524320 | tf_op jit(solution)/shard_map/all_to_all | solution.py:20
  78.9 0.0 copy-start
  78.9 0.0 collective-permute-done.2.refs_3_
  78.9 0.0 copy-done.2
  78.9 0.8 copy-done
  79.7 4.8 %logits.1 = f32[16,1,128]{2,1,0:T(1,128)} custom-call(s32[4]{0:T(128)} %add_multiply_fusion.firsts_ref, bf16[8,16,2048]{2,1,0:T(8,128)(2,1)} %copy-done, s32[64,1]{1,0:T(8,128)} %reshape.64.ids_ref, bf16[4096,128]{1,0:T(8,128)(2,1)} %refs_0_.3, bf16[4096,128]{1,0:T(8,128)(2,1)} %collective-permute-done.refs_1_, bf16[4096,128]{1,0:T(8,128)(2,1)} %copy-done.2, ...), custom_call_target="tpu_custom_call" | custom-call | flops 270000000 | bytes 4700000 | tf_op jit(solution)/shard_map/logits/pallas_call | solution.py:252
  84.5 12.5 %all_to_all.26 = f32[16,1,128]{2,1,0:T(1,128)S(1)} all-to-all(f32[16,1,128]{2,1,0:T(1,128)} %logits.1), channel_id=1, replica_groups=mesh['heads_0'=8,'heads_1'=2,'z_pair'=4,'z_side'=2,'x'=4] {'z_pair','x'}, dimensions={0} | all-to-all | bytes 16384 | tf_op jit(solution)/shard_map/all_to_all | solution.py:20
  97.0 0.1 copy.46
  97.1 0.1 slice_reduce_fusion.2
  97.2 0.2 fusion.4
  97.4 0.0 copy-done.5
  97.4 0.1 pad_maximum_fusion
  97.6 12.7 %all_to_all.27 = f32[16,1,13]{2,1,0:T(1,128)S(1)} all-to-all(f32[16,1,13]{2,1,0:T(1,128)S(1)} %broadcast_in_dim.16), channel_id=1, replica_groups=mesh['heads_0'=8,'heads_1'=2,'z_pair'=4,'z_side'=2,'x'=4] {'heads_0','he..., dimensions={0} | all-to-all | bytes 1664 | tf_op jit(solution)/shard_map/all_to_all | solution.py:20
  110.2 0.1 slice.39
  110.3 0.1 copy.53
  110.4 0.6 reshape.63
  111.0 0.1 copy.47
  111.1 0.1 fusion.6
  111.2 0.1 copy.50
  111.3 0.2 fusion.2
  111.5 0.1 copy.51
  111.6 0.1 copy.52
  111.7 0.6 sub.36
  (5 shorter events, 0.1 us)
Async XLA Ops:
  0.6 17.5 %copy-start.1 = (bf16[4096,128]{1,0:T(8,128)(2,1)S(1)}, bf16[4096,128]{1,0:T(8,128)(2,1)}, u32[]{:S(2)}) copy-start(bf16[4096,128]{1,0:T(8,128)(2,1)} %refs_0_.3) | copy-start | bytes 3145732
  0.6 24.1 %collective-permute-start.1 = (bf16[4096,128]{1,0:T(8,128)(2,1)}, bf16[4096,128]{1,0:T(8,128)(2,1)S(1)}, u32[]{:S(2)}, u32[]{:S(2)}) collective-permute-start(bf16[4096,128]{1,0:T(8,128)(2,1)} %refs_0_.3), channel_id=1, source_target_pairs={{0,4},{4,0},{1,5},{5,1},{2,6},{6,2},{3,7},{7,3},{8,12},{12,8},{9,1... | collective-permute-start | bytes 3145736 | tf_op jit(solution)/shard_map/ppermute | solution.py:300
  10.1 52.8 %copy-start.4 = (s32[256]{0:T(256)S(1)}, s32[256]{0:T(256)}, u32[]{:S(2)}) copy-start(s32[256]{0:T(256)} %param.29) | copy-start | bytes 3076
  10.1 21.7 %all-to-all-start = ((f32[16,32,128]{2,1,0:T(8,128)}), f32[16,32,128]{2,1,0:T(8,128)S(1)}, u32[]{:S(2)}, u32[]{:S(2)}) async-start(f32[16,32,128]{2,1,0:T(8,128)} %heads.1), calls=%async_computation | async-start | bytes 524288 | tf_op jit(solution)/shard_map/all_to_all | solution.py:20
  18.2 46.3 %collective-permute-start = (bf16[4096,128]{1,0:T(8,128)(2,1)S(1)}, bf16[4096,128]{1,0:T(8,128)(2,1)}, u32[]{:S(2)}, u32[]{:S(2)}) collective-permute-start(bf16[4096,128]{1,0:T(8,128)(2,1)S(1)} %copy-done.1), channel_id=1, source_target_pairs={{0,32},{32,0},{1,33},{33,1},{2,34},{34,2},{3,35},{35,3},{4,36},{36... | collective-permute-start | bytes 3145736 | tf_op jit(solution)/shard_map/ppermute | solution.py:301
  24.8 54.2 %copy-start.2 = (bf16[4096,128]{1,0:T(8,128)(2,1)}, bf16[4096,128]{1,0:T(8,128)(2,1)S(1)}, u32[]{:S(2)}) copy-start(bf16[4096,128]{1,0:T(8,128)(2,1)S(1)} %collective-permute-done.1.refs_2_) | copy-start | bytes 3145732
  24.8 54.2 %collective-permute-start.2 = (bf16[4096,128]{1,0:T(8,128)(2,1)S(1)}, bf16[4096,128]{1,0:T(8,128)(2,1)}, u32[]{:S(2)}, u32[]{:S(2)}) collective-permute-start(bf16[4096,128]{1,0:T(8,128)(2,1)S(1)} %collective-permute-done.1.refs_2_), channel_id=1, source_target_pairs={{0,32},{32,0},{1,33},{33,1},{2,34},{34,2},{3,35},{35,3},{4,36},{36... | collective-permute-start | bytes 3145736 | tf_op jit(solution)/shard_map/ppermute | solution.py:302
  31.8 0.7 copy-start.3
  56.1 22.8 %all-to-all-start.2 = ((bf16[8,16,2048]{2,1,0:T(8,128)(2,1)}), bf16[8,16,2048]{2,1,0:T(8,128)(2,1)S(1)}, u32[]{:S(2)}, u32[]{:S(2)}) async-start(bf16[8,16,2048]{2,1,0:T(8,128)(2,1)} %broadcast_in_dim.7), calls=%async_computation.2 | async-start | bytes 1048576 | tf_op jit(solution)/shard_map/all_to_all | solution.py:20
  64.4 33.0 %copy-start.5 = (f32[1,128]{1,0:T(1,128)S(1)}, f32[1,128]{1,0:T(1,128)}, u32[]{:S(2)}) copy-start(f32[1,128]{1,0:T(1,128)} %get-tuple-element.5) | copy-start | bytes 1540
  78.9 0.8 copy-start

commit v4 on v3

--- a/solution.py
+++ b/solution.py
@@ -1,3 +1,5 @@
+import functools
+
 import jax
 import jax.numpy as jnp
 from jax import lax
@@ -6,6 +8,7 @@
 from jax.sharding import Mesh
 from jax.sharding import PartitionSpec as P
 
+
 HEADS = ("heads_0", "heads_1")
 BATCH = ("z_pair", "z_side", "x")
 GROUP = ("z_pair", "x")
@@ -18,11 +21,6 @@
 
 def exchange(parts, axis):
     return lax.all_to_all(parts, axis, split_axis=0, concat_axis=0, tiled=True)
-
-
-def copy_for_each(array, axis):
-    size = lax.axis_size(axis)
-    return exchange(jnp.broadcast_to(array[None], (size, *array.shape)), axis)
 
 
 def any_spec():
@@ -154,7 +152,7 @@
     width = out_proj.shape[1]
     return pl.pallas_call(
         heads_kernel,
-        out_shape=jax.ShapeDtypeStruct((places, width // 128, 128), jnp.float32),
+        out_shape=pltpu.VMEM((places, width // 128, 128), jnp.float32),
         in_specs=[smem_spec(), smem_spec()] + [any_spec() for _ in arrays],
         out_specs=vmem_spec(),
         scratch_shapes=[pltpu.VMEM(a.shape, a.dtype) for a in arrays]
@@ -186,8 +184,8 @@
     return pl.pallas_call(
         norm_kernel,
         out_shape=(
-            jax.ShapeDtypeStruct((copies, lines, 128), jnp.bfloat16),
-            jax.ShapeDtypeStruct((1, 128), jnp.float32),
+            pltpu.VMEM((copies, lines, 128), jnp.bfloat16),
+            pltpu.VMEM((1, 128), jnp.float32),
         ),
         in_specs=[smem_spec(), vmem_spec(), vmem_spec(), vmem_spec()],
         out_specs=(vmem_spec(), vmem_spec()),
@@ -251,7 +249,7 @@
     depth = matrices[0].shape[0]
     return pl.pallas_call(
         logits_kernel,
-        out_shape=jax.ShapeDtypeStruct((groups, 1, 128), jnp.float32),
+        out_shape=pltpu.VMEM((groups, 1, 128), jnp.float32),
         in_specs=[smem_spec(), vmem_spec(), vmem_spec()] + [any_spec() for _ in matrices],
         out_specs=vmem_spec(),
         scratch_shapes=[
@@ -263,10 +261,90 @@
     )(firsts, all_rows, ids, *matrices)
 
 
-def merged(top, total, chosen, axis):
-    highest = jnp.max(top, axis=axis, keepdims=True)
-    scaled = jnp.sum(total * jnp.exp(top - highest), axis=axis)
-    return jnp.squeeze(highest, axis), scaled, jnp.sum(chosen, axis=axis)
+def spread_kernel(groups_ref, out_ref):
+    flat = groups_ref[...].astype(jnp.float32)
+    flat = flat.reshape(out_ref.shape[1:]).astype(jnp.bfloat16)
+    for n in range(out_ref.shape[0]):
+        out_ref[n] = flat
+
+
+def spread(pieces, copies):
+    groups, lines, lanes = pieces.shape
+    return pl.pallas_call(
+        spread_kernel,
+        out_shape=pltpu.VMEM((copies, groups, lines * lanes), jnp.bfloat16),
+        in_specs=[vmem_spec()],
+        out_specs=vmem_spec(),
+        cost_estimate=pl.CostEstimate(flops=1000000, bytes_accessed=600000, transcendentals=0),
+        name="spread",
+    )(pieces)
+
+
+def shifted(lines, places):
+    return pltpu.roll(lines, places % 128, 1)
+
+
+def merged(lines, keep, owned):
+    low = jnp.min(lines, axis=0, keepdims=True)
+    top = jnp.max(jnp.where(keep, lines, low), axis=0, keepdims=True)
+    weight = jnp.where(keep, jnp.exp(jnp.minimum(lines - top, 0.0)), 0.0)
+    total = jnp.sum(shifted(lines, -owned) * weight, axis=0, keepdims=True)
+    chosen = jnp.sum(jnp.where(keep, lines, 0.0), axis=0, keepdims=True)
+    return top, total, chosen
+
+
+def group_kernel(owned, stats_ref, value_ref, out_ref):
+    lines = stats_ref[...].reshape(stats_ref.shape[0], 128)
+    top, total, chosen = merged(lines, jnp.full(lines.shape, True), owned)
+    lane = lax.broadcasted_iota(jnp.int32, (1, 128), 1)
+    packed = jnp.where(lane < owned, top, shifted(total, owned))
+    packed = jnp.where(lane < 2 * owned, packed, chosen)
+    packed = jnp.where(lane < 3 * owned, packed, value_ref[...])
+    for n in range(out_ref.shape[0]):
+        out_ref[n] = packed
+
+
+def group_stats(stats, value, owned, copies):
+    return pl.pallas_call(
+        functools.partial(group_kernel, owned),
+        out_shape=pltpu.VMEM((copies, 1, 128), jnp.float32),
+        in_specs=[vmem_spec(), vmem_spec()],
+        out_specs=vmem_spec(),
+        name="group",
+    )(stats, value)
+
+
+def final_kernel(owned, cores, stats_ref, logprob_ref, value_ref):
+    count = stats_ref.shape[0]
+    lines = stats_ref[...].reshape(count, 128)
+    place = lax.broadcasted_iota(jnp.int32, lines.shape, 0)
+    lane = lax.broadcasted_iota(jnp.int32, lines.shape, 1)
+    row = lax.broadcasted_iota(jnp.int32, (1, 128), 1)
+    logprob = jnp.zeros((1, 128), jnp.float32)
+    for core in range(cores):
+        top, total, chosen = merged(lines, place % cores == core, owned)
+        total = jnp.where(row < owned, total, 1.0)
+        found = shifted(chosen, -2 * owned) - (top + jnp.log(total))
+        logprob = jnp.where(row // owned == core, shifted(found, core * owned), logprob)
+    values = jnp.broadcast_to(lines[:, 3 * owned : 3 * owned + 1], lines.shape)
+    here = place == (lane % owned) * (count // owned) + lane // owned
+    value = jnp.sum(jnp.where(here, values, 0.0), axis=0, keepdims=True)
+    logprob_ref[...] = logprob[:, : logprob_ref.shape[1]]
+    value_ref[...] = value[:, : value_ref.shape[1]]
+
+
+def final_values(stats, owned, cores):
+    rows = owned * cores
+    return pl.pallas_call(
+        functools.partial(final_kernel, owned, cores),
+        out_shape=(
+            jax.ShapeDtypeStruct((1, rows), jnp.float32),
+            jax.ShapeDtypeStruct((1, rows), jnp.float32),
+        ),
+        in_specs=[vmem_spec()],
+        out_specs=(vmem_spec(), vmem_spec()),
+        name="final",
+    )(stats)
 
 
 def per_device(
@@ -295,7 +373,6 @@
     copies = chips // rows_core
     lanes = 128
     lines = width // lanes
-    half = width // copies
 
     z_head = lax.ppermute(lm_head, "z_side", SWAP)
     core_head = lax.ppermute(lm_head, "heads_1", SWAP)
@@ -322,8 +399,8 @@
     weight = value_weight.reshape(lines, lanes)
     half_here = (chip % copies).astype(jnp.int32).reshape(1)
     pieces, value = norm_pieces(arrived, gain, weight, half_here, groups, lines // copies)
-    all_groups = exchange(pieces, GROUP).reshape(groups, half)
-    all_rows = copy_for_each(all_groups, "heads_0")
+    for_chips = spread(exchange(pieces, GROUP), chips)
+    all_rows = exchange(for_chips, "heads_0")
 
     vocab_own = lm_head.shape[1]
     flat = lax.axis_index(HEADS_BATCH)
@@ -336,15 +413,9 @@
     ids = lax.dynamic_index_in_dim(ids, core, 2, keepdims=False)
     ids = ids.reshape(groups, rows_core).T.reshape(-1, 1)
     stats = logit_stats(all_rows, matrices, firsts.astype(jnp.int32), ids)
-    stats = exchange(stats, GROUP)[:, 0, : 3 * rows_core].reshape(groups, 3, rows_core)
-    stats = merged(stats[:, 0], stats[:, 1], stats[:, 2], 0)
-    packed = jnp.concatenate([*stats, value[0, :1]])
-    packed = copy_for_each(packed[None], HEADS).reshape(chips, cores, -1)
-    found = packed[..., : 3 * rows_core].reshape(chips, cores, 3, rows_core)
-    top, total, chosen = merged(found[:, :, 0], found[:, :, 1], found[:, :, 2], 0)
-    logprob = (chosen - (top + jnp.log(total))).reshape(-1)
-    values = packed[::copies, :, 3 * rows_core].T.reshape(-1)
-    return (logprob, values)
+    stats = group_stats(exchange(stats, GROUP), value, rows_core, chips * cores)
+    logprob, values = final_values(exchange(stats, HEADS), rows_core, cores)
+    return (logprob.reshape(-1), values.reshape(-1))
 
 
 def solution(mesh):

time: 113 us -> 113 us (level)
  Pallas kernels: 11 us -> 13.7 us
  local copies, waits for them, and re-layouts: 5.13 us -> 2.96 us
    pallas_call x3 -> x6, Pallas kernels: 11 us -> 13.7 us  [the longest x1 4.43 us: head_partials(): pl.pallas_call(heads_kernel, out_shape=pltpu.VMEM((places, width // 128,...]
  transfers between devices with their start and end apart: 5 -> 5, of which waited for: 2 -> 2; matrix products, arithmetic and copies ran while one was open for 2% -> 1% of each run, Pallas kernels for 6% -> 6%
where the time goes in v4:
time: 113 us; the launch traced here: 112 us
  blocking collectives  46.4 us (41%)
  starting transfers between devices  28.9 us (26%)
  waiting for transfers between devices  19 us (17%)
  Pallas kernels  13.7 us (12%)
  local copies, waits for them, and re-layouts  2.96 us (3%)
    all_to_all x3, blocking collectives, exchange(): return lax.all_to_all(parts, axis, split_axis=0, concat_axis=0, tiled=True)  46.4 us
    all_to_all x2, starting transfers between devices, exchange(): return lax.all_to_all(parts, axis, split_axis=0, concat_axis=0, tiled=True)  14.9 us
    all_to_all x2, waiting for transfers between devices, exchange(): return lax.all_to_all(parts, axis, split_axis=0, concat_axis=0, tiled=True)  14.5 us
    ppermute x1, starting transfers between devices, per_device(): both_head = lax.ppermute(z_head, 'heads_1', SWAP)  7.06 us
    ppermute x1, starting transfers between devices, per_device(): z_head = lax.ppermute(lm_head, 'z_side', SWAP)  4.95 us
    ppermute x1, waiting for transfers between devices, per_device(): z_head = lax.ppermute(lm_head, 'z_side', SWAP)  4.57 us
    pallas_call x1, Pallas kernels, head_partials(): pl.pallas_call(heads_kernel, out_shape=pltpu.VMEM((places, width // 128,...  4.43 us
    pallas_call x1, Pallas kernels, logit_stats(): pl.pallas_call(logits_kernel, out_shape=pltpu.VMEM((groups, 1, 128), jnp....  4.18 us
  transfers between devices with their start and end apart: 5, of which 2 were waited for; matrix products, arithmetic and copies ran while one was open for 1% of the time, Pallas kernels for 6%

profile of v4, /device:TPU:1, one launch (start us, length us, event | category | flops | bytes accessed | tf_op | source)
XLA Modules:
  0.0 112.4 jit_solution(15286183922303192501)
XLA Ops:
  0.6 0.0 copy-start.2
  0.6 5.0 %collective-permute-start.1 = (bf16[4096,128]{1,0:T(8,128)(2,1)}, bf16[4096,128]{1,0:T(8,128)(2,1)S(1)}, u32[]{:S(2)}, u32[]{:S(2)}) collective-permute-start(bf16[4096,128]{1,0:T(8,128)(2,1)} %refs_0_.3), channel_id=1, source_target_pairs={{0,4},{4,0},{1,5},{5,1},{2,6},{6,2},{3,7},{7,3},{8,12},{12,8},{9,1... | collective-permute-start | bytes 3145736 | tf_op jit(solution)/shard_map/ppermute | solution.py:377
  5.6 4.4 %heads.1 = f32[16,32,128]{2,1,0:T(8,128)} custom-call(f32[1]{0:T(128)} %bitcast.5.first_ref, f32[2]{0:T(128)} %rate_ref.1, bf16[8,256]{1,0:T(8,128)(2,1)} %refs_0_.2, bf16[8,256]{1,0:T(8,128)(2,1)} %refs_1_.1, bf16[8,256]{1,0:T(8,128)(2,1)} %refs_2_.1, bf16[8,256]{1,0:T(8,128)(2,1)} %refs_3_.1, f32[2,8]{1,0:T(2,128)} %bitcast.19, f32[2,8]{1,0:T(2,128)} %bitcast.20, ...), custom_call_target="tpu_custom_call" | custom-call | flops 40000000 | bytes 3500000 | tf_op jit(solution)/shard_map/heads/pallas_call | solution.py:153
  10.1 0.0 copy-start.5
  10.1 8.1 %all-to-all-start = ((f32[16,32,128]{2,1,0:T(8,128)}), f32[16,32,128]{2,1,0:T(8,128)S(1)}, u32[]{:S(2)}, u32[]{:S(2)}) async-start(f32[16,32,128]{2,1,0:T(8,128)} %heads.1), calls=%async_computation | async-start | bytes 524288 | tf_op jit(solution)/shard_map/all_to_all | solution.py:23
  18.2 0.0 copy-done.2
  18.2 2.0 %collective-permute-start = (bf16[4096,128]{1,0:T(8,128)(2,1)S(1)}, bf16[4096,128]{1,0:T(8,128)(2,1)}, u32[]{:S(2)}, u32[]{:S(2)}) collective-permute-start(bf16[4096,128]{1,0:T(8,128)(2,1)S(1)} %copy-done.2), channel_id=1, source_target_pairs={{0,32},{32,0},{1,33},{33,1},{2,34},{34,2},{3,35},{35,3},{4,36},{36... | collective-permute-start | bytes 3145736 | tf_op jit(solution)/shard_map/ppermute | solution.py:378
  20.2 4.6 %collective-permute-done.1.refs_2_ = bf16[4096,128]{1,0:T(8,128)(2,1)S(1)} collective-permute-done((bf16[4096,128]{1,0:T(8,128)(2,1)}, bf16[4096,128]{1,0:T(8,128)(2,1)S(1)}, u32[]{:S(2)}, u32[]{:S(2)}) %collective-permute-start.1) | collective-permute-done | bytes 1048608 | tf_op jit(solution)/shard_map/ppermute | solution.py:377
  24.8 0.0 copy-start.3
  24.8 7.1 %collective-permute-start.2 = (bf16[4096,128]{1,0:T(8,128)(2,1)S(1)}, bf16[4096,128]{1,0:T(8,128)(2,1)}, u32[]{:S(2)}, u32[]{:S(2)}) collective-permute-start(bf16[4096,128]{1,0:T(8,128)(2,1)S(1)} %collective-permute-done.1.refs_2_), channel_id=1, source_target_pairs={{0,32},{32,0},{1,33},{33,1},{2,34},{34,2},{3,35},{35,3},{4,36},{36... | collective-permute-start | bytes 3145736 | tf_op jit(solution)/shard_map/ppermute | solution.py:379
  31.8 0.0 all-to-all-done.arrived_ref
  31.8 0.0 copy-start.4
  31.9 0.7 copy-done.4
  32.5 1.1 %norm.1 = (bf16[16,16,128]{2,1,0:T(8,128)(2,1)S(1)}, f32[1,128]{1,0:T(1,128)S(1)}) custom-call(s32[1]{0:T(128)} %bitcast.4.half_ref, f32[16,32,128]{2,1,0:T(8,128)} %copy-done.4, f32[32,128]{1,0:T(8,128)} %bitcast.16, f32[32,128]{1,0:T(8,128)} %bitcast.17), custom_call_target="tpu_custom_call" | custom-call | flops 4000000 | bytes 400000 | tf_op jit(solution)/shard_map/norm/pallas_call | solution.py:184
  33.7 0.0 copy-start
  33.7 0.5 copy-done
  34.2 20.8 %all_to_all.25.groups_ref = bf16[16,16,128]{2,1,0:T(8,128)(2,1)} all-to-all(bf16[16,16,128]{2,1,0:T(8,128)(2,1)S(1)} %get-tuple-element.6), channel_id=1, replica_groups=mesh['heads_0'=8,'heads_1'=2,'z_pair'=4,'z_side'=2,'x'=4] {'z_pair','x'}, dimensions={0} | all-to-all | bytes 131072 | tf_op jit(solution)/shard_map/all_to_all | solution.py:23
  55.0 1.7 %spread.1 = bf16[8,16,2048]{2,1,0:T(8,128)(2,1)} custom-call(bf16[16,16,128]{2,1,0:T(8,128)(2,1)} %all_to_all.25.groups_ref), custom_call_target="tpu_custom_call" | custom-call | flops 1000000 | bytes 600000 | tf_op jit(solution)/shard_map/spread/pallas_call | solution.py:273
  56.7 6.8 %all-to-all-start.2 = ((bf16[8,16,2048]{2,1,0:T(8,128)(2,1)}), bf16[8,16,2048]{2,1,0:T(8,128)(2,1)S(1)}, u32[]{:S(2)}, u32[]{:S(2)}) async-start(bf16[8,16,2048]{2,1,0:T(8,128)(2,1)} %spread.1), calls=%async_computation.2 | async-start | bytes 1048576 | tf_op jit(solution)/shard_map/all_to_all | solution.py:23
  63.5 0.0 copy-done.5
  63.5 0.1 reshape.42
  63.7 0.1 copy.20
  63.8 0.7 reshape.47.ids_ref
  64.5 0.6 add_multiply_fusion.firsts_ref
  65.1 0.0 collective-permute-done.refs_1_
  65.1 14.5 %all-to-all-done.2.rows_ref = bf16[8,16,2048]{2,1,0:T(8,128)(2,1)S(1)} async-done(((bf16[8,16,2048]{2,1,0:T(8,128)(2,1)}), bf16[8,16,2048]{2,1,0:T(8,128)(2,1)S(1)}, u32[]{:S(2)}, u32[]{:S(2)}) %all-to-all-start.2) | async-done | bytes 524320 | tf_op jit(solution)/shard_map/all_to_all | solution.py:23
  79.6 0.0 copy-start.1
  79.6 0.0 collective-permute-done.2.refs_3_
  79.6 0.0 copy-done.3
  79.6 0.8 copy-done.1
  80.4 4.2 %logits.1 = f32[16,1,128]{2,1,0:T(1,128)S(1)} custom-call(s32[4]{0:T(128)} %add_multiply_fusion.firsts_ref, bf16[8,16,2048]{2,1,0:T(8,128)(2,1)} %copy-done.1, s32[64,1]{1,0:T(8,128)} %reshape.47.ids_ref, bf16[4096,128]{1,0:T(8,128)(2,1)} %refs_0_.3, bf16[4096,128]{1,0:T(8,128)(2,1)} %collective-permute-done.refs_1_, bf16[4096,128]{1,0:T(8,128)(2,1)} %copy-done.3, ...), custom_call_target="tpu_custom_call" | custom-call | flops 270000000 | bytes 4700000 | tf_op jit(solution)/shard_map/logits/pallas_call | solution.py:250
  84.5 12.2 %all_to_all.26.stats_ref = f32[16,1,128]{2,1,0:T(1,128)} all-to-all(f32[16,1,128]{2,1,0:T(1,128)S(1)} %logits.1), channel_id=1, replica_groups=mesh['heads_0'=8,'heads_1'=2,'z_pair'=4,'z_side'=2,'x'=4] {'z_pair','x'}, dimensions={0} | all-to-all | bytes 16384 | tf_op jit(solution)/shard_map/all_to_all | solution.py:23
  96.8 0.9 group.1
  97.6 13.3 %all_to_all.27.stats_ref = f32[16,1,128]{2,1,0:T(1,128)} all-to-all(f32[16,1,128]{2,1,0:T(1,128)S(1)} %group.1), channel_id=1, replica_groups=mesh['heads_0'=8,'heads_1'=2,'z_pair'=4,'z_side'=2,'x'=4] {'heads_0','he..., dimensions={0} | all-to-all | bytes 16384 | tf_op jit(solution)/shard_map/all_to_all | solution.py:23
  111.0 1.4 %final.1 = (f32[1,8]{1,0:T(1,128)}, f32[1,8]{1,0:T(1,128)}) custom-call(f32[16,1,128]{2,1,0:T(1,128)} %all_to_all.27.stats_ref), custom_call_target="tpu_custom_call" | custom-call | tf_op jit(solution)/shard_map/final/pallas_call | solution.py:338
  (1 shorter events, 0.0 us)
Async XLA Ops:
  0.6 17.5 %copy-start.2 = (bf16[4096,128]{1,0:T(8,128)(2,1)S(1)}, bf16[4096,128]{1,0:T(8,128)(2,1)}, u32[]{:S(2)}) copy-start(bf16[4096,128]{1,0:T(8,128)(2,1)} %refs_0_.3) | copy-start | bytes 3145732
  0.6 24.1 %collective-permute-start.1 = (bf16[4096,128]{1,0:T(8,128)(2,1)}, bf16[4096,128]{1,0:T(8,128)(2,1)S(1)}, u32[]{:S(2)}, u32[]{:S(2)}) collective-permute-start(bf16[4096,128]{1,0:T(8,128)(2,1)} %refs_0_.3), channel_id=1, source_target_pairs={{0,4},{4,0},{1,5},{5,1},{2,6},{6,2},{3,7},{7,3},{8,12},{12,8},{9,1... | collective-permute-start | bytes 3145736 | tf_op jit(solution)/shard_map/ppermute | solution.py:377
  10.1 53.5 %copy-start.5 = (s32[256]{0:T(256)S(1)}, s32[256]{0:T(256)}, u32[]{:S(2)}) copy-start(s32[256]{0:T(256)} %param.29) | copy-start | bytes 3076
  10.1 21.8 %all-to-all-start = ((f32[16,32,128]{2,1,0:T(8,128)}), f32[16,32,128]{2,1,0:T(8,128)S(1)}, u32[]{:S(2)}, u32[]{:S(2)}) async-start(f32[16,32,128]{2,1,0:T(8,128)} %heads.1), calls=%async_computation | async-start | bytes 524288 | tf_op jit(solution)/shard_map/all_to_all | solution.py:23
  18.2 46.9 %collective-permute-start = (bf16[4096,128]{1,0:T(8,128)(2,1)S(1)}, bf16[4096,128]{1,0:T(8,128)(2,1)}, u32[]{:S(2)}, u32[]{:S(2)}) collective-permute-start(bf16[4096,128]{1,0:T(8,128)(2,1)S(1)} %copy-done.2), channel_id=1, source_target_pairs={{0,32},{32,0},{1,33},{33,1},{2,34},{34,2},{3,35},{35,3},{4,36},{36... | collective-permute-start | bytes 3145736 | tf_op jit(solution)/shard_map/ppermute | solution.py:378
  24.8 54.8 %copy-start.3 = (bf16[4096,128]{1,0:T(8,128)(2,1)}, bf16[4096,128]{1,0:T(8,128)(2,1)S(1)}, u32[]{:S(2)}) copy-start(bf16[4096,128]{1,0:T(8,128)(2,1)S(1)} %collective-permute-done.1.refs_2_) | copy-start | bytes 3145732
  24.8 54.8 %collective-permute-start.2 = (bf16[4096,128]{1,0:T(8,128)(2,1)S(1)}, bf16[4096,128]{1,0:T(8,128)(2,1)}, u32[]{:S(2)}, u32[]{:S(2)}) collective-permute-start(bf16[4096,128]{1,0:T(8,128)(2,1)S(1)} %collective-permute-done.1.refs_2_), channel_id=1, source_target_pairs={{0,32},{32,0},{1,33},{33,1},{2,34},{34,2},{3,35},{35,3},{4,36},{36... | collective-permute-start | bytes 3145736 | tf_op jit(solution)/shard_map/ppermute | solution.py:379
  31.8 0.7 copy-start.4
  33.7 0.5 copy-start
  56.7 22.8 %all-to-all-start.2 = ((bf16[8,16,2048]{2,1,0:T(8,128)(2,1)}), bf16[8,16,2048]{2,1,0:T(8,128)(2,1)S(1)}, u32[]{:S(2)}, u32[]{:S(2)}) async-start(bf16[8,16,2048]{2,1,0:T(8,128)(2,1)} %spread.1), calls=%async_computation.2 | async-start | bytes 1048576 | tf_op jit(solution)/shard_map/all_to_all | solution.py:23
  79.6 0.8 copy-start.1

commit v5 on v4

--- a/solution.py
+++ b/solution.py
@@ -12,6 +12,7 @@
 HEADS = ("heads_0", "heads_1")
 BATCH = ("z_pair", "z_side", "x")
 GROUP = ("z_pair", "x")
+GATHER = ("heads_0", "z_pair", "x")
 HEADS_BATCH = ("heads_0", "heads_1", "z_pair", "z_side", "x")
 SWAP = [(0, 1), (1, 0)]
 
@@ -24,7 +25,11 @@
 
 
 def any_spec():
-    return pl.BlockSpec(memory_space=pl.ANY)
+    return pl.BlockSpec(memory_space=pltpu.HBM)
+
+
+def room(mebibytes):
+    return pltpu.CompilerParams(vmem_limit_bytes=mebibytes * 2**20)
 
 
 def vmem_spec():
@@ -191,14 +196,16 @@
         out_specs=(vmem_spec(), vmem_spec()),
         scratch_shapes=[pltpu.VMEM(gain.shape, jnp.float32)],
         cost_estimate=pl.CostEstimate(flops=4000000, bytes_accessed=400000, transcendentals=0),
+        compiler_params=room(4),
         name="norm",
     )(half, arrived, gain, weight)
 
 
 def logits_kernel(firsts_ref, rows_ref, ids_ref, *refs):
     count = 4
-    matrices, out_ref, local, sems = refs[:count], refs[count], refs[count + 1], refs[count + 2]
-    pieces, groups, deep = rows_ref.shape
+    matrices, out_ref, local, flat, sems = refs[:count], *refs[count:]
+    pieces, groups, tiles, lanes = rows_ref.shape
+    deep = tiles * lanes
     halves = local.shape[1] // deep
     copies = []
     for k in range(halves):
@@ -212,10 +219,18 @@
             )
     for copy in copies:
         copy.start()
+    flat[...] = rows_ref[...].reshape(flat.shape).astype(jnp.float32)
+
+    def rows_of(piece):
+        start = piece * groups * tiles
+        return jnp.concatenate(
+            [flat[pl.ds(start + t, groups, stride=tiles), :] for t in range(tiles)], axis=1
+        ).astype(jnp.bfloat16)
+
     sums = [None] * count
     for k in range(halves):
         part = slice(k * deep, (k + 1) * deep)
-        lhs = jnp.concatenate([rows_ref[p] for p in range(k, pieces, halves)], axis=0)
+        lhs = jnp.concatenate([rows_of(p) for p in range(k, pieces, halves)], axis=0)
         for n in range(count):
             copies[k * count + n].wait()
             term = jnp.dot(lhs, local[n, part], preferred_element_type=jnp.float32)
@@ -254,30 +269,13 @@
         out_specs=vmem_spec(),
         scratch_shapes=[
             pltpu.VMEM((len(matrices), depth, 128), jnp.bfloat16),
+            pltpu.VMEM((all_rows.size // 128, 128), jnp.float32),
             pltpu.SemaphoreType.DMA((2 * len(matrices),)),
         ],
         cost_estimate=pl.CostEstimate(flops=270000000, bytes_accessed=4700000, transcendentals=0),
+        compiler_params=room(12),
         name="logits",
     )(firsts, all_rows, ids, *matrices)
-
-
-def spread_kernel(groups_ref, out_ref):
-    flat = groups_ref[...].astype(jnp.float32)
-    flat = flat.reshape(out_ref.shape[1:]).astype(jnp.bfloat16)
-    for n in range(out_ref.shape[0]):
-        out_ref[n] = flat
-
-
-def spread(pieces, copies):
-    groups, lines, lanes = pieces.shape
-    return pl.pallas_call(
-        spread_kernel,
-        out_shape=pltpu.VMEM((copies, groups, lines * lanes), jnp.bfloat16),
-        in_specs=[vmem_spec()],
-        out_specs=vmem_spec(),
-        cost_estimate=pl.CostEstimate(flops=1000000, bytes_accessed=600000, transcendentals=0),
-        name="spread",
-    )(pieces)
 
 
 def shifted(lines, places):
@@ -310,6 +308,7 @@
         out_shape=pltpu.VMEM((copies, 1, 128), jnp.float32),
         in_specs=[vmem_spec(), vmem_spec()],
         out_specs=vmem_spec(),
+        compiler_params=room(2),
         name="group",
     )(stats, value)
 
@@ -343,6 +342,7 @@
         ),
         in_specs=[vmem_spec()],
         out_specs=(vmem_spec(), vmem_spec()),
+        compiler_params=room(2),
         name="final",
     )(stats)
 
@@ -398,9 +398,9 @@
     gain = final_gain.reshape(lines, lanes)
     weight = value_weight.reshape(lines, lanes)
     half_here = (chip % copies).astype(jnp.int32).reshape(1)
-    pieces, value = norm_pieces(arrived, gain, weight, half_here, groups, lines // copies)
-    for_chips = spread(exchange(pieces, GROUP), chips)
-    all_rows = exchange(for_chips, "heads_0")
+    pieces, value = norm_pieces(arrived, gain, weight, half_here, chips * groups, lines // copies)
+    all_rows = exchange(pieces, GATHER)
+    all_rows = all_rows.reshape(chips, groups, lines // copies, lanes)
 
     vocab_own = lm_head.shape[1]
     flat = lax.axis_index(HEADS_BATCH)

time: 113 us -> 103 us (0.912)
  blocking collectives: 46.4 us -> 24.4 us
  starting transfers between devices: 28.9 us -> 41.4 us
  waiting for transfers between devices: 19 us -> 25.6 us
  Pallas kernels: 13.7 us -> 9.85 us
  local copies, waits for them, and re-layouts: 2.96 us -> 0.32 us
    all_to_all x3 -> x2, blocking collectives: 46.4 us -> 24.4 us  [exchange(): return lax.all_to_all(parts, axis, split_axis=0, concat_axis=0, tiled=True)]
    all_to_all x2, starting transfers between devices: 14.9 us -> 27.4 us  [exchange(): return lax.all_to_all(parts, axis, split_axis=0, concat_axis=0, tiled=True)]
    all_to_all x2, waiting for transfers between devices: 14.5 us -> 21.2 us  [exchange(): return lax.all_to_all(parts, axis, split_axis=0, concat_axis=0, tiled=True)]
    unnamed x12 -> x8, local copies, waits for them, and re-layouts: 2.04 us -> 0.02 us
    pallas_call x1 -> x0, Pallas kernels: 1.69 us -> none  [spread(): pl.pallas_call(spread_kernel, out_shape=pltpu.VMEM((copies, groups, lines...]
  transfers between devices with their start and end apart: 5 -> 5, of which waited for: 2 -> 2; matrix products, arithmetic and copies ran while one was open for 1% -> 0% of each run, Pallas kernels for 6% -> 5%
where the time goes in v5:
time: 103 us
  starting transfers between devices  41.4 us (40%)
  waiting for transfers between devices  25.6 us (25%)
  blocking collectives  24.4 us (24%)
  Pallas kernels  9.85 us (10%)
    all_to_all x2, starting transfers between devices, exchange(): return lax.all_to_all(parts, axis, split_axis=0, concat_axis=0, tiled=True)  27.4 us
    all_to_all x2, blocking collectives, exchange(): return lax.all_to_all(parts, axis, split_axis=0, concat_axis=0, tiled=True)  24.4 us
    all_to_all x2, waiting for transfers between devices, exchange(): return lax.all_to_all(parts, axis, split_axis=0, concat_axis=0, tiled=True)  21.2 us
    ppermute x1, starting transfers between devices, per_device(): both_head = lax.ppermute(z_head, 'heads_1', SWAP)  7.06 us
    ppermute x1, starting transfers between devices, per_device(): z_head = lax.ppermute(lm_head, 'z_side', SWAP)  4.95 us
    pallas_call x1, Pallas kernels, head_partials(): pl.pallas_call(heads_kernel, out_shape=pltpu.VMEM((places, width // 128,...  4.55 us
    ppermute x1, waiting for transfers between devices, per_device(): z_head = lax.ppermute(lm_head, 'z_side', SWAP)  4.45 us
    pallas_call x1, Pallas kernels, logit_stats(): pl.pallas_call(logits_kernel, out_shape=pltpu.VMEM((groups, 1, 128), jnp....  3.45 us
  transfers between devices with their start and end apart: 5, of which 2 were waited for; matrix products, arithmetic and copies ran while one was open for 0% of the time, Pallas kernels for 5%

profile of v5, /device:TPU:1, one launch (start us, length us, event | category | flops | bytes accessed | tf_op | source)
XLA Modules:
  0.0 102.6 jit_solution(12916003088746606853)
XLA Ops:
  0.6 0.0 copy-start
  0.6 0.0 copy-start.2
  0.7 0.0 copy-start.1
  0.7 4.9 %collective-permute-start.1 = (bf16[4096,128]{1,0:T(8,128)(2,1)}, bf16[4096,128]{1,0:T(8,128)(2,1)S(1)}, u32[]{:S(2)}, u32[]{:S(2)}) collective-permute-start(bf16[4096,128]{1,0:T(8,128)(2,1)} %refs_0_.3), channel_id=1, source_target_pairs={{0,4},{4,0},{1,5},{5,1},{2,6},{6,2},{3,7},{7,3},{8,12},{12,8},{9,1... | collective-permute-start | bytes 3145736 | tf_op jit(solution)/shard_map/ppermute | solution.py:377
  5.6 0.0 copy-start.3
  5.6 4.6 %heads.1 = f32[16,32,128]{2,1,0:T(8,128)} custom-call(f32[1]{0:T(128)} %bitcast.5.first_ref, f32[2]{0:T(128)} %rate_ref.1, bf16[8,256]{1,0:T(8,128)(2,1)} %refs_0_.2, bf16[8,256]{1,0:T(8,128)(2,1)} %refs_1_.1, bf16[8,256]{1,0:T(8,128)(2,1)} %refs_2_.1, bf16[8,256]{1,0:T(8,128)(2,1)} %refs_3_.1, f32[2,8]{1,0:T(2,128)} %bitcast.21, f32[2,8]{1,0:T(2,128)} %bitcast.22, ...), custom_call_target="tpu_custom_call" | custom-call | flops 40000000 | bytes 3500000 | tf_op jit(solution)/shard_map/heads/pallas_call | solution.py:158
  10.2 8.1 %all-to-all-start = ((f32[16,32,128]{2,1,0:T(8,128)}), f32[16,32,128]{2,1,0:T(8,128)S(1)}, u32[]{:S(2)}, u32[]{:S(2)}) async-start(f32[16,32,128]{2,1,0:T(8,128)} %heads.1), calls=%async_computation | async-start | bytes 524288 | tf_op jit(solution)/shard_map/all_to_all | solution.py:24
  18.3 0.0 copy-done
  18.3 2.0 %collective-permute-start = (bf16[4096,128]{1,0:T(8,128)(2,1)S(1)}, bf16[4096,128]{1,0:T(8,128)(2,1)}, u32[]{:S(2)}, u32[]{:S(2)}) collective-permute-start(bf16[4096,128]{1,0:T(8,128)(2,1)S(1)} %copy-done), channel_id=1, source_target_pairs={{0,32},{32,0},{1,33},{33,1},{2,34},{34,2},{3,35},{35,3},{4,36},{36... | collective-permute-start | bytes 3145736 | tf_op jit(solution)/shard_map/ppermute | solution.py:378
  20.3 4.5 %collective-permute-done.1.refs_2_ = bf16[4096,128]{1,0:T(8,128)(2,1)S(1)} collective-permute-done((bf16[4096,128]{1,0:T(8,128)(2,1)}, bf16[4096,128]{1,0:T(8,128)(2,1)S(1)}, u32[]{:S(2)}, u32[]{:S(2)}) %collective-permute-start.1) | collective-permute-done | bytes 1048608 | tf_op jit(solution)/shard_map/ppermute | solution.py:377
  24.8 7.1 %collective-permute-start.2 = (bf16[4096,128]{1,0:T(8,128)(2,1)S(1)}, bf16[4096,128]{1,0:T(8,128)(2,1)}, u32[]{:S(2)}, u32[]{:S(2)}) collective-permute-start(bf16[4096,128]{1,0:T(8,128)(2,1)S(1)} %collective-permute-done.1.refs_2_), channel_id=1, source_target_pairs={{0,32},{32,0},{1,33},{33,1},{2,34},{34,2},{3,35},{35,3},{4,36},{36... | collective-permute-start | bytes 3145736 | tf_op jit(solution)/shard_map/ppermute | solution.py:379
  31.8 0.0 all-to-all-done.arrived_ref
  31.9 0.0 copy-done.2
  31.9 0.0 copy-done.1
  31.9 1.0 norm.1
  32.9 19.3 %all-to-all-start.1 = ((bf16[128,16,128]{2,1,0:T(8,128)(2,1)}), bf16[128,16,128]{2,1,0:T(8,128)(2,1)S(1)}, u32[]{:S(2)}, u32[]{:S(2)}) async-start(bf16[128,16,128]{2,1,0:T(8,128)(2,1)} %get-tuple-element.6), calls=%async_computation.1 | async-start | bytes 1048576 | tf_op jit(solution)/shard_map/all_to_all | solution.py:24
  52.3 0.0 copy-done.3
  52.3 0.1 reshape.46
  52.4 0.1 copy.20
  52.5 0.1 reshape.51.ids_ref
  52.6 0.1 add_multiply_fusion.firsts_ref
  52.7 0.0 collective-permute-done.refs_1_
  52.7 21.2 %all-to-all-done.1 = bf16[128,16,128]{2,1,0:T(8,128)(2,1)S(1)} async-done(((bf16[128,16,128]{2,1,0:T(8,128)(2,1)}), bf16[128,16,128]{2,1,0:T(8,128)(2,1)S(1)}, u32[]{:S(2)}, u32[]{:S(2)}) %all-to-all-start.1) | async-done | bytes 524320 | tf_op jit(solution)/shard_map/all_to_all | solution.py:24
  73.9 0.0 collective-permute-done.2.refs_3_
  73.9 3.5 %logits.1 = f32[16,1,128]{2,1,0:T(1,128)S(1)} custom-call(s32[4]{0:T(128)S(1)} %add_multiply_fusion.firsts_ref, bf16[8,16,16,128]{3,2,1,0:T(8,128)(2,1)S(1)} %bitcast.16, s32[64,1]{1,0:T(8,128)S(1)} %reshape.51.ids_ref, bf16[4096,128]{1,0:T(8,128)(2,1)S(1)} %copy-done, bf16[4096,128]{1,0:T(8,128)(2,1)} %collective-permute-done.refs_1_, ...), custom_call_target="tpu_custom_call" | custom-call | flops 270000000 | bytes 4700000 | tf_op jit(solution)/shard_map/logits/pallas_call | solution.py:265
  77.3 11.4 %all_to_all.20.stats_ref = f32[16,1,128]{2,1,0:T(1,128)S(1)} all-to-all(f32[16,1,128]{2,1,0:T(1,128)S(1)} %logits.1), channel_id=1, replica_groups=mesh['heads_0'=8,'heads_1'=2,'z_pair'=4,'z_side'=2,'x'=4] {'z_pair','x'}, dimensions={0} | all-to-all | bytes 16384 | tf_op jit(solution)/shard_map/all_to_all | solution.py:24
  88.7 0.2 group.1
  88.9 13.0 %all_to_all.21.stats_ref = f32[16,1,128]{2,1,0:T(1,128)S(1)} all-to-all(f32[16,1,128]{2,1,0:T(1,128)S(1)} %group.1), channel_id=1, replica_groups=mesh['heads_0'=8,'heads_1'=2,'z_pair'=4,'z_side'=2,'x'=4] {'heads_0','he..., dimensions={0} | all-to-all | bytes 16384 | tf_op jit(solution)/shard_map/all_to_all | solution.py:24
  101.9 0.7 final.1
  (1 shorter events, 0.0 us)
Async XLA Ops:
  0.6 17.7 %copy-start = (bf16[4096,128]{1,0:T(8,128)(2,1)S(1)}, bf16[4096,128]{1,0:T(8,128)(2,1)}, u32[]{:S(2)}) copy-start(bf16[4096,128]{1,0:T(8,128)(2,1)} %refs_0_.3) | copy-start | bytes 3145732
  0.6 31.2 %copy-start.2 = (f32[4096]{0:T(1024)S(1)}, f32[4096]{0:T(1024)}, u32[]{:S(2)}) copy-start(f32[4096]{0:T(1024)} %param.27) | copy-start | bytes 49156
  0.7 31.2 %copy-start.1 = (f32[4096]{0:T(1024)S(1)}, f32[4096]{0:T(1024)}, u32[]{:S(2)}) copy-start(f32[4096]{0:T(1024)} %param.26) | copy-start | bytes 49156
  0.7 24.1 %collective-permute-start.1 = (bf16[4096,128]{1,0:T(8,128)(2,1)}, bf16[4096,128]{1,0:T(8,128)(2,1)S(1)}, u32[]{:S(2)}, u32[]{:S(2)}) collective-permute-start(bf16[4096,128]{1,0:T(8,128)(2,1)} %refs_0_.3), channel_id=1, source_target_pairs={{0,4},{4,0},{1,5},{5,1},{2,6},{6,2},{3,7},{7,3},{8,12},{12,8},{9,1... | collective-permute-start | bytes 3145736 | tf_op jit(solution)/shard_map/ppermute | solution.py:377
  5.6 46.6 %copy-start.3 = (s32[256]{0:T(256)S(1)}, s32[256]{0:T(256)}, u32[]{:S(2)}) copy-start(s32[256]{0:T(256)} %param.29) | copy-start | bytes 3076
  10.2 21.6 %all-to-all-start = ((f32[16,32,128]{2,1,0:T(8,128)}), f32[16,32,128]{2,1,0:T(8,128)S(1)}, u32[]{:S(2)}, u32[]{:S(2)}) async-start(f32[16,32,128]{2,1,0:T(8,128)} %heads.1), calls=%async_computation | async-start | bytes 524288 | tf_op jit(solution)/shard_map/all_to_all | solution.py:24
  18.3 34.4 %collective-permute-start = (bf16[4096,128]{1,0:T(8,128)(2,1)S(1)}, bf16[4096,128]{1,0:T(8,128)(2,1)}, u32[]{:S(2)}, u32[]{:S(2)}) collective-permute-start(bf16[4096,128]{1,0:T(8,128)(2,1)S(1)} %copy-done), channel_id=1, source_target_pairs={{0,32},{32,0},{1,33},{33,1},{2,34},{34,2},{3,35},{35,3},{4,36},{36... | collective-permute-start | bytes 3145736 | tf_op jit(solution)/shard_map/ppermute | solution.py:378
  24.8 49.1 %collective-permute-start.2 = (bf16[4096,128]{1,0:T(8,128)(2,1)S(1)}, bf16[4096,128]{1,0:T(8,128)(2,1)}, u32[]{:S(2)}, u32[]{:S(2)}) collective-permute-start(bf16[4096,128]{1,0:T(8,128)(2,1)S(1)} %collective-permute-done.1.refs_2_), channel_id=1, source_target_pairs={{0,32},{32,0},{1,33},{33,1},{2,34},{34,2},{3,35},{35,3},{4,36},{36... | collective-permute-start | bytes 3145736 | tf_op jit(solution)/shard_map/ppermute | solution.py:379
  32.9 41.0 %all-to-all-start.1 = ((bf16[128,16,128]{2,1,0:T(8,128)(2,1)}), bf16[128,16,128]{2,1,0:T(8,128)(2,1)S(1)}, u32[]{:S(2)}, u32[]{:S(2)}) async-start(bf16[128,16,128]{2,1,0:T(8,128)(2,1)} %get-tuple-element.6), calls=%async_computation.1 | async-start | bytes 1048576 | tf_op jit(solution)/shard_map/all_to_all | solution.py:24

commit v6 on v5

--- a/solution.py
+++ b/solution.py
@@ -13,6 +13,7 @@
 BATCH = ("z_pair", "z_side", "x")
 GROUP = ("z_pair", "x")
 GATHER = ("heads_0", "z_pair", "x")
+ROWS = ("heads_0", "heads_1", "z_pair", "x")
 HEADS_BATCH = ("heads_0", "heads_1", "z_pair", "z_side", "x")
 SWAP = [(0, 1), (1, 0)]
 
@@ -201,7 +202,7 @@
     )(half, arrived, gain, weight)
 
 
-def logits_kernel(firsts_ref, rows_ref, ids_ref, *refs):
+def logits_kernel(firsts_ref, rows_ref, ids_ref, value_ref, *refs):
     count = 4
     matrices, out_ref, local, flat, sems = refs[:count], *refs[count:]
     pieces, groups, tiles, lanes = rows_ref.shape
@@ -249,23 +250,25 @@
     total = jnp.sum(total, axis=1, keepdims=True)
     chosen = jnp.sum(chosen, axis=1, keepdims=True)
     lane = lax.broadcasted_iota(jnp.int32, (groups, 128), 1)
-    packed = jnp.zeros((groups, 128), jnp.float32)
+    packed = jnp.broadcast_to(value_ref[...], (groups, 128))
     owned = pieces // halves
     for n, column in enumerate((top, total, chosen)):
         for r in range(owned):
             part = column[r * groups : (r + 1) * groups]
             packed = jnp.where(lane == n * owned + r, part, packed)
-    for g in range(groups):
-        out_ref[g] = packed[g : g + 1]
-
-
-def logit_stats(all_rows, matrices, firsts, ids):
+    for place in range(out_ref.shape[0]):
+        g = place % groups
+        out_ref[place] = packed[g : g + 1]
+
+
+def logit_stats(all_rows, matrices, firsts, ids, value, places):
     groups = all_rows.shape[1]
     depth = matrices[0].shape[0]
     return pl.pallas_call(
         logits_kernel,
-        out_shape=pltpu.VMEM((groups, 1, 128), jnp.float32),
-        in_specs=[smem_spec(), vmem_spec(), vmem_spec()] + [any_spec() for _ in matrices],
+        out_shape=pltpu.VMEM((places * groups, 1, 128), jnp.float32),
+        in_specs=[smem_spec(), vmem_spec(), vmem_spec(), vmem_spec()]
+        + [any_spec() for _ in matrices],
         out_specs=vmem_spec(),
         scratch_shapes=[
             pltpu.VMEM((len(matrices), depth, 128), jnp.bfloat16),
@@ -275,7 +278,7 @@
         cost_estimate=pl.CostEstimate(flops=270000000, bytes_accessed=4700000, transcendentals=0),
         compiler_params=room(12),
         name="logits",
-    )(firsts, all_rows, ids, *matrices)
+    )(firsts, all_rows, ids, value, *matrices)
 
 
 def shifted(lines, places):
@@ -291,29 +294,7 @@
     return top, total, chosen
 
 
-def group_kernel(owned, stats_ref, value_ref, out_ref):
-    lines = stats_ref[...].reshape(stats_ref.shape[0], 128)
-    top, total, chosen = merged(lines, jnp.full(lines.shape, True), owned)
-    lane = lax.broadcasted_iota(jnp.int32, (1, 128), 1)
-    packed = jnp.where(lane < owned, top, shifted(total, owned))
-    packed = jnp.where(lane < 2 * owned, packed, chosen)
-    packed = jnp.where(lane < 3 * owned, packed, value_ref[...])
-    for n in range(out_ref.shape[0]):
-        out_ref[n] = packed
-
-
-def group_stats(stats, value, owned, copies):
-    return pl.pallas_call(
-        functools.partial(group_kernel, owned),
-        out_shape=pltpu.VMEM((copies, 1, 128), jnp.float32),
-        in_specs=[vmem_spec(), vmem_spec()],
-        out_specs=vmem_spec(),
-        compiler_params=room(2),
-        name="group",
-    )(stats, value)
-
-
-def final_kernel(owned, cores, stats_ref, logprob_ref, value_ref):
+def final_kernel(owned, cores, groups, group_ref, stats_ref, logprob_ref, value_ref):
     count = stats_ref.shape[0]
     lines = stats_ref[...].reshape(count, 128)
     place = lax.broadcasted_iota(jnp.int32, lines.shape, 0)
@@ -321,30 +302,31 @@
     row = lax.broadcasted_iota(jnp.int32, (1, 128), 1)
     logprob = jnp.zeros((1, 128), jnp.float32)
     for core in range(cores):
-        top, total, chosen = merged(lines, place % cores == core, owned)
+        top, total, chosen = merged(lines, place // groups % cores == core, owned)
         total = jnp.where(row < owned, total, 1.0)
         found = shifted(chosen, -2 * owned) - (top + jnp.log(total))
         logprob = jnp.where(row // owned == core, shifted(found, core * owned), logprob)
     values = jnp.broadcast_to(lines[:, 3 * owned : 3 * owned + 1], lines.shape)
-    here = place == (lane % owned) * (count // owned) + lane // owned
+    source = (lane % owned) * (count // groups // owned) + lane // owned
+    here = place == source * groups + group_ref[0]
     value = jnp.sum(jnp.where(here, values, 0.0), axis=0, keepdims=True)
     logprob_ref[...] = logprob[:, : logprob_ref.shape[1]]
     value_ref[...] = value[:, : value_ref.shape[1]]
 
 
-def final_values(stats, owned, cores):
+def final_values(stats, owned, cores, groups, group):
     rows = owned * cores
     return pl.pallas_call(
-        functools.partial(final_kernel, owned, cores),
+        functools.partial(final_kernel, owned, cores, groups),
         out_shape=(
             jax.ShapeDtypeStruct((1, rows), jnp.float32),
             jax.ShapeDtypeStruct((1, rows), jnp.float32),
         ),
-        in_specs=[vmem_spec()],
+        in_specs=[smem_spec(), vmem_spec()],
         out_specs=(vmem_spec(), vmem_spec()),
         compiler_params=room(2),
         name="final",
-    )(stats)
+    )(group, stats)
 
 
 def per_device(
@@ -412,9 +394,9 @@
     ids = lax.dynamic_index_in_dim(ids, side, 1, keepdims=False)
     ids = lax.dynamic_index_in_dim(ids, core, 2, keepdims=False)
     ids = ids.reshape(groups, rows_core).T.reshape(-1, 1)
-    stats = logit_stats(all_rows, matrices, firsts.astype(jnp.int32), ids)
-    stats = group_stats(exchange(stats, GROUP), value, rows_core, chips * cores)
-    logprob, values = final_values(exchange(stats, HEADS), rows_core, cores)
+    stats = logit_stats(all_rows, matrices, firsts.astype(jnp.int32), ids, value, chips * cores)
+    group = lax.axis_index(GROUP).astype(jnp.int32).reshape(1)
+    logprob, values = final_values(exchange(stats, ROWS), rows_core, cores, groups, group)
     return (logprob.reshape(-1), values.reshape(-1))
 
 

time: 103 us -> 105 us (1.019)
  blocking collectives: 24.4 us -> 0 us
  waiting for transfers between devices: 25.6 us -> 40.9 us
  starting transfers between devices: 41.4 us -> 51.2 us
    all_to_all x2 -> x0, blocking collectives: 24.4 us -> none  [exchange(): return lax.all_to_all(parts, axis, split_axis=0, concat_axis=0, tiled=True)]
    all_to_all x2 -> x3, waiting for transfers between devices: 21.2 us -> 36.5 us  [exchange(): return lax.all_to_all(parts, axis, split_axis=0, concat_axis=0, tiled=True)]
    all_to_all x2 -> x3, starting transfers between devices: 27.4 us -> 37.2 us  [exchange(): return lax.all_to_all(parts, axis, split_axis=0, concat_axis=0, tiled=True)]
    pallas_call x3 -> x2, Pallas kernels: 4.29 us -> 5.24 us  [the longest x1 4.11 us: logit_stats(): pl.pallas_call(logits_kernel, out_shape=pltpu.VMEM((places * groups, 1, 1...]
  transfers between devices with their start and end apart: 5 -> 6, of which waited for: 2 -> 3; matrix products, arithmetic and copies ran while one was open for 0% -> 0% of each run, Pallas kernels for 5% -> 5%
where the time goes in v6:
time: 105 us; the launch traced here: 104 us
  starting transfers between devices  51.2 us (49%)
  waiting for transfers between devices  40.9 us (39%)
  Pallas kernels  10.8 us (10%)
    all_to_all x3, starting transfers between devices, exchange(): return lax.all_to_all(parts, axis, split_axis=0, concat_axis=0, tiled=True)  37.2 us
    all_to_all x3, waiting for transfers between devices, exchange(): return lax.all_to_all(parts, axis, split_axis=0, concat_axis=0, tiled=True)  36.5 us
    ppermute x1, starting transfers between devices, per_device(): both_head = lax.ppermute(z_head, 'heads_1', SWAP)  7.06 us
    ppermute x1, starting transfers between devices, per_device(): z_head = lax.ppermute(lm_head, 'z_side', SWAP)  4.95 us
    pallas_call x1, Pallas kernels, head_partials(): pl.pallas_call(heads_kernel, out_shape=pltpu.VMEM((places, width // 128,...  4.58 us
    ppermute x1, waiting for transfers between devices, per_device(): z_head = lax.ppermute(lm_head, 'z_side', SWAP)  4.43 us
    pallas_call x1, Pallas kernels, logit_stats(): pl.pallas_call(logits_kernel, out_shape=pltpu.VMEM((places * groups, 1, 1...  4.11 us
  transfers between devices with their start and end apart: 6, of which 3 were waited for; matrix products, arithmetic and copies ran while one was open for 0% of the time, Pallas kernels for 5%

profile of v6, /device:TPU:1, one launch (start us, length us, event | category | flops | bytes accessed | tf_op | source)
XLA Modules:
  0.0 104.2 jit_solution(8515325031811392004)
XLA Ops:
  0.6 0.0 copy-start
  0.6 0.0 copy-start.2
  0.7 0.0 copy-start.1
  0.7 4.9 %collective-permute-start.1 = (bf16[4096,128]{1,0:T(8,128)(2,1)}, bf16[4096,128]{1,0:T(8,128)(2,1)S(1)}, u32[]{:S(2)}, u32[]{:S(2)}) collective-permute-start(bf16[4096,128]{1,0:T(8,128)(2,1)} %refs_0_.3), channel_id=1, source_target_pairs={{0,4},{4,0},{1,5},{5,1},{2,6},{6,2},{3,7},{7,3},{8,12},{12,8},{9,1... | collective-permute-start | bytes 3145736 | tf_op jit(solution)/shard_map/ppermute | solution.py:359
  5.6 0.0 copy-start.3
  5.6 4.6 %heads.1 = f32[16,32,128]{2,1,0:T(8,128)} custom-call(f32[1]{0:T(128)} %bitcast.6.first_ref, f32[2]{0:T(128)} %rate_ref.1, bf16[8,256]{1,0:T(8,128)(2,1)} %refs_0_.2, bf16[8,256]{1,0:T(8,128)(2,1)} %refs_1_.1, bf16[8,256]{1,0:T(8,128)(2,1)} %refs_2_.1, bf16[8,256]{1,0:T(8,128)(2,1)} %refs_3_.1, f32[2,8]{1,0:T(2,128)} %bitcast.22, f32[2,8]{1,0:T(2,128)} %bitcast.23, ...), custom_call_target="tpu_custom_call" | custom-call | flops 40000000 | bytes 3500000 | tf_op jit(solution)/shard_map/heads/pallas_call | solution.py:159
  10.2 8.1 %all-to-all-start = ((f32[16,32,128]{2,1,0:T(8,128)}), f32[16,32,128]{2,1,0:T(8,128)S(1)}, u32[]{:S(2)}, u32[]{:S(2)}) async-start(f32[16,32,128]{2,1,0:T(8,128)} %heads.1), calls=%async_computation | async-start | bytes 524288 | tf_op jit(solution)/shard_map/all_to_all | solution.py:25
  18.3 0.0 copy-done
  18.3 2.0 %collective-permute-start = (bf16[4096,128]{1,0:T(8,128)(2,1)S(1)}, bf16[4096,128]{1,0:T(8,128)(2,1)}, u32[]{:S(2)}, u32[]{:S(2)}) collective-permute-start(bf16[4096,128]{1,0:T(8,128)(2,1)S(1)} %copy-done), channel_id=1, source_target_pairs={{0,32},{32,0},{1,33},{33,1},{2,34},{34,2},{3,35},{35,3},{4,36},{36... | collective-permute-start | bytes 3145736 | tf_op jit(solution)/shard_map/ppermute | solution.py:360
  20.3 4.4 %collective-permute-done.1.refs_2_ = bf16[4096,128]{1,0:T(8,128)(2,1)S(1)} collective-permute-done((bf16[4096,128]{1,0:T(8,128)(2,1)}, bf16[4096,128]{1,0:T(8,128)(2,1)S(1)}, u32[]{:S(2)}, u32[]{:S(2)}) %collective-permute-start.1) | collective-permute-done | bytes 1048608 | tf_op jit(solution)/shard_map/ppermute | solution.py:359
  24.8 7.1 %collective-permute-start.2 = (bf16[4096,128]{1,0:T(8,128)(2,1)S(1)}, bf16[4096,128]{1,0:T(8,128)(2,1)}, u32[]{:S(2)}, u32[]{:S(2)}) collective-permute-start(bf16[4096,128]{1,0:T(8,128)(2,1)S(1)} %collective-permute-done.1.refs_2_), channel_id=1, source_target_pairs={{0,32},{32,0},{1,33},{33,1},{2,34},{34,2},{3,35},{35,3},{4,36},{36... | collective-permute-start | bytes 3145736 | tf_op jit(solution)/shard_map/ppermute | solution.py:361
  31.8 0.0 all-to-all-done.arrived_ref
  31.9 0.0 copy-done.2
  31.9 0.0 copy-done.1
  31.9 1.0 norm.1
  32.9 19.3 %all-to-all-start.1 = ((bf16[128,16,128]{2,1,0:T(8,128)(2,1)}), bf16[128,16,128]{2,1,0:T(8,128)(2,1)S(1)}, u32[]{:S(2)}, u32[]{:S(2)}) async-start(bf16[128,16,128]{2,1,0:T(8,128)(2,1)} %get-tuple-element.6), calls=%async_computation.1 | async-start | bytes 1048576 | tf_op jit(solution)/shard_map/all_to_all | solution.py:25
  52.2 0.0 copy-done.3
  52.3 0.1 reshape.50
  52.4 0.1 copy.20
  52.5 0.1 reshape.55.ids_ref
  52.6 0.1 add_multiply_fusion.firsts_ref
  52.7 0.0 collective-permute-done.refs_1_
  52.7 21.2 %all-to-all-done.1 = bf16[128,16,128]{2,1,0:T(8,128)(2,1)S(1)} async-done(((bf16[128,16,128]{2,1,0:T(8,128)(2,1)}), bf16[128,16,128]{2,1,0:T(8,128)(2,1)S(1)}, u32[]{:S(2)}, u32[]{:S(2)}) %all-to-all-start.1) | async-done | bytes 524320 | tf_op jit(solution)/shard_map/all_to_all | solution.py:25
  73.8 0.0 collective-permute-done.2.refs_3_
  73.9 4.1 %logits.1 = f32[256,1,128]{2,1,0:T(1,128)} custom-call(s32[4]{0:T(128)S(1)} %add_multiply_fusion.firsts_ref, bf16[8,16,16,128]{3,2,1,0:T(8,128)(2,1)S(1)} %bitcast.17, s32[64,1]{1,0:T(8,128)S(1)} %reshape.55.ids_ref, f32[1,128]{1,0:T(1,128)S(1)} %get-tuple-element.7.value_ref, bf16[4096,128]{1,0:T(8,128)(2,1)S(1)} %copy-done, ...), custom_call_target="tpu_custom_call" | custom-call | flops 270000000 | bytes 4700000 | tf_op jit(solution)/shard_map/logits/pallas_call | solution.py:267
  78.0 9.7 %all-to-all-start.2 = ((f32[256,1,128]{2,1,0:T(1,128)}), f32[256,1,128]{2,1,0:T(1,128)S(1)}, u32[]{:S(2)}, u32[]{:S(2)}) async-start(f32[256,1,128]{2,1,0:T(1,128)} %logits.1), calls=%async_computation.2 | async-start | bytes 262144 | tf_op jit(solution)/shard_map/all_to_all | solution.py:25
  87.7 15.3 %all-to-all-done.2.stats_ref = f32[256,1,128]{2,1,0:T(1,128)S(1)} async-done(((f32[256,1,128]{2,1,0:T(1,128)}), f32[256,1,128]{2,1,0:T(1,128)S(1)}, u32[]{:S(2)}, u32[]{:S(2)}) %all-to-all-start.2) | async-done | bytes 131104 | tf_op jit(solution)/shard_map/all_to_all | solution.py:25
  103.0 1.1 %final.1 = (f32[1,8]{1,0:T(1,128)}, f32[1,8]{1,0:T(1,128)}) custom-call(s32[1]{0:T(128)} %bitcast.group_ref, f32[256,1,128]{2,1,0:T(1,128)S(1)} %all-to-all-done.2.stats_ref), custom_call_target="tpu_custom_call" | custom-call | tf_op jit(solution)/shard_map/final/pallas_call | solution.py:319
  (1 shorter events, 0.0 us)
Async XLA Ops:
  0.6 17.7 %copy-start = (bf16[4096,128]{1,0:T(8,128)(2,1)S(1)}, bf16[4096,128]{1,0:T(8,128)(2,1)}, u32[]{:S(2)}) copy-start(bf16[4096,128]{1,0:T(8,128)(2,1)} %refs_0_.3) | copy-start | bytes 3145732
  0.6 31.2 %copy-start.2 = (f32[4096]{0:T(1024)S(1)}, f32[4096]{0:T(1024)}, u32[]{:S(2)}) copy-start(f32[4096]{0:T(1024)} %param.27) | copy-start | bytes 49156
  0.7 31.2 %copy-start.1 = (f32[4096]{0:T(1024)S(1)}, f32[4096]{0:T(1024)}, u32[]{:S(2)}) copy-start(f32[4096]{0:T(1024)} %param.26) | copy-start | bytes 49156
  0.7 24.1 %collective-permute-start.1 = (bf16[4096,128]{1,0:T(8,128)(2,1)}, bf16[4096,128]{1,0:T(8,128)(2,1)S(1)}, u32[]{:S(2)}, u32[]{:S(2)}) collective-permute-start(bf16[4096,128]{1,0:T(8,128)(2,1)} %refs_0_.3), channel_id=1, source_target_pairs={{0,4},{4,0},{1,5},{5,1},{2,6},{6,2},{3,7},{7,3},{8,12},{12,8},{9,1... | collective-permute-start | bytes 3145736 | tf_op jit(solution)/shard_map/ppermute | solution.py:359
  5.6 46.6 %copy-start.3 = (s32[256]{0:T(256)S(1)}, s32[256]{0:T(256)}, u32[]{:S(2)}) copy-start(s32[256]{0:T(256)} %param.29) | copy-start | bytes 3076
  10.2 21.6 %all-to-all-start = ((f32[16,32,128]{2,1,0:T(8,128)}), f32[16,32,128]{2,1,0:T(8,128)S(1)}, u32[]{:S(2)}, u32[]{:S(2)}) async-start(f32[16,32,128]{2,1,0:T(8,128)} %heads.1), calls=%async_computation | async-start | bytes 524288 | tf_op jit(solution)/shard_map/all_to_all | solution.py:25
  18.3 34.3 %collective-permute-start = (bf16[4096,128]{1,0:T(8,128)(2,1)S(1)}, bf16[4096,128]{1,0:T(8,128)(2,1)}, u32[]{:S(2)}, u32[]{:S(2)}) collective-permute-start(bf16[4096,128]{1,0:T(8,128)(2,1)S(1)} %copy-done), channel_id=1, source_target_pairs={{0,32},{32,0},{1,33},{33,1},{2,34},{34,2},{3,35},{35,3},{4,36},{36... | collective-permute-start | bytes 3145736 | tf_op jit(solution)/shard_map/ppermute | solution.py:360
  24.8 49.1 %collective-permute-start.2 = (bf16[4096,128]{1,0:T(8,128)(2,1)S(1)}, bf16[4096,128]{1,0:T(8,128)(2,1)}, u32[]{:S(2)}, u32[]{:S(2)}) collective-permute-start(bf16[4096,128]{1,0:T(8,128)(2,1)S(1)} %collective-permute-done.1.refs_2_), channel_id=1, source_target_pairs={{0,32},{32,0},{1,33},{33,1},{2,34},{34,2},{3,35},{35,3},{4,36},{36... | collective-permute-start | bytes 3145736 | tf_op jit(solution)/shard_map/ppermute | solution.py:361
  32.9 41.0 %all-to-all-start.1 = ((bf16[128,16,128]{2,1,0:T(8,128)(2,1)}), bf16[128,16,128]{2,1,0:T(8,128)(2,1)S(1)}, u32[]{:S(2)}, u32[]{:S(2)}) async-start(bf16[128,16,128]{2,1,0:T(8,128)(2,1)} %get-tuple-element.6), calls=%async_computation.1 | async-start | bytes 1048576 | tf_op jit(solution)/shard_map/all_to_all | solution.py:25
  78.0 25.1 %all-to-all-start.2 = ((f32[256,1,128]{2,1,0:T(1,128)}), f32[256,1,128]{2,1,0:T(1,128)S(1)}, u32[]{:S(2)}, u32[]{:S(2)}) async-start(f32[256,1,128]{2,1,0:T(1,128)} %logits.1), calls=%async_computation.2 | async-start | bytes 262144 | tf_op jit(solution)/shard_map/all_to_all | solution.py:25

commit v7 on v5

--- a/solution.py
+++ b/solution.py
@@ -11,8 +11,8 @@
 
 HEADS = ("heads_0", "heads_1")
 BATCH = ("z_pair", "z_side", "x")
-GROUP = ("z_pair", "x")
-GATHER = ("heads_0", "z_pair", "x")
+GROUP = ("x", "z_pair")
+NEAR = ("z_pair", "heads_0")
 HEADS_BATCH = ("heads_0", "heads_1", "z_pair", "z_side", "x")
 SWAP = [(0, 1), (1, 0)]
 
@@ -204,7 +204,7 @@
 def logits_kernel(firsts_ref, rows_ref, ids_ref, *refs):
     count = 4
     matrices, out_ref, local, flat, sems = refs[:count], *refs[count:]
-    pieces, groups, tiles, lanes = rows_ref.shape
+    groups, pieces, tiles, lanes = rows_ref.shape
     deep = tiles * lanes
     halves = local.shape[1] // deep
     copies = []
@@ -222,9 +222,9 @@
     flat[...] = rows_ref[...].reshape(flat.shape).astype(jnp.float32)
 
     def rows_of(piece):
-        start = piece * groups * tiles
+        first, step = piece * tiles, pieces * tiles
         return jnp.concatenate(
-            [flat[pl.ds(start + t, groups, stride=tiles), :] for t in range(tiles)], axis=1
+            [flat[pl.ds(first + t, groups, stride=step), :] for t in range(tiles)], axis=1
         ).astype(jnp.bfloat16)
 
     sums = [None] * count
@@ -260,7 +260,7 @@
 
 
 def logit_stats(all_rows, matrices, firsts, ids):
-    groups = all_rows.shape[1]
+    groups = all_rows.shape[0]
     depth = matrices[0].shape[0]
     return pl.pallas_call(
         logits_kernel,
@@ -398,9 +398,12 @@
     gain = final_gain.reshape(lines, lanes)
     weight = value_weight.reshape(lines, lanes)
     half_here = (chip % copies).astype(jnp.int32).reshape(1)
-    pieces, value = norm_pieces(arrived, gain, weight, half_here, chips * groups, lines // copies)
-    all_rows = exchange(pieces, GATHER)
-    all_rows = all_rows.reshape(chips, groups, lines // copies, lanes)
+    near = lax.axis_size(NEAR)
+    pieces, value = norm_pieces(arrived, gain, weight, half_here, near, lines // copies)
+    near_rows = exchange(pieces, NEAR)
+    far = lax.axis_size("x")
+    all_rows = exchange(jnp.broadcast_to(near_rows[None], (far, *near_rows.shape)), "x")
+    all_rows = all_rows.reshape(groups, chips, lines // copies, lanes)
 
     vocab_own = lm_head.shape[1]
     flat = lax.axis_index(HEADS_BATCH)
@@ -411,7 +414,7 @@
     ids = sampled.reshape(-1, lax.axis_size("z_side"), lax.axis_size("x"), cores, rows_core)
     ids = lax.dynamic_index_in_dim(ids, side, 1, keepdims=False)
     ids = lax.dynamic_index_in_dim(ids, core, 2, keepdims=False)
-    ids = ids.reshape(groups, rows_core).T.reshape(-1, 1)
+    ids = ids.transpose(2, 1, 0).reshape(-1, 1)
     stats = logit_stats(all_rows, matrices, firsts.astype(jnp.int32), ids)
     stats = group_stats(exchange(stats, GROUP), value, rows_core, chips * cores)
     logprob, values = final_values(exchange(stats, HEADS), rows_core, cores)

time: 103 us -> 102 us (level)
  blocking collectives: 24.4 us -> 53.2 us
  starting transfers between devices: 41.4 us -> 26.1 us
  waiting for transfers between devices: 25.6 us -> 11.1 us
    all_to_all x2 -> x3, blocking collectives: 24.4 us -> 53.2 us  [exchange(): return lax.all_to_all(parts, axis, split_axis=0, concat_axis=0, tiled=True)]
    all_to_all x2, starting transfers between devices: 27.4 us -> 12.1 us  [exchange(): return lax.all_to_all(parts, axis, split_axis=0, concat_axis=0, tiled=True)]
    all_to_all x2, waiting for transfers between devices: 21.2 us -> 6.54 us  [exchange(): return lax.all_to_all(parts, axis, split_axis=0, concat_axis=0, tiled=True)]
  transfers between devices with their start and end apart: 5 -> 5, of which waited for: 2 -> 2; matrix products, arithmetic and copies ran while one was open for 0% -> 1% of each run, Pallas kernels for 5% -> 5%
where the time goes in v7:
time: 102 us; the launch traced here: 101 us
  blocking collectives  53.2 us (52%)
  starting transfers between devices  26.1 us (26%)
  waiting for transfers between devices  11.1 us (11%)
  Pallas kernels  9.01 us (9%)
  local copies, waits for them, and re-layouts  1.22 us (1%)
    all_to_all x3, blocking collectives, exchange(): return lax.all_to_all(parts, axis, split_axis=0, concat_axis=0, tiled=True)  53.2 us
    all_to_all x2, starting transfers between devices, exchange(): return lax.all_to_all(parts, axis, split_axis=0, concat_axis=0, tiled=True)  12.1 us
    ppermute x1, starting transfers between devices, per_device(): both_head = lax.ppermute(z_head, 'heads_1', SWAP)  7.06 us
    all_to_all x2, waiting for transfers between devices, exchange(): return lax.all_to_all(parts, axis, split_axis=0, concat_axis=0, tiled=True)  6.54 us
    ppermute x1, starting transfers between devices, per_device(): z_head = lax.ppermute(lm_head, 'z_side', SWAP)  4.95 us
    ppermute x1, waiting for transfers between devices, per_device(): z_head = lax.ppermute(lm_head, 'z_side', SWAP)  4.58 us
    pallas_call x1, Pallas kernels, head_partials(): pl.pallas_call(heads_kernel, out_shape=pltpu.VMEM((places, width // 128,...  4.42 us
    pallas_call x1, Pallas kernels, logit_stats(): pl.pallas_call(logits_kernel, out_shape=pltpu.VMEM((groups, 1, 128), jnp....  3.59 us
  transfers between devices with their start and end apart: 5, of which 2 were waited for; matrix products, arithmetic and copies ran while one was open for 1% of the time, Pallas kernels for 5%

profile of v7, /device:TPU:1, one launch (start us, length us, event | category | flops | bytes accessed | tf_op | source)
XLA Modules:
  0.0 101.5 jit_solution(3271757562996511600)
XLA Ops:
  0.6 0.0 copy-start
  0.6 0.0 copy-start.2
  0.7 0.0 copy-start.1
  0.7 4.9 %collective-permute-start.1 = (bf16[4096,128]{1,0:T(8,128)(2,1)}, bf16[4096,128]{1,0:T(8,128)(2,1)S(1)}, u32[]{:S(2)}, u32[]{:S(2)}) collective-permute-start(bf16[4096,128]{1,0:T(8,128)(2,1)} %refs_0_.3), channel_id=1, source_target_pairs={{0,4},{4,0},{1,5},{5,1},{2,6},{6,2},{3,7},{7,3},{8,12},{12,8},{9,1... | collective-permute-start | bytes 3145736 | tf_op jit(solution)/shard_map/ppermute | solution.py:377
  5.6 4.4 %heads.1 = f32[16,32,128]{2,1,0:T(8,128)} custom-call(f32[1]{0:T(128)} %bitcast.5.first_ref, f32[2]{0:T(128)} %rate_ref.1, bf16[8,256]{1,0:T(8,128)(2,1)} %refs_0_.2, bf16[8,256]{1,0:T(8,128)(2,1)} %refs_1_.1, bf16[8,256]{1,0:T(8,128)(2,1)} %refs_2_.1, bf16[8,256]{1,0:T(8,128)(2,1)} %refs_3_.1, f32[2,8]{1,0:T(2,128)} %bitcast.21, f32[2,8]{1,0:T(2,128)} %bitcast.22, ...), custom_call_target="tpu_custom_call" | custom-call | flops 40000000 | bytes 3500000 | tf_op jit(solution)/shard_map/heads/pallas_call | solution.py:158
  10.1 0.0 copy-start.3
  10.1 8.1 %all-to-all-start = ((f32[16,32,128]{2,1,0:T(8,128)}), f32[16,32,128]{2,1,0:T(8,128)S(1)}, u32[]{:S(2)}, u32[]{:S(2)}) async-start(f32[16,32,128]{2,1,0:T(8,128)} %heads.1), calls=%async_computation | async-start | bytes 524288 | tf_op jit(solution)/shard_map/all_to_all | solution.py:24
  18.2 0.0 copy-done
  18.2 2.0 %collective-permute-start = (bf16[4096,128]{1,0:T(8,128)(2,1)S(1)}, bf16[4096,128]{1,0:T(8,128)(2,1)}, u32[]{:S(2)}, u32[]{:S(2)}) collective-permute-start(bf16[4096,128]{1,0:T(8,128)(2,1)S(1)} %copy-done), channel_id=1, source_target_pairs={{0,32},{32,0},{1,33},{33,1},{2,34},{34,2},{3,35},{35,3},{4,36},{36... | collective-permute-start | bytes 3145736 | tf_op jit(solution)/shard_map/ppermute | solution.py:378
  20.2 4.6 %collective-permute-done.1.refs_2_ = bf16[4096,128]{1,0:T(8,128)(2,1)S(1)} collective-permute-done((bf16[4096,128]{1,0:T(8,128)(2,1)}, bf16[4096,128]{1,0:T(8,128)(2,1)S(1)}, u32[]{:S(2)}, u32[]{:S(2)}) %collective-permute-start.1) | collective-permute-done | bytes 1048608 | tf_op jit(solution)/shard_map/ppermute | solution.py:377
  24.8 7.1 %collective-permute-start.2 = (bf16[4096,128]{1,0:T(8,128)(2,1)S(1)}, bf16[4096,128]{1,0:T(8,128)(2,1)}, u32[]{:S(2)}, u32[]{:S(2)}) collective-permute-start(bf16[4096,128]{1,0:T(8,128)(2,1)S(1)} %collective-permute-done.1.refs_2_), channel_id=1, source_target_pairs={{0,32},{32,0},{1,33},{33,1},{2,34},{34,2},{3,35},{35,3},{4,36},{36... | collective-permute-start | bytes 3145736 | tf_op jit(solution)/shard_map/ppermute | solution.py:379
  31.8 0.0 all-to-all-done.arrived_ref
  31.9 0.0 copy-done.2
  31.9 0.0 copy-done.1
  31.9 0.2 norm.1
  32.0 26.4 %all_to_all.25 = bf16[32,16,128]{2,1,0:T(8,128)(2,1)S(1)} all-to-all(bf16[32,16,128]{2,1,0:T(8,128)(2,1)S(1)} %get-tuple-element.6), channel_id=1, replica_groups=mesh['heads_0'=8,'heads_1'=2,'z_pair'=4,'z_side'=2,'x'=4] {'z_pair','hea..., dimensions={0} | all-to-all | bytes 262144 | tf_op jit(solution)/shard_map/all_to_all | solution.py:24
  58.5 0.9 broadcast_in_dim.2
  59.4 4.0 %all-to-all-start.2 = ((bf16[4,32,16,128]{3,2,1,0:T(8,128)(2,1)}), bf16[4,32,16,128]{3,2,1,0:T(8,128)(2,1)S(1)}, u32[]{:S(2)}, u32[]{:S(2)}) async-start(bf16[4,32,16,128]{3,2,1,0:T(8,128)(2,1)} %broadcast_in_dim.2), calls=%async_computation.2 | async-start | bytes 1048576 | tf_op jit(solution)/shard_map/all_to_all | solution.py:24
  63.4 0.0 copy-done.3
  63.4 0.1 reshape.43
  63.5 0.1 copy.19
  63.6 0.1 reshape.47.ids_ref
  63.7 0.1 add_multiply_fusion.firsts_ref
  63.8 0.0 collective-permute-done.refs_1_
  63.8 6.5 %all-to-all-done.2 = bf16[4,32,16,128]{3,2,1,0:T(8,128)(2,1)S(1)} async-done(((bf16[4,32,16,128]{3,2,1,0:T(8,128)(2,1)}), bf16[4,32,16,128]{3,2,1,0:T(8,128)(2,1)S(1)}, u32[]{:S(2)}, u32[]{:S(2)}) %all-to-all-start.2) | async-done | bytes 524320 | tf_op jit(solution)/shard_map/all_to_all | solution.py:24
  70.3 0.0 collective-permute-done.2.refs_3_
  70.3 3.6 %logits.1 = f32[16,1,128]{2,1,0:T(1,128)S(1)} custom-call(s32[4]{0:T(128)S(1)} %add_multiply_fusion.firsts_ref, bf16[16,8,16,128]{3,2,1,0:T(8,128)(2,1)S(1)} %bitcast.17, s32[64,1]{1,0:T(8,128)S(1)} %reshape.47.ids_ref, bf16[4096,128]{1,0:T(8,128)(2,1)S(1)} %copy-done, bf16[4096,128]{1,0:T(8,128)(2,1)} %collective-permute-done.refs_1_, ...), custom_call_target="tpu_custom_call" | custom-call | flops 270000000 | bytes 4700000 | tf_op jit(solution)/shard_map/logits/pallas_call | solution.py:265
  73.9 12.1 %all_to_all.26.stats_ref = f32[16,1,128]{2,1,0:T(1,128)S(1)} all-to-all(f32[16,1,128]{2,1,0:T(1,128)S(1)} %logits.1), channel_id=1, replica_groups=mesh['heads_0'=8,'heads_1'=2,'z_pair'=4,'z_side'=2,'x'=4] {'x','z_pair'}, dimensions={0} | all-to-all | bytes 16384 | tf_op jit(solution)/shard_map/all_to_all | solution.py:24
  86.0 0.2 group.1
  86.1 14.7 %all_to_all.27.stats_ref = f32[16,1,128]{2,1,0:T(1,128)S(1)} all-to-all(f32[16,1,128]{2,1,0:T(1,128)S(1)} %group.1), channel_id=1, replica_groups=mesh['heads_0'=8,'heads_1'=2,'z_pair'=4,'z_side'=2,'x'=4] {'heads_0','he..., dimensions={0} | all-to-all | bytes 16384 | tf_op jit(solution)/shard_map/all_to_all | solution.py:24
  100.8 0.7 final.1
  (1 shorter events, 0.0 us)
Async XLA Ops:
  0.6 17.5 %copy-start = (bf16[4096,128]{1,0:T(8,128)(2,1)S(1)}, bf16[4096,128]{1,0:T(8,128)(2,1)}, u32[]{:S(2)}) copy-start(bf16[4096,128]{1,0:T(8,128)(2,1)} %refs_0_.3) | copy-start | bytes 3145732
  0.6 31.2 %copy-start.2 = (f32[4096]{0:T(1024)S(1)}, f32[4096]{0:T(1024)}, u32[]{:S(2)}) copy-start(f32[4096]{0:T(1024)} %param.27) | copy-start | bytes 49156
  0.7 31.2 %copy-start.1 = (f32[4096]{0:T(1024)S(1)}, f32[4096]{0:T(1024)}, u32[]{:S(2)}) copy-start(f32[4096]{0:T(1024)} %param.26) | copy-start | bytes 49156
  0.7 24.1 %collective-permute-start.1 = (bf16[4096,128]{1,0:T(8,128)(2,1)}, bf16[4096,128]{1,0:T(8,128)(2,1)S(1)}, u32[]{:S(2)}, u32[]{:S(2)}) collective-permute-start(bf16[4096,128]{1,0:T(8,128)(2,1)} %refs_0_.3), channel_id=1, source_target_pairs={{0,4},{4,0},{1,5},{5,1},{2,6},{6,2},{3,7},{7,3},{8,12},{12,8},{9,1... | collective-permute-start | bytes 3145736 | tf_op jit(solution)/shard_map/ppermute | solution.py:377
  10.1 53.3 %copy-start.3 = (s32[256]{0:T(256)S(1)}, s32[256]{0:T(256)}, u32[]{:S(2)}) copy-start(s32[256]{0:T(256)} %param.29) | copy-start | bytes 3076
  10.1 21.8 %all-to-all-start = ((f32[16,32,128]{2,1,0:T(8,128)}), f32[16,32,128]{2,1,0:T(8,128)S(1)}, u32[]{:S(2)}, u32[]{:S(2)}) async-start(f32[16,32,128]{2,1,0:T(8,128)} %heads.1), calls=%async_computation | async-start | bytes 524288 | tf_op jit(solution)/shard_map/all_to_all | solution.py:24
  18.2 45.6 %collective-permute-start = (bf16[4096,128]{1,0:T(8,128)(2,1)S(1)}, bf16[4096,128]{1,0:T(8,128)(2,1)}, u32[]{:S(2)}, u32[]{:S(2)}) collective-permute-start(bf16[4096,128]{1,0:T(8,128)(2,1)S(1)} %copy-done), channel_id=1, source_target_pairs={{0,32},{32,0},{1,33},{33,1},{2,34},{34,2},{3,35},{35,3},{4,36},{36... | collective-permute-start | bytes 3145736 | tf_op jit(solution)/shard_map/ppermute | solution.py:378
  24.8 45.6 %collective-permute-start.2 = (bf16[4096,128]{1,0:T(8,128)(2,1)S(1)}, bf16[4096,128]{1,0:T(8,128)(2,1)}, u32[]{:S(2)}, u32[]{:S(2)}) collective-permute-start(bf16[4096,128]{1,0:T(8,128)(2,1)S(1)} %collective-permute-done.1.refs_2_), channel_id=1, source_target_pairs={{0,32},{32,0},{1,33},{33,1},{2,34},{34,2},{3,35},{35,3},{4,36},{36... | collective-permute-start | bytes 3145736 | tf_op jit(solution)/shard_map/ppermute | solution.py:379
  59.4 11.0 %all-to-all-start.2 = ((bf16[4,32,16,128]{3,2,1,0:T(8,128)(2,1)}), bf16[4,32,16,128]{3,2,1,0:T(8,128)(2,1)S(1)}, u32[]{:S(2)}, u32[]{:S(2)}) async-start(bf16[4,32,16,128]{3,2,1,0:T(8,128)(2,1)} %broadcast_in_dim.2), calls=%async_computation.2 | async-start | bytes 1048576 | tf_op jit(solution)/shard_map/all_to_all | solution.py:24

commit v8 on v7

--- a/solution.py
+++ b/solution.py
@@ -10,10 +10,10 @@
 
 
 HEADS = ("heads_0", "heads_1")
-BATCH = ("z_pair", "z_side", "x")
-GROUP = ("x", "z_pair")
-NEAR = ("z_pair", "heads_0")
-HEADS_BATCH = ("heads_0", "heads_1", "z_pair", "z_side", "x")
+BATCH = ("z", "x_pair", "x_side")
+GROUP = ("x_pair", "z")
+NEAR = ("z", "heads_0")
+HEADS_BATCH = ("heads_0", "heads_1", "z", "x_pair", "x_side")
 SWAP = [(0, 1), (1, 0)]
 
 
@@ -201,10 +201,11 @@
     )(half, arrived, gain, weight)
 
 
-def logits_kernel(firsts_ref, rows_ref, ids_ref, *refs):
+def logits_kernel(groups, firsts_ref, pair_ref, near_ref, far_ref, ids_ref, *refs):
     count = 4
     matrices, out_ref, local, flat, sems = refs[:count], *refs[count:]
-    groups, pieces, tiles, lanes = rows_ref.shape
+    size, (_, tiles, lanes) = near_ref.shape[0] * near_ref.shape[1], near_ref.shape
+    pieces = flat.shape[0] // (groups * tiles)
     deep = tiles * lanes
     halves = local.shape[1] // deep
     copies = []
@@ -219,7 +220,9 @@
             )
     for copy in copies:
         copy.start()
-    flat[...] = rows_ref[...].reshape(flat.shape).astype(jnp.float32)
+    for start, ref in ((pair_ref[0] * size, near_ref), ((1 - pair_ref[0]) * size, far_ref)):
+        part = pl.ds(pl.multiple_of(start, size), size)
+        flat[part, :] = ref[...].reshape(size, lanes).astype(jnp.float32)
 
     def rows_of(piece):
         first, step = piece * tiles, pieces * tiles
@@ -259,23 +262,23 @@
         out_ref[g] = packed[g : g + 1]
 
 
-def logit_stats(all_rows, matrices, firsts, ids):
-    groups = all_rows.shape[0]
+def logit_stats(near_rows, far_rows, pair, matrices, firsts, ids, groups):
     depth = matrices[0].shape[0]
     return pl.pallas_call(
-        logits_kernel,
+        functools.partial(logits_kernel, groups),
         out_shape=pltpu.VMEM((groups, 1, 128), jnp.float32),
-        in_specs=[smem_spec(), vmem_spec(), vmem_spec()] + [any_spec() for _ in matrices],
+        in_specs=[smem_spec(), smem_spec(), vmem_spec(), vmem_spec(), vmem_spec()]
+        + [any_spec() for _ in matrices],
         out_specs=vmem_spec(),
         scratch_shapes=[
             pltpu.VMEM((len(matrices), depth, 128), jnp.bfloat16),
-            pltpu.VMEM((all_rows.size // 128, 128), jnp.float32),
+            pltpu.VMEM((2 * near_rows.size // 128, 128), jnp.float32),
             pltpu.SemaphoreType.DMA((2 * len(matrices),)),
         ],
         cost_estimate=pl.CostEstimate(flops=270000000, bytes_accessed=4700000, transcendentals=0),
         compiler_params=room(12),
         name="logits",
-    )(firsts, all_rows, ids, *matrices)
+    )(firsts, pair, near_rows, far_rows, ids, *matrices)
 
 
 def shifted(lines, places):
@@ -367,17 +370,16 @@
     chips, cores = lax.axis_size("heads_0"), lax.axis_size("heads_1")
     groups = lax.axis_size(GROUP)
     chip, core = lax.axis_index("heads_0"), lax.axis_index("heads_1")
-    side = lax.axis_index("z_side")
+    side = lax.axis_index("x_side")
     rows_own, width = residual.shape
     rows_core = rows_own // cores
     copies = chips // rows_core
     lanes = 128
     lines = width // lanes
 
-    z_head = lax.ppermute(lm_head, "z_side", SWAP)
+    x_head = lax.ppermute(lm_head, "x_side", SWAP)
     core_head = lax.ppermute(lm_head, "heads_1", SWAP)
-    both_head = lax.ppermute(z_head, "heads_1", SWAP)
-
+    both_head = lax.ppermute(x_head, "heads_1", SWAP)
     first = jnp.where((chip == 0) & (core == 0), 1.0, 0.0).reshape(1)
     partial_out = head_partials(
         queries,
@@ -401,21 +403,20 @@
     near = lax.axis_size(NEAR)
     pieces, value = norm_pieces(arrived, gain, weight, half_here, near, lines // copies)
     near_rows = exchange(pieces, NEAR)
-    far = lax.axis_size("x")
-    all_rows = exchange(jnp.broadcast_to(near_rows[None], (far, *near_rows.shape)), "x")
-    all_rows = all_rows.reshape(groups, chips, lines // copies, lanes)
+    far_rows = lax.ppermute(near_rows, "x_pair", SWAP)
 
     vocab_own = lm_head.shape[1]
     flat = lax.axis_index(HEADS_BATCH)
     across = (1 - 2 * core) * lax.axis_size(BATCH)
-    along = (1 - 2 * side) * lax.axis_size("x")
-    matrices = (lm_head, core_head, z_head, both_head)
+    along = 1 - 2 * side
+    matrices = (lm_head, core_head, x_head, both_head)
     firsts = jnp.stack([flat, flat + across, flat + along, flat + across + along]) * vocab_own
-    ids = sampled.reshape(-1, lax.axis_size("z_side"), lax.axis_size("x"), cores, rows_core)
-    ids = lax.dynamic_index_in_dim(ids, side, 1, keepdims=False)
+    pair = lax.axis_index("x_pair").astype(jnp.int32).reshape(1)
+    ids = sampled.reshape(lax.axis_size("z"), lax.axis_size("x_pair"), -1, cores, rows_core)
+    ids = lax.dynamic_index_in_dim(ids, side, 2, keepdims=False)
     ids = lax.dynamic_index_in_dim(ids, core, 2, keepdims=False)
     ids = ids.transpose(2, 1, 0).reshape(-1, 1)
-    stats = logit_stats(all_rows, matrices, firsts.astype(jnp.int32), ids)
+    stats = logit_stats(near_rows, far_rows, pair, matrices, firsts.astype(jnp.int32), ids, groups)
     stats = group_stats(exchange(stats, GROUP), value, rows_core, chips * cores)
     logprob, values = final_values(exchange(stats, HEADS), rows_core, cores)
     return (logprob.reshape(-1), values.reshape(-1))
@@ -423,7 +424,7 @@
 
 def solution(mesh):
     torus = Mesh(
-        mesh.devices.reshape(8, 2, 4, 2, 4), ("heads_0", "heads_1", "z_pair", "z_side", "x")
+        mesh.devices.reshape(8, 2, 8, 2, 2), ("heads_0", "heads_1", "z", "x_pair", "x_side")
     )
     return jax.shard_map(
         per_device,

time: 102 us -> 104 us (1.020)
  blocking collectives: 53.2 us -> 58.5 us
  waiting for transfers between devices: 11.1 us -> 7.4 us
    all_to_all x2 -> x1, waiting for transfers between devices: 6.54 us -> 0.01 us  [exchange(): return lax.all_to_all(parts, axis, split_axis=0, concat_axis=0, tiled=True)]
    all_to_all x3, blocking collectives: 53.2 us -> 58.5 us  [exchange(): return lax.all_to_all(parts, axis, split_axis=0, concat_axis=0, tiled=True)]
    ppermute x2 -> x3, starting transfers between devices: 12 us -> 16.6 us  [the longest x1 7.94 us: per_device(): both_head = lax.ppermute(x_head, 'heads_1', SWAP)]
    all_to_all x2 -> x1, starting transfers between devices: 12.1 us -> 8.15 us  [exchange(): return lax.all_to_all(parts, axis, split_axis=0, concat_axis=0, tiled=True)]
    ppermute x2 -> x3, waiting for transfers between devices: 4.58 us -> 7.39 us  [the longest x1 4.03 us: per_device(): far_rows = lax.ppermute(near_rows, 'x_pair', SWAP)]
  transfers between devices with their start and end apart: 5 -> 5, of which waited for: 2 -> 2; matrix products, arithmetic and copies ran while one was open for 1% -> 0% of each run, Pallas kernels for 5% -> 5%
where the time goes in v8:
time: 104 us
  blocking collectives  58.5 us (56%)
  starting transfers between devices  26.9 us (26%)
  Pallas kernels  9.5 us (9%)
  waiting for transfers between devices  7.4 us (7%)
    all_to_all x3, blocking collectives, exchange(): return lax.all_to_all(parts, axis, split_axis=0, concat_axis=0, tiled=True)  58.5 us
    all_to_all x1, starting transfers between devices, exchange(): return lax.all_to_all(parts, axis, split_axis=0, concat_axis=0, tiled=True)  8.15 us
    ppermute x1, starting transfers between devices, per_device(): both_head = lax.ppermute(x_head, 'heads_1', SWAP)  7.94 us
    ppermute x1, starting transfers between devices, per_device(): far_rows = lax.ppermute(near_rows, 'x_pair', SWAP)  4.64 us
    pallas_call x1, Pallas kernels, head_partials(): pl.pallas_call(heads_kernel, out_shape=pltpu.VMEM((places, width // 128,...  4.57 us
    ppermute x1, starting transfers between devices, per_device(): x_head = lax.ppermute(lm_head, 'x_side', SWAP)  4.07 us
    ppermute x1, waiting for transfers between devices, per_device(): far_rows = lax.ppermute(near_rows, 'x_pair', SWAP)  4.03 us
    pallas_call x1, Pallas kernels, logit_stats(): pl.pallas_call(functools.partial(logits_kernel, groups), out_shape=pltpu....  3.92 us
  transfers between devices with their start and end apart: 5, of which 2 were waited for; matrix products, arithmetic and copies ran while one was open for 0% of the time, Pallas kernels for 5%

profile of v8, /device:TPU:1, one launch (start us, length us, event | category | flops | bytes accessed | tf_op | source)
XLA Modules:
  0.0 103.6 jit_solution(17366569729411877902)
XLA Ops:
  0.6 0.0 copy-start
  0.6 0.0 copy-start.2
  0.7 0.0 copy-start.1
  0.7 4.1 %collective-permute-start.2 = (bf16[4096,128]{1,0:T(8,128)(2,1)}, bf16[4096,128]{1,0:T(8,128)(2,1)S(1)}, u32[]{:S(2)}, u32[]{:S(2)}) collective-permute-start(bf16[4096,128]{1,0:T(8,128)(2,1)} %refs_0_.3), channel_id=1, source_target_pairs={{0,1},{1,0},{2,3},{3,2},{4,5},{5,4},{6,7},{7,6},{8,9},{9,8},{10,11... | collective-permute-start | bytes 3145736 | tf_op jit(solution)/shard_map/ppermute | solution.py:380
  4.8 0.0 copy-start.3
  4.8 4.6 %heads.1 = f32[16,32,128]{2,1,0:T(8,128)} custom-call(f32[1]{0:T(128)} %bitcast.6.first_ref, f32[2]{0:T(128)} %rate_ref.1, bf16[8,256]{1,0:T(8,128)(2,1)} %refs_0_.2, bf16[8,256]{1,0:T(8,128)(2,1)} %refs_1_.1, bf16[8,256]{1,0:T(8,128)(2,1)} %refs_2_.1, bf16[8,256]{1,0:T(8,128)(2,1)} %refs_3_.1, f32[2,8]{1,0:T(2,128)} %bitcast.20, f32[2,8]{1,0:T(2,128)} %bitcast.21, ...), custom_call_target="tpu_custom_call" | custom-call | flops 40000000 | bytes 3500000 | tf_op jit(solution)/shard_map/heads/pallas_call | solution.py:158
  9.3 8.2 %all-to-all-start = ((f32[16,32,128]{2,1,0:T(8,128)}), f32[16,32,128]{2,1,0:T(8,128)S(1)}, u32[]{:S(2)}, u32[]{:S(2)}) async-start(f32[16,32,128]{2,1,0:T(8,128)} %heads.1), calls=%async_computation | async-start | bytes 524288 | tf_op jit(solution)/shard_map/all_to_all | solution.py:24
  17.5 0.0 copy-done
  17.5 2.1 %collective-permute-start.1 = (bf16[4096,128]{1,0:T(8,128)(2,1)S(1)}, bf16[4096,128]{1,0:T(8,128)(2,1)S(1)}, u32[]{:S(2)}, u32[]{:S(2)}) collective-permute-start(bf16[4096,128]{1,0:T(8,128)(2,1)S(1)} %copy-done), channel_id=1, source_target_pairs={{0,32},{32,0},{1,33},{33,1},{2,34},{34,2},{3,35},{35,3},{4,36},{36... | collective-permute-start | bytes 3145736 | tf_op jit(solution)/shard_map/ppermute | solution.py:381
  19.6 3.4 %collective-permute-done.2.refs_2_ = bf16[4096,128]{1,0:T(8,128)(2,1)S(1)} collective-permute-done((bf16[4096,128]{1,0:T(8,128)(2,1)}, bf16[4096,128]{1,0:T(8,128)(2,1)S(1)}, u32[]{:S(2)}, u32[]{:S(2)}) %collective-permute-start.2) | collective-permute-done | bytes 1048608 | tf_op jit(solution)/shard_map/ppermute | solution.py:380
  23.0 7.9 %collective-permute-start.3 = (bf16[4096,128]{1,0:T(8,128)(2,1)S(1)}, bf16[4096,128]{1,0:T(8,128)(2,1)}, u32[]{:S(2)}, u32[]{:S(2)}) collective-permute-start(bf16[4096,128]{1,0:T(8,128)(2,1)S(1)} %collective-permute-done.2.refs_2_), channel_id=1, source_target_pairs={{0,32},{32,0},{1,33},{33,1},{2,34},{34,2},{3,35},{35,3},{4,36},{36... | collective-permute-start | bytes 3145736 | tf_op jit(solution)/shard_map/ppermute | solution.py:382
  31.0 0.0 all-to-all-done.arrived_ref
  31.0 0.0 copy-done.2
  31.0 0.0 copy-done.1
  31.0 0.2 norm.1
  31.2 29.9 %all_to_all.20.near_ref = bf16[64,16,128]{2,1,0:T(8,128)(2,1)S(1)} all-to-all(bf16[64,16,128]{2,1,0:T(8,128)(2,1)S(1)} %get-tuple-element.6), channel_id=1, replica_groups=mesh['heads_0'=8,'heads_1'=2,'z'=8,'x_pair'=2,'x_side'=2] {'z','heads_0'}, dimensions={0} | all-to-all | bytes 524288 | tf_op jit(solution)/shard_map/all_to_all | solution.py:24
  61.1 4.6 %collective-permute-start = (bf16[64,16,128]{2,1,0:T(8,128)(2,1)S(1)}, bf16[64,16,128]{2,1,0:T(8,128)(2,1)}, u32[]{:S(2)}, u32[]{:S(2)}) collective-permute-start(bf16[64,16,128]{2,1,0:T(8,128)(2,1)S(1)} %all_to_all.20.near_ref), channel_id=1, source_target_pairs={{0,2},{2,0},{1,3},{3,1},{4,6},{6,4},{5,7},{7,5},{8,10},{10,8},{9,1... | collective-permute-start | bytes 786440 | tf_op jit(solution)/shard_map/ppermute | solution.py:406
  65.8 0.0 copy-done.3
  65.8 0.1 reshape.42
  65.9 0.1 copy.19
  66.0 0.1 reshape.46.ids_ref
  66.1 0.1 add_multiply_fusion.firsts_ref
  66.2 0.0 collective-permute-done.1.refs_1_
  66.2 4.0 %collective-permute-done.far_ref = bf16[64,16,128]{2,1,0:T(8,128)(2,1)} collective-permute-done((bf16[64,16,128]{2,1,0:T(8,128)(2,1)S(1)}, bf16[64,16,128]{2,1,0:T(8,128)(2,1)}, u32[]{:S(2)}, u32[]{:S(2)}) %collective-permute-start) | collective-permute-done | bytes 262176 | tf_op jit(solution)/shard_map/ppermute | solution.py:406
  70.2 0.0 collective-permute-done.3.refs_3_
  70.2 3.9 %logits.1 = f32[16,1,128]{2,1,0:T(1,128)S(1)} custom-call(s32[4]{0:T(128)S(1)} %add_multiply_fusion.firsts_ref, s32[1]{0:T(128)} %bitcast.4.pair_ref, bf16[64,16,128]{2,1,0:T(8,128)(2,1)S(1)} %all_to_all.20.near_ref, bf16[64,16,128]{2,1,0:T(8,128)(2,1)} %collective-permute-done.far_ref, s32[64,1]{1,0:T(8,128)S(1)} %reshape.46.ids_ref, ...), custom_call_target="tpu_custom_call" | custom-call | flops 270000000 | bytes 4700000 | tf_op jit(solution)/shard_map/logits/pallas_call | solution.py:267
  74.2 15.3 %all_to_all.21.stats_ref = f32[16,1,128]{2,1,0:T(1,128)S(1)} all-to-all(f32[16,1,128]{2,1,0:T(1,128)S(1)} %logits.1), channel_id=1, replica_groups=mesh['heads_0'=8,'heads_1'=2,'z'=8,'x_pair'=2,'x_side'=2] {'x_pair','z'}, dimensions={0} | all-to-all | bytes 16384 | tf_op jit(solution)/shard_map/all_to_all | solution.py:24
  89.5 0.2 group.1
  89.7 13.2 %all_to_all.22.stats_ref = f32[16,1,128]{2,1,0:T(1,128)S(1)} all-to-all(f32[16,1,128]{2,1,0:T(1,128)S(1)} %group.1), channel_id=1, replica_groups=mesh['heads_0'=8,'heads_1'=2,'z'=8,'x_pair'=2,'x_side'=2] {'heads_0','he..., dimensions={0} | all-to-all | bytes 16384 | tf_op jit(solution)/shard_map/all_to_all | solution.py:24
  102.9 0.7 final.1
  (2 shorter events, 0.0 us)
Async XLA Ops:
  0.6 16.9 %copy-start = (bf16[4096,128]{1,0:T(8,128)(2,1)S(1)}, bf16[4096,128]{1,0:T(8,128)(2,1)}, u32[]{:S(2)}) copy-start(bf16[4096,128]{1,0:T(8,128)(2,1)} %refs_0_.3) | copy-start | bytes 3145732
  0.6 30.3 %copy-start.2 = (f32[4096]{0:T(1024)S(1)}, f32[4096]{0:T(1024)}, u32[]{:S(2)}) copy-start(f32[4096]{0:T(1024)} %param.27) | copy-start | bytes 49156
  0.7 30.3 %copy-start.1 = (f32[4096]{0:T(1024)S(1)}, f32[4096]{0:T(1024)}, u32[]{:S(2)}) copy-start(f32[4096]{0:T(1024)} %param.26) | copy-start | bytes 49156
  0.7 22.3 %collective-permute-start.2 = (bf16[4096,128]{1,0:T(8,128)(2,1)}, bf16[4096,128]{1,0:T(8,128)(2,1)S(1)}, u32[]{:S(2)}, u32[]{:S(2)}) collective-permute-start(bf16[4096,128]{1,0:T(8,128)(2,1)} %refs_0_.3), channel_id=1, source_target_pairs={{0,1},{1,0},{2,3},{3,2},{4,5},{5,4},{6,7},{7,6},{8,9},{9,8},{10,11... | collective-permute-start | bytes 3145736 | tf_op jit(solution)/shard_map/ppermute | solution.py:380
  4.8 61.0 %copy-start.3 = (s32[256]{0:T(256)S(1)}, s32[256]{0:T(256)}, u32[]{:S(2)}) copy-start(s32[256]{0:T(256)} %param.29) | copy-start | bytes 3076
  9.3 21.6 %all-to-all-start = ((f32[16,32,128]{2,1,0:T(8,128)}), f32[16,32,128]{2,1,0:T(8,128)S(1)}, u32[]{:S(2)}, u32[]{:S(2)}) async-start(f32[16,32,128]{2,1,0:T(8,128)} %heads.1), calls=%async_computation | async-start | bytes 524288 | tf_op jit(solution)/shard_map/all_to_all | solution.py:24
  17.5 48.7 %collective-permute-start.1 = (bf16[4096,128]{1,0:T(8,128)(2,1)S(1)}, bf16[4096,128]{1,0:T(8,128)(2,1)S(1)}, u32[]{:S(2)}, u32[]{:S(2)}) collective-permute-start(bf16[4096,128]{1,0:T(8,128)(2,1)S(1)} %copy-done), channel_id=1, source_target_pairs={{0,32},{32,0},{1,33},{33,1},{2,34},{34,2},{3,35},{35,3},{4,36},{36... | collective-permute-start | bytes 3145736 | tf_op jit(solution)/shard_map/ppermute | solution.py:381
  23.0 47.2 %collective-permute-start.3 = (bf16[4096,128]{1,0:T(8,128)(2,1)S(1)}, bf16[4096,128]{1,0:T(8,128)(2,1)}, u32[]{:S(2)}, u32[]{:S(2)}) collective-permute-start(bf16[4096,128]{1,0:T(8,128)(2,1)S(1)} %collective-permute-done.2.refs_2_), channel_id=1, source_target_pairs={{0,32},{32,0},{1,33},{33,1},{2,34},{34,2},{3,35},{35,3},{4,36},{36... | collective-permute-start | bytes 3145736 | tf_op jit(solution)/shard_map/ppermute | solution.py:382
  61.1 9.1 %collective-permute-start = (bf16[64,16,128]{2,1,0:T(8,128)(2,1)S(1)}, bf16[64,16,128]{2,1,0:T(8,128)(2,1)}, u32[]{:S(2)}, u32[]{:S(2)}) collective-permute-start(bf16[64,16,128]{2,1,0:T(8,128)(2,1)S(1)} %all_to_all.20.near_ref), channel_id=1, source_target_pairs={{0,2},{2,0},{1,3},{3,1},{4,6},{6,4},{5,7},{7,5},{8,10},{10,8},{9,1... | collective-permute-start | bytes 786440 | tf_op jit(solution)/shard_map/ppermute | solution.py:406

commit v9 on v8

--- a/solution.py
+++ b/solution.py
@@ -47,18 +47,19 @@
     return jnp.sum(jnp.where(here, jnp.broadcast_to(line, shape), 0.0), axis=1, keepdims=True)
 
 
-def heads_kernel(
-    first_ref,
-    rate_ref,
-    *refs,
-):
-    inputs, out_ref, local, sems = refs[:10], refs[10], refs[11:21], refs[21]
-    q_ref, k_ref, v_ref, g_ref, dl_ref, bl_ref, gain_ref, res_ref, state_ref, proj_ref = local
-    copies = [pltpu.make_async_copy(inputs[n], local[n], sems.at[n]) for n in range(8)]
+def heads_kernel(*refs):
+    small = 9
+    inputs, out_ref, local = refs[:11], refs[11], refs[12:23]
+    done_ref, sems, out_sems = refs[23:]
+    q_ref, k_ref, v_ref, g_ref, dl_ref, bl_ref, gain_ref, rate_ref, res_ref = local[:small]
+    state_ref, proj_ref = local[small:]
+    copies = [pltpu.make_async_copy(inputs[n], local[n], sems.at[n]) for n in range(small)]
     heads = state_ref.shape[1]
     for h in range(heads):
         copies.append(
-            pltpu.make_async_copy(inputs[8].at[:, h], state_ref.at[:, h], sems.at[8 + h])
+            pltpu.make_async_copy(
+                inputs[small].at[:, h], state_ref.at[:, h], sems.at[small + h]
+            )
         )
     blocks = 4
     wide = proj_ref.shape[1] // blocks
@@ -66,12 +67,12 @@
         part = pl.ds(n * wide, wide)
         copies.append(
             pltpu.make_async_copy(
-                inputs[9].at[:, part], proj_ref.at[:, part], sems.at[8 + heads + n]
+                inputs[small + 1].at[:, part], proj_ref.at[:, part], sems.at[small + heads + n]
             )
         )
     for copy in copies:
         copy.start()
-    for copy in copies[:8]:
+    for copy in copies[:small]:
         copy.wait()
     rows = q_ref.shape[0]
     size = state_ref.shape[2]
@@ -90,12 +91,12 @@
         lanes = slice(h * size, (h + 1) * size)
         logit = dl_ref[h : h + 1, :]
         soft = jnp.maximum(logit, 0.0) + jnp.log1p(jnp.exp(-jnp.abs(logit)))
-        decay = as_column(jnp.exp(-rate_ref[h] * soft))
+        decay = as_column(jnp.exp(-rate_ref[:, h : h + 1] * soft))
         strength = as_column(1.0 / (1.0 + jnp.exp(-bl_ref[h : h + 1, :])))
         inter = jnp.sum(queries[h] * keys[h], axis=1, keepdims=True)
         value = v_ref[:, lanes].astype(jnp.float32)
         gate = g_ref[:, lanes].astype(jnp.float32)
-        copies[8 + h].wait()
+        copies[small + h].wait()
         by_query, by_key = [], []
         for b in range(rows):
             block = state_ref[b, h]
@@ -111,11 +112,13 @@
         normed = output / jnp.sqrt(mean + epsilon)
         parts.append(normed * gain * (gate / (1.0 + jnp.exp(-gate))))
     headout = jnp.concatenate(parts, axis=1).astype(jnp.bfloat16)
-    first = first_ref[0]
+    chip, core = lax.axis_index("heads_0"), lax.axis_index("heads_1")
+    first = jnp.where((chip == 0) & (core == 0), 1.0, 0.0)
+    finished = []
     lines = wide // 128
     cores, halves = 2, out_ref.shape[0] // rows
     for n in range(blocks):
-        copies[8 + heads + n].wait()
+        copies[small + heads + n].wait()
         part = slice(n * wide, (n + 1) * wide)
         total = jnp.dot(headout, proj_ref[:, part], preferred_element_type=jnp.float32)
         total = total + res_ref[:, part].astype(jnp.float32) * first
@@ -124,7 +127,14 @@
             for half in range(halves):
                 core, r = row // (rows // cores), row % (rows // cores)
                 place = (r * halves + half) * cores + core
-                out_ref[place, n * lines : (n + 1) * lines, :] = total[row]
+                done_ref[place, n * lines : (n + 1) * lines, :] = total[row]
+        part = pl.ds(n * lines, lines)
+        finished.append(
+            pltpu.make_async_copy(done_ref.at[:, part], out_ref.at[:, part], out_sems.at[n])
+        )
+        finished[-1].start()
+    for copy in finished:
+        copy.wait()
 
 
 def head_partials(
@@ -139,7 +149,6 @@
     norm_gain,
     out_proj,
     residual,
-    first,
     places,
 ):
     arrays = (
@@ -150,6 +159,7 @@
         decay_logit.T,
         beta_logit.T,
         norm_gain.reshape(1, -1),
+        decay_rate.reshape(1, -1),
         residual,
         state,
         out_proj,
@@ -157,14 +167,18 @@
     width = out_proj.shape[1]
     return pl.pallas_call(
         heads_kernel,
-        out_shape=pltpu.VMEM((places, width // 128, 128), jnp.float32),
-        in_specs=[smem_spec(), smem_spec()] + [any_spec() for _ in arrays],
-        out_specs=vmem_spec(),
+        out_shape=jax.ShapeDtypeStruct((places, width // 128, 128), jnp.float32),
+        in_specs=[any_spec() for _ in arrays],
+        out_specs=any_spec(),
         scratch_shapes=[pltpu.VMEM(a.shape, a.dtype) for a in arrays]
-        + [pltpu.SemaphoreType.DMA((8 + state.shape[1] + 4,))],
+        + [
+            pltpu.VMEM((places, width // 128, 128), jnp.float32),
+            pltpu.SemaphoreType.DMA((9 + state.shape[1] + 4,)),
+            pltpu.SemaphoreType.DMA((4,)),
+        ],
         cost_estimate=pl.CostEstimate(flops=40000000, bytes_accessed=3500000, transcendentals=0),
         name="heads",
-    )(first, decay_rate, *arrays)
+    )(*arrays)
 
 
 def norm_kernel(half_ref, arrived_ref, gain_ref, weight_ref, piece_ref, value_ref, scratch):
@@ -201,13 +215,26 @@
     )(half, arrived, gain, weight)
 
 
-def logits_kernel(groups, firsts_ref, pair_ref, near_ref, far_ref, ids_ref, *refs):
+def logits_kernel(groups, near_ref, far_ref, ids_ref, *refs):
     count = 4
-    matrices, out_ref, local, flat, sems = refs[:count], *refs[count:]
-    size, (_, tiles, lanes) = near_ref.shape[0] * near_ref.shape[1], near_ref.shape
+    matrices, out_ref, local, rows, flat, sems = refs[:count], *refs[count:]
+    tiles, lanes = near_ref.shape[1:]
     pieces = flat.shape[0] // (groups * tiles)
     deep = tiles * lanes
     halves = local.shape[1] // deep
+    pair, core, side = (lax.axis_index(a) for a in ("x_pair", "heads_1", "x_side"))
+    flat_place = 0
+    for axis in HEADS_BATCH:
+        flat_place = flat_place * lax.axis_size(axis) + lax.axis_index(axis)
+    across = (1 - 2 * core) * lax.axis_size(BATCH)
+    along = 1 - 2 * side
+    firsts = [(flat_place + step) * lanes for step in (0, across, along, across + along)]
+    moved = [
+        pltpu.make_async_copy(near_ref, rows.at[pair], sems.at[halves * count]),
+        pltpu.make_async_copy(far_ref, rows.at[1 - pair], sems.at[halves * count + 1]),
+    ]
+    for copy in moved:
+        copy.start()
     copies = []
     for k in range(halves):
         part = pl.ds(k * deep, deep)
@@ -220,9 +247,9 @@
             )
     for copy in copies:
         copy.start()
-    for start, ref in ((pair_ref[0] * size, near_ref), ((1 - pair_ref[0]) * size, far_ref)):
-        part = pl.ds(pl.multiple_of(start, size), size)
-        flat[part, :] = ref[...].reshape(size, lanes).astype(jnp.float32)
+    for copy in moved:
+        copy.wait()
+    flat[...] = rows[...].reshape(flat.shape).astype(jnp.float32)
 
     def rows_of(piece):
         first, step = piece * tiles, pieces * tiles
@@ -247,7 +274,7 @@
     chosen = jnp.zeros(sums[0].shape, jnp.float32)
     for n in range(count):
         total = total + jnp.exp(sums[n] - top)
-        columns = lax.broadcasted_iota(jnp.int32, sums[n].shape, 1) + firsts_ref[n]
+        columns = lax.broadcasted_iota(jnp.int32, sums[n].shape, 1) + firsts[n]
         chosen = chosen + jnp.where(columns == ids, sums[n], 0.0)
     total = jnp.sum(total, axis=1, keepdims=True)
     chosen = jnp.sum(chosen, axis=1, keepdims=True)
@@ -262,23 +289,23 @@
         out_ref[g] = packed[g : g + 1]
 
 
-def logit_stats(near_rows, far_rows, pair, matrices, firsts, ids, groups):
+def logit_stats(near_rows, far_rows, matrices, ids, groups):
     depth = matrices[0].shape[0]
     return pl.pallas_call(
         functools.partial(logits_kernel, groups),
         out_shape=pltpu.VMEM((groups, 1, 128), jnp.float32),
-        in_specs=[smem_spec(), smem_spec(), vmem_spec(), vmem_spec(), vmem_spec()]
-        + [any_spec() for _ in matrices],
+        in_specs=[any_spec(), any_spec(), vmem_spec()] + [any_spec() for _ in matrices],
         out_specs=vmem_spec(),
         scratch_shapes=[
             pltpu.VMEM((len(matrices), depth, 128), jnp.bfloat16),
+            pltpu.VMEM((2, *near_rows.shape), near_rows.dtype),
             pltpu.VMEM((2 * near_rows.size // 128, 128), jnp.float32),
-            pltpu.SemaphoreType.DMA((2 * len(matrices),)),
+            pltpu.SemaphoreType.DMA((2 * len(matrices) + 2,)),
         ],
         cost_estimate=pl.CostEstimate(flops=270000000, bytes_accessed=4700000, transcendentals=0),
         compiler_params=room(12),
         name="logits",
-    )(firsts, pair, near_rows, far_rows, ids, *matrices)
+    )(near_rows, far_rows, ids, *matrices)
 
 
 def shifted(lines, places):
@@ -380,7 +407,6 @@
     x_head = lax.ppermute(lm_head, "x_side", SWAP)
     core_head = lax.ppermute(lm_head, "heads_1", SWAP)
     both_head = lax.ppermute(x_head, "heads_1", SWAP)
-    first = jnp.where((chip == 0) & (core == 0), 1.0, 0.0).reshape(1)
     partial_out = head_partials(
         queries,
         keys_new,
@@ -393,7 +419,6 @@
         norm_gain,
         out_proj,
         residual,
-        first,
         chips * cores,
     )
     arrived = exchange(partial_out, HEADS)
@@ -405,18 +430,12 @@
     near_rows = exchange(pieces, NEAR)
     far_rows = lax.ppermute(near_rows, "x_pair", SWAP)
 
-    vocab_own = lm_head.shape[1]
-    flat = lax.axis_index(HEADS_BATCH)
-    across = (1 - 2 * core) * lax.axis_size(BATCH)
-    along = 1 - 2 * side
     matrices = (lm_head, core_head, x_head, both_head)
-    firsts = jnp.stack([flat, flat + across, flat + along, flat + across + along]) * vocab_own
-    pair = lax.axis_index("x_pair").astype(jnp.int32).reshape(1)
     ids = sampled.reshape(lax.axis_size("z"), lax.axis_size("x_pair"), -1, cores, rows_core)
     ids = lax.dynamic_index_in_dim(ids, side, 2, keepdims=False)
     ids = lax.dynamic_index_in_dim(ids, core, 2, keepdims=False)
     ids = ids.transpose(2, 1, 0).reshape(-1, 1)
-    stats = logit_stats(near_rows, far_rows, pair, matrices, firsts.astype(jnp.int32), ids, groups)
+    stats = logit_stats(near_rows, far_rows, matrices, ids, groups)
     stats = group_stats(exchange(stats, GROUP), value, rows_core, chips * cores)
     logprob, values = final_values(exchange(stats, HEADS), rows_core, cores)
     return (logprob.reshape(-1), values.reshape(-1))

time: 104 us -> 103 us (level)
  Pallas kernels: 9.5 us -> 8.15 us
  transfers between devices with their start and end apart: 5 -> 5, of which waited for: 2 -> 2; matrix products, arithmetic and copies ran while one was open for 0% -> 0% of each run, Pallas kernels for 5% -> 4%
where the time goes in v9:
time: 103 us
  blocking collectives  58.5 us (57%)
  starting transfers between devices  26.9 us (26%)
  waiting for transfers between devices  8.3 us (8%)
  Pallas kernels  8.15 us (8%)
    all_to_all x3, blocking collectives, exchange(): return lax.all_to_all(parts, axis, split_axis=0, concat_axis=0, tiled=True)  58.5 us
    all_to_all x1, starting transfers between devices, exchange(): return lax.all_to_all(parts, axis, split_axis=0, concat_axis=0, tiled=True)  8.15 us
    ppermute x1, starting transfers between devices, per_device(): both_head = lax.ppermute(x_head, 'heads_1', SWAP)  7.94 us
    ppermute x1, starting transfers between devices, per_device(): far_rows = lax.ppermute(near_rows, 'x_pair', SWAP)  4.64 us
    ppermute x1, waiting for transfers between devices, per_device(): x_head = lax.ppermute(lm_head, 'x_side', SWAP)  4.17 us
    ppermute x1, waiting for transfers between devices, per_device(): far_rows = lax.ppermute(near_rows, 'x_pair', SWAP)  4.12 us
    ppermute x1, starting transfers between devices, per_device(): x_head = lax.ppermute(lm_head, 'x_side', SWAP)  4.07 us
    pallas_call x1, Pallas kernels, head_partials(): pl.pallas_call(heads_kernel, out_shape=jax.ShapeDtypeStruct((places, widt...  3.79 us
  transfers between devices with their start and end apart: 5, of which 2 were waited for; matrix products, arithmetic and copies ran while one was open for 0% of the time, Pallas kernels for 4%

profile of v9, /device:TPU:1, one launch (start us, length us, event | category | flops | bytes accessed | tf_op | source)
XLA Modules:
  0.0 103.0 jit_solution(9451865177483029385)
XLA Ops:
  0.6 0.0 copy-start
  0.6 0.0 copy-start.2
  0.7 0.0 copy-start.1
  0.7 4.1 %collective-permute-start.2 = (bf16[4096,128]{1,0:T(8,128)(2,1)}, bf16[4096,128]{1,0:T(8,128)(2,1)S(1)}, u32[]{:S(2)}, u32[]{:S(2)}) collective-permute-start(bf16[4096,128]{1,0:T(8,128)(2,1)} %refs_0_.3), channel_id=1, source_target_pairs={{0,1},{1,0},{2,3},{3,2},{4,5},{5,4},{6,7},{7,6},{8,9},{9,8},{10,11... | collective-permute-start | bytes 3145736 | tf_op jit(solution)/shard_map/ppermute | solution.py:407
  4.7 0.0 copy-start.3
  4.8 3.8 %heads.1 = f32[16,32,128]{2,1,0:T(8,128)} custom-call(bf16[8,256]{1,0:T(8,128)(2,1)} %refs_0_.2, bf16[8,256]{1,0:T(8,128)(2,1)} %refs_1_.1, bf16[8,256]{1,0:T(8,128)(2,1)} %refs_2_.1, bf16[8,256]{1,0:T(8,128)(2,1)} %refs_3_.1, f32[2,8]{1,0:T(2,128)} %bitcast.15, f32[2,8]{1,0:T(2,128)} %bitcast.16, f32[1,128]{1,0:T(1,128)} %bitcast.17, f32[1,2]{1,0:T(1,128)} %bitcast.18, ...), custom_call_target="tpu_custom_call" | custom-call | flops 40000000 | bytes 3500000 | tf_op jit(solution)/shard_map/heads/pallas_call | solution.py:168
  8.5 8.2 %all-to-all-start = ((f32[16,32,128]{2,1,0:T(8,128)}), f32[16,32,128]{2,1,0:T(8,128)S(1)}, u32[]{:S(2)}, u32[]{:S(2)}) async-start(f32[16,32,128]{2,1,0:T(8,128)} %heads.1), calls=%async_computation | async-start | bytes 524288 | tf_op jit(solution)/shard_map/all_to_all | solution.py:24
  16.7 0.0 copy-done
  16.7 2.1 %collective-permute-start.1 = (bf16[4096,128]{1,0:T(8,128)(2,1)S(1)}, bf16[4096,128]{1,0:T(8,128)(2,1)S(1)}, u32[]{:S(2)}, u32[]{:S(2)}) collective-permute-start(bf16[4096,128]{1,0:T(8,128)(2,1)S(1)} %copy-done), channel_id=1, source_target_pairs={{0,32},{32,0},{1,33},{33,1},{2,34},{34,2},{3,35},{35,3},{4,36},{36... | collective-permute-start | bytes 3145736 | tf_op jit(solution)/shard_map/ppermute | solution.py:408
  18.8 4.2 %collective-permute-done.2.refs_2_ = bf16[4096,128]{1,0:T(8,128)(2,1)S(1)} collective-permute-done((bf16[4096,128]{1,0:T(8,128)(2,1)}, bf16[4096,128]{1,0:T(8,128)(2,1)S(1)}, u32[]{:S(2)}, u32[]{:S(2)}) %collective-permute-start.2) | collective-permute-done | bytes 1048608 | tf_op jit(solution)/shard_map/ppermute | solution.py:407
  23.0 7.9 %collective-permute-start.3 = (bf16[4096,128]{1,0:T(8,128)(2,1)S(1)}, bf16[4096,128]{1,0:T(8,128)(2,1)}, u32[]{:S(2)}, u32[]{:S(2)}) collective-permute-start(bf16[4096,128]{1,0:T(8,128)(2,1)S(1)} %collective-permute-done.2.refs_2_), channel_id=1, source_target_pairs={{0,32},{32,0},{1,33},{33,1},{2,34},{34,2},{3,35},{35,3},{4,36},{36... | collective-permute-start | bytes 3145736 | tf_op jit(solution)/shard_map/ppermute | solution.py:409
  31.0 0.0 all-to-all-done.arrived_ref
  31.0 0.0 copy-done.2
  31.0 0.0 copy-done.1
  31.0 0.2 norm.1
  31.2 29.9 %all_to_all.20.near_ref = bf16[64,16,128]{2,1,0:T(8,128)(2,1)S(1)} all-to-all(bf16[64,16,128]{2,1,0:T(8,128)(2,1)S(1)} %get-tuple-element.6), channel_id=1, replica_groups=mesh['heads_0'=8,'heads_1'=2,'z'=8,'x_pair'=2,'x_side'=2] {'z','heads_0'}, dimensions={0} | all-to-all | bytes 524288 | tf_op jit(solution)/shard_map/all_to_all | solution.py:24
  61.1 4.6 %collective-permute-start = (bf16[64,16,128]{2,1,0:T(8,128)(2,1)S(1)}, bf16[64,16,128]{2,1,0:T(8,128)(2,1)}, u32[]{:S(2)}, u32[]{:S(2)}) collective-permute-start(bf16[64,16,128]{2,1,0:T(8,128)(2,1)S(1)} %all_to_all.20.near_ref), channel_id=1, source_target_pairs={{0,2},{2,0},{1,3},{3,1},{4,6},{6,4},{5,7},{7,5},{8,10},{10,8},{9,1... | collective-permute-start | bytes 786440 | tf_op jit(solution)/shard_map/ppermute | solution.py:431
  65.8 0.0 copy-done.3
  65.8 0.1 reshape.38
  65.9 0.1 copy.19
  66.0 0.1 reshape.42.ids_ref
  66.1 0.0 collective-permute-done.1.refs_1_
  66.1 4.1 %collective-permute-done.far_ref = bf16[64,16,128]{2,1,0:T(8,128)(2,1)} collective-permute-done((bf16[64,16,128]{2,1,0:T(8,128)(2,1)S(1)}, bf16[64,16,128]{2,1,0:T(8,128)(2,1)}, u32[]{:S(2)}, u32[]{:S(2)}) %collective-permute-start) | collective-permute-done | bytes 262176 | tf_op jit(solution)/shard_map/ppermute | solution.py:431
  70.2 0.0 collective-permute-done.3.refs_3_
  70.2 3.4 %logits.1 = f32[16,1,128]{2,1,0:T(1,128)S(1)} custom-call(bf16[64,16,128]{2,1,0:T(8,128)(2,1)S(1)} %all_to_all.20.near_ref, bf16[64,16,128]{2,1,0:T(8,128)(2,1)} %collective-permute-done.far_ref, s32[64,1]{1,0:T(8,128)S(1)} %reshape.42.ids_ref, bf16[4096,128]{1,0:T(8,128)(2,1)S(1)} %copy-done, bf16[4096,128]{1,0:T(8,128)(2,1)S(1)} %collective-permute-done.1.refs_1_, ...), custom_call_target="tpu_custom_call" | custom-call | flops 270000000 | bytes 4700000 | tf_op jit(solution)/shard_map/logits/pallas_call | solution.py:294
  73.6 15.3 %all_to_all.21.stats_ref = f32[16,1,128]{2,1,0:T(1,128)S(1)} all-to-all(f32[16,1,128]{2,1,0:T(1,128)S(1)} %logits.1), channel_id=1, replica_groups=mesh['heads_0'=8,'heads_1'=2,'z'=8,'x_pair'=2,'x_side'=2] {'x_pair','z'}, dimensions={0} | all-to-all | bytes 16384 | tf_op jit(solution)/shard_map/all_to_all | solution.py:24
  88.9 0.2 group.1
  89.1 13.2 %all_to_all.22.stats_ref = f32[16,1,128]{2,1,0:T(1,128)S(1)} all-to-all(f32[16,1,128]{2,1,0:T(1,128)S(1)} %group.1), channel_id=1, replica_groups=mesh['heads_0'=8,'heads_1'=2,'z'=8,'x_pair'=2,'x_side'=2] {'heads_0','he..., dimensions={0} | all-to-all | bytes 16384 | tf_op jit(solution)/shard_map/all_to_all | solution.py:24
  102.3 0.7 final.1
  (2 shorter events, 0.0 us)
Async XLA Ops:
  0.6 16.1 %copy-start = (bf16[4096,128]{1,0:T(8,128)(2,1)S(1)}, bf16[4096,128]{1,0:T(8,128)(2,1)}, u32[]{:S(2)}) copy-start(bf16[4096,128]{1,0:T(8,128)(2,1)} %refs_0_.3) | copy-start | bytes 3145732
  0.6 30.3 %copy-start.2 = (f32[4096]{0:T(1024)S(1)}, f32[4096]{0:T(1024)}, u32[]{:S(2)}) copy-start(f32[4096]{0:T(1024)} %param.27) | copy-start | bytes 49156
  0.7 30.3 %copy-start.1 = (f32[4096]{0:T(1024)S(1)}, f32[4096]{0:T(1024)}, u32[]{:S(2)}) copy-start(f32[4096]{0:T(1024)} %param.26) | copy-start | bytes 49156
  0.7 22.3 %collective-permute-start.2 = (bf16[4096,128]{1,0:T(8,128)(2,1)}, bf16[4096,128]{1,0:T(8,128)(2,1)S(1)}, u32[]{:S(2)}, u32[]{:S(2)}) collective-permute-start(bf16[4096,128]{1,0:T(8,128)(2,1)} %refs_0_.3), channel_id=1, source_target_pairs={{0,1},{1,0},{2,3},{3,2},{4,5},{5,4},{6,7},{7,6},{8,9},{9,8},{10,11... | collective-permute-start | bytes 3145736 | tf_op jit(solution)/shard_map/ppermute | solution.py:407
  4.7 61.0 %copy-start.3 = (s32[256]{0:T(256)S(1)}, s32[256]{0:T(256)}, u32[]{:S(2)}) copy-start(s32[256]{0:T(256)} %param.29) | copy-start | bytes 3076
  8.5 22.4 %all-to-all-start = ((f32[16,32,128]{2,1,0:T(8,128)}), f32[16,32,128]{2,1,0:T(8,128)S(1)}, u32[]{:S(2)}, u32[]{:S(2)}) async-start(f32[16,32,128]{2,1,0:T(8,128)} %heads.1), calls=%async_computation | async-start | bytes 524288 | tf_op jit(solution)/shard_map/all_to_all | solution.py:24
  16.7 49.4 %collective-permute-start.1 = (bf16[4096,128]{1,0:T(8,128)(2,1)S(1)}, bf16[4096,128]{1,0:T(8,128)(2,1)S(1)}, u32[]{:S(2)}, u32[]{:S(2)}) collective-permute-start(bf16[4096,128]{1,0:T(8,128)(2,1)S(1)} %copy-done), channel_id=1, source_target_pairs={{0,32},{32,0},{1,33},{33,1},{2,34},{34,2},{3,35},{35,3},{4,36},{36... | collective-permute-start | bytes 3145736 | tf_op jit(solution)/shard_map/ppermute | solution.py:408
  23.0 47.2 %collective-permute-start.3 = (bf16[4096,128]{1,0:T(8,128)(2,1)S(1)}, bf16[4096,128]{1,0:T(8,128)(2,1)}, u32[]{:S(2)}, u32[]{:S(2)}) collective-permute-start(bf16[4096,128]{1,0:T(8,128)(2,1)S(1)} %collective-permute-done.2.refs_2_), channel_id=1, source_target_pairs={{0,32},{32,0},{1,33},{33,1},{2,34},{34,2},{3,35},{35,3},{4,36},{36... | collective-permute-start | bytes 3145736 | tf_op jit(solution)/shard_map/ppermute | solution.py:409
  61.1 9.1 %collective-permute-start = (bf16[64,16,128]{2,1,0:T(8,128)(2,1)S(1)}, bf16[64,16,128]{2,1,0:T(8,128)(2,1)}, u32[]{:S(2)}, u32[]{:S(2)}) collective-permute-start(bf16[64,16,128]{2,1,0:T(8,128)(2,1)S(1)} %all_to_all.20.near_ref), channel_id=1, source_target_pairs={{0,2},{2,0},{1,3},{3,1},{4,6},{6,4},{5,7},{7,5},{8,10},{10,8},{9,1... | collective-permute-start | bytes 786440 | tf_op jit(solution)/shard_map/ppermute | solution.py:431

commit v10 on v9

--- a/solution.py
+++ b/solution.py
@@ -10,10 +10,10 @@
 
 
 HEADS = ("heads_0", "heads_1")
-BATCH = ("z", "x_pair", "x_side")
+BATCH = ("z", "x_side", "x_pair")
 GROUP = ("x_pair", "z")
 NEAR = ("z", "heads_0")
-HEADS_BATCH = ("heads_0", "heads_1", "z", "x_pair", "x_side")
+HEADS_BATCH = ("heads_0", "heads_1", "z", "x_side", "x_pair")
 SWAP = [(0, 1), (1, 0)]
 
 
@@ -227,7 +227,7 @@
     for axis in HEADS_BATCH:
         flat_place = flat_place * lax.axis_size(axis) + lax.axis_index(axis)
     across = (1 - 2 * core) * lax.axis_size(BATCH)
-    along = 1 - 2 * side
+    along = (1 - 2 * side) * lax.axis_size("x_pair")
     firsts = [(flat_place + step) * lanes for step in (0, across, along, across + along)]
     moved = [
         pltpu.make_async_copy(near_ref, rows.at[pair], sems.at[halves * count]),
@@ -431,8 +431,8 @@
     far_rows = lax.ppermute(near_rows, "x_pair", SWAP)
 
     matrices = (lm_head, core_head, x_head, both_head)
-    ids = sampled.reshape(lax.axis_size("z"), lax.axis_size("x_pair"), -1, cores, rows_core)
-    ids = lax.dynamic_index_in_dim(ids, side, 2, keepdims=False)
+    ids = sampled.reshape(lax.axis_size("z"), lax.axis_size("x_side"), -1, cores, rows_core)
+    ids = lax.dynamic_index_in_dim(ids, side, 1, keepdims=False)
     ids = lax.dynamic_index_in_dim(ids, core, 2, keepdims=False)
     ids = ids.transpose(2, 1, 0).reshape(-1, 1)
     stats = logit_stats(near_rows, far_rows, matrices, ids, groups)
@@ -443,7 +443,7 @@
 
 def solution(mesh):
     torus = Mesh(
-        mesh.devices.reshape(8, 2, 8, 2, 2), ("heads_0", "heads_1", "z", "x_pair", "x_side")
+        mesh.devices.reshape(8, 2, 8, 2, 2), ("heads_0", "heads_1", "z", "x_side", "x_pair")
     )
     return jax.shard_map(
         per_device,

time: 103 us -> 100 us (0.971)
  blocking collectives: 58.5 us -> 55.4 us
  starting transfers between devices: 26.9 us -> 25.2 us
  waiting for transfers between devices: 8.3 us -> 10 us
    all_to_all x3, blocking collectives: 58.5 us -> 55.4 us  [exchange(): return lax.all_to_all(parts, axis, split_axis=0, concat_axis=0, tiled=True)]
    ppermute x1, waiting for transfers between devices: 4.17 us -> 5.89 us  [per_device(): x_head = lax.ppermute(lm_head, 'x_side', SWAP)]
    ppermute x1, starting transfers between devices: 4.07 us -> 5.6 us  [per_device(): x_head = lax.ppermute(lm_head, 'x_side', SWAP)]
    ppermute x1, starting transfers between devices: 4.64 us -> 3.11 us  [per_device(): far_rows = lax.ppermute(near_rows, 'x_pair', SWAP)]
    ppermute x1, starting transfers between devices: 7.94 us -> 6.41 us  [per_device(): both_head = lax.ppermute(x_head, 'heads_1', SWAP)]
where the time goes in v10:
time: 100 us
  blocking collectives  55.4 us (55%)
  starting transfers between devices  25.2 us (25%)
  waiting for transfers between devices  10 us (10%)
  Pallas kernels  8.15 us (8%)
    all_to_all x3, blocking collectives, exchange(): return lax.all_to_all(parts, axis, split_axis=0, concat_axis=0, tiled=True)  55.4 us
    all_to_all x1, starting transfers between devices, exchange(): return lax.all_to_all(parts, axis, split_axis=0, concat_axis=0, tiled=True)  8.08 us
    ppermute x1, starting transfers between devices, per_device(): both_head = lax.ppermute(x_head, 'heads_1', SWAP)  6.41 us
    ppermute x1, waiting for transfers between devices, per_device(): x_head = lax.ppermute(lm_head, 'x_side', SWAP)  5.89 us
    ppermute x1, starting transfers between devices, per_device(): x_head = lax.ppermute(lm_head, 'x_side', SWAP)  5.6 us
    ppermute x1, waiting for transfers between devices, per_device(): far_rows = lax.ppermute(near_rows, 'x_pair', SWAP)  4.15 us
    pallas_call x1, Pallas kernels, head_partials(): pl.pallas_call(heads_kernel, out_shape=jax.ShapeDtypeStruct((places, widt...  3.79 us
    pallas_call x1, Pallas kernels, logit_stats(): pl.pallas_call(functools.partial(logits_kernel, groups), out_shape=pltpu....  3.35 us
  transfers between devices with their start and end apart: 5, of which 2 were waited for; matrix products, arithmetic and copies ran while one was open for 0% of the time, Pallas kernels for 4%

profile of v10, /device:TPU:1, one launch (start us, length us, event | category | flops | bytes accessed | tf_op | source)
XLA Modules:
  0.0 100.0 jit_solution(164254451388773502)
XLA Ops:
  0.6 0.0 copy-start
  0.6 0.0 copy-start.2
  0.7 0.0 copy-start.1
  0.7 5.6 %collective-permute-start.2 = (bf16[4096,128]{1,0:T(8,128)(2,1)}, bf16[4096,128]{1,0:T(8,128)(2,1)S(1)}, u32[]{:S(2)}, u32[]{:S(2)}) collective-permute-start(bf16[4096,128]{1,0:T(8,128)(2,1)} %refs_0_.3), channel_id=1, source_target_pairs={{0,2},{2,0},{1,3},{3,1},{4,6},{6,4},{5,7},{7,5},{8,10},{10,8},{9,1... | collective-permute-start | bytes 3145736 | tf_op jit(solution)/shard_map/ppermute | solution.py:407
  6.3 0.0 copy-start.3
  6.3 3.8 %heads.1 = f32[16,32,128]{2,1,0:T(8,128)} custom-call(bf16[8,256]{1,0:T(8,128)(2,1)} %refs_0_.2, bf16[8,256]{1,0:T(8,128)(2,1)} %refs_1_.1, bf16[8,256]{1,0:T(8,128)(2,1)} %refs_2_.1, bf16[8,256]{1,0:T(8,128)(2,1)} %refs_3_.1, f32[2,8]{1,0:T(2,128)} %bitcast.15, f32[2,8]{1,0:T(2,128)} %bitcast.16, f32[1,128]{1,0:T(1,128)} %bitcast.17, f32[1,2]{1,0:T(1,128)} %bitcast.18, ...), custom_call_target="tpu_custom_call" | custom-call | flops 40000000 | bytes 3500000 | tf_op jit(solution)/shard_map/heads/pallas_call | solution.py:168
  10.1 8.1 %all-to-all-start = ((f32[16,32,128]{2,1,0:T(8,128)}), f32[16,32,128]{2,1,0:T(8,128)S(1)}, u32[]{:S(2)}, u32[]{:S(2)}) async-start(f32[16,32,128]{2,1,0:T(8,128)} %heads.1), calls=%async_computation | async-start | bytes 524288 | tf_op jit(solution)/shard_map/all_to_all | solution.py:24
  18.2 0.0 copy-done
  18.2 2.0 %collective-permute-start.1 = (bf16[4096,128]{1,0:T(8,128)(2,1)S(1)}, bf16[4096,128]{1,0:T(8,128)(2,1)S(1)}, u32[]{:S(2)}, u32[]{:S(2)}) collective-permute-start(bf16[4096,128]{1,0:T(8,128)(2,1)S(1)} %copy-done), channel_id=1, source_target_pairs={{0,32},{32,0},{1,33},{33,1},{2,34},{34,2},{3,35},{35,3},{4,36},{36... | collective-permute-start | bytes 3145736 | tf_op jit(solution)/shard_map/ppermute | solution.py:408
  20.2 5.9 %collective-permute-done.2.refs_2_ = bf16[4096,128]{1,0:T(8,128)(2,1)S(1)} collective-permute-done((bf16[4096,128]{1,0:T(8,128)(2,1)}, bf16[4096,128]{1,0:T(8,128)(2,1)S(1)}, u32[]{:S(2)}, u32[]{:S(2)}) %collective-permute-start.2) | collective-permute-done | bytes 1048608 | tf_op jit(solution)/shard_map/ppermute | solution.py:407
  26.1 6.4 %collective-permute-start.3 = (bf16[4096,128]{1,0:T(8,128)(2,1)S(1)}, bf16[4096,128]{1,0:T(8,128)(2,1)}, u32[]{:S(2)}, u32[]{:S(2)}) collective-permute-start(bf16[4096,128]{1,0:T(8,128)(2,1)S(1)} %collective-permute-done.2.refs_2_), channel_id=1, source_target_pairs={{0,32},{32,0},{1,33},{33,1},{2,34},{34,2},{3,35},{35,3},{4,36},{36... | collective-permute-start | bytes 3145736 | tf_op jit(solution)/shard_map/ppermute | solution.py:409
  32.5 0.0 all-to-all-done.arrived_ref
  32.5 0.0 copy-done.2
  32.5 0.0 copy-done.1
  32.5 0.2 norm.1
  32.7 29.9 %all_to_all.20.near_ref = bf16[64,16,128]{2,1,0:T(8,128)(2,1)S(1)} all-to-all(bf16[64,16,128]{2,1,0:T(8,128)(2,1)S(1)} %get-tuple-element.6), channel_id=1, replica_groups=mesh['heads_0'=8,'heads_1'=2,'z'=8,'x_side'=2,'x_pair'=2] {'z','heads_0'}, dimensions={0} | all-to-all | bytes 524288 | tf_op jit(solution)/shard_map/all_to_all | solution.py:24
  62.6 3.1 %collective-permute-start = (bf16[64,16,128]{2,1,0:T(8,128)(2,1)S(1)}, bf16[64,16,128]{2,1,0:T(8,128)(2,1)}, u32[]{:S(2)}, u32[]{:S(2)}) collective-permute-start(bf16[64,16,128]{2,1,0:T(8,128)(2,1)S(1)} %all_to_all.20.near_ref), channel_id=1, source_target_pairs={{0,1},{1,0},{2,3},{3,2},{4,5},{5,4},{6,7},{7,6},{8,9},{9,8},{10,11... | collective-permute-start | bytes 786440 | tf_op jit(solution)/shard_map/ppermute | solution.py:431
  65.7 0.0 copy-done.3
  65.8 0.1 reshape.38
  65.9 0.1 copy.19
  66.0 0.1 reshape.42.ids_ref
  66.1 0.0 collective-permute-done.1.refs_1_
  66.1 4.2 %collective-permute-done.far_ref = bf16[64,16,128]{2,1,0:T(8,128)(2,1)} collective-permute-done((bf16[64,16,128]{2,1,0:T(8,128)(2,1)S(1)}, bf16[64,16,128]{2,1,0:T(8,128)(2,1)}, u32[]{:S(2)}, u32[]{:S(2)}) %collective-permute-start) | collective-permute-done | bytes 262176 | tf_op jit(solution)/shard_map/ppermute | solution.py:431
  70.2 0.0 collective-permute-done.3.refs_3_
  70.2 3.4 %logits.1 = f32[16,1,128]{2,1,0:T(1,128)S(1)} custom-call(bf16[64,16,128]{2,1,0:T(8,128)(2,1)S(1)} %all_to_all.20.near_ref, bf16[64,16,128]{2,1,0:T(8,128)(2,1)} %collective-permute-done.far_ref, s32[64,1]{1,0:T(8,128)S(1)} %reshape.42.ids_ref, bf16[4096,128]{1,0:T(8,128)(2,1)S(1)} %copy-done, bf16[4096,128]{1,0:T(8,128)(2,1)S(1)} %collective-permute-done.1.refs_1_, ...), custom_call_target="tpu_custom_call" | custom-call | flops 270000000 | bytes 4700000 | tf_op jit(solution)/shard_map/logits/pallas_call | solution.py:294
  73.6 12.3 %all_to_all.21.stats_ref = f32[16,1,128]{2,1,0:T(1,128)S(1)} all-to-all(f32[16,1,128]{2,1,0:T(1,128)S(1)} %logits.1), channel_id=1, replica_groups=mesh['heads_0'=8,'heads_1'=2,'z'=8,'x_side'=2,'x_pair'=2] {'x_pair','z'}, dimensions={0} | all-to-all | bytes 16384 | tf_op jit(solution)/shard_map/all_to_all | solution.py:24
  85.9 0.2 group.1
  86.1 13.2 %all_to_all.22.stats_ref = f32[16,1,128]{2,1,0:T(1,128)S(1)} all-to-all(f32[16,1,128]{2,1,0:T(1,128)S(1)} %group.1), channel_id=1, replica_groups=mesh['heads_0'=8,'heads_1'=2,'z'=8,'x_side'=2,'x_pair'=2] {'heads_0','he..., dimensions={0} | all-to-all | bytes 16384 | tf_op jit(solution)/shard_map/all_to_all | solution.py:24
  99.3 0.7 final.1
  (2 shorter events, 0.0 us)
Async XLA Ops:
  0.6 17.5 %copy-start = (bf16[4096,128]{1,0:T(8,128)(2,1)S(1)}, bf16[4096,128]{1,0:T(8,128)(2,1)}, u32[]{:S(2)}) copy-start(bf16[4096,128]{1,0:T(8,128)(2,1)} %refs_0_.3) | copy-start | bytes 3145732
  0.6 31.9 %copy-start.2 = (f32[4096]{0:T(1024)S(1)}, f32[4096]{0:T(1024)}, u32[]{:S(2)}) copy-start(f32[4096]{0:T(1024)} %param.27) | copy-start | bytes 49156
  0.7 31.9 %copy-start.1 = (f32[4096]{0:T(1024)S(1)}, f32[4096]{0:T(1024)}, u32[]{:S(2)}) copy-start(f32[4096]{0:T(1024)} %param.26) | copy-start | bytes 49156
  0.7 25.4 %collective-permute-start.2 = (bf16[4096,128]{1,0:T(8,128)(2,1)}, bf16[4096,128]{1,0:T(8,128)(2,1)S(1)}, u32[]{:S(2)}, u32[]{:S(2)}) collective-permute-start(bf16[4096,128]{1,0:T(8,128)(2,1)} %refs_0_.3), channel_id=1, source_target_pairs={{0,2},{2,0},{1,3},{3,1},{4,6},{6,4},{5,7},{7,5},{8,10},{10,8},{9,1... | collective-permute-start | bytes 3145736 | tf_op jit(solution)/shard_map/ppermute | solution.py:407
  6.3 59.5 %copy-start.3 = (s32[256]{0:T(256)S(1)}, s32[256]{0:T(256)}, u32[]{:S(2)}) copy-start(s32[256]{0:T(256)} %param.29) | copy-start | bytes 3076
  10.1 22.4 %all-to-all-start = ((f32[16,32,128]{2,1,0:T(8,128)}), f32[16,32,128]{2,1,0:T(8,128)S(1)}, u32[]{:S(2)}, u32[]{:S(2)}) async-start(f32[16,32,128]{2,1,0:T(8,128)} %heads.1), calls=%async_computation | async-start | bytes 524288 | tf_op jit(solution)/shard_map/all_to_all | solution.py:24
  18.2 47.9 %collective-permute-start.1 = (bf16[4096,128]{1,0:T(8,128)(2,1)S(1)}, bf16[4096,128]{1,0:T(8,128)(2,1)S(1)}, u32[]{:S(2)}, u32[]{:S(2)}) collective-permute-start(bf16[4096,128]{1,0:T(8,128)(2,1)S(1)} %copy-done), channel_id=1, source_target_pairs={{0,32},{32,0},{1,33},{33,1},{2,34},{34,2},{3,35},{35,3},{4,36},{36... | collective-permute-start | bytes 3145736 | tf_op jit(solution)/shard_map/ppermute | solution.py:408
  26.1 44.2 %collective-permute-start.3 = (bf16[4096,128]{1,0:T(8,128)(2,1)S(1)}, bf16[4096,128]{1,0:T(8,128)(2,1)}, u32[]{:S(2)}, u32[]{:S(2)}) collective-permute-start(bf16[4096,128]{1,0:T(8,128)(2,1)S(1)} %collective-permute-done.2.refs_2_), channel_id=1, source_target_pairs={{0,32},{32,0},{1,33},{33,1},{2,34},{34,2},{3,35},{35,3},{4,36},{36... | collective-permute-start | bytes 3145736 | tf_op jit(solution)/shard_map/ppermute | solution.py:409
  62.6 7.6 %collective-permute-start = (bf16[64,16,128]{2,1,0:T(8,128)(2,1)S(1)}, bf16[64,16,128]{2,1,0:T(8,128)(2,1)}, u32[]{:S(2)}, u32[]{:S(2)}) collective-permute-start(bf16[64,16,128]{2,1,0:T(8,128)(2,1)S(1)} %all_to_all.20.near_ref), channel_id=1, source_target_pairs={{0,1},{1,0},{2,3},{3,2},{4,5},{5,4},{6,7},{7,6},{8,9},{9,8},{10,11... | collective-permute-start | bytes 786440 | tf_op jit(solution)/shard_map/ppermute | solution.py:431
